TPU v7x, 256 devices: a whole 4x4x8 slice. The times are simulated.
256 devices in a mesh: row: 32 (over x, z_lo, y), col: 8 (over z_hi, core).
Axes of the slice: x: 4, y: 4, z: 8 (z_hi: 4, z_lo: 2; z = z_hi * 2 + z_lo), core: 2. Of those that a mesh axis runs over, the one named last changes fastest.
Arguments:
- adj_tiles: bfloat16 [32, 8, 128, 128, 128], P('row', 'col'), may hold values from 0 to 1, as said below
- tile_rows: int32 [32, 8, 128], P('row', 'col'), may hold values from 0 to 7, as said below
- tile_cols: int32 [32, 8, 128], P('row', 'col'), may hold values from 0 to 31, as said below
- tile_count: int32 [32, 8], P('row', 'col'), may hold values from 1 to 128, as said below
- tile_depth: int32 [256, 128], P(('row', 'col')), may hold values from 1 to 7, as said below
- source_ids: int32 [128], replicated, may hold values from 0 to 32767
Outputs:
- path_sums: float32 [32768, 128], P(('row', 'col'))
- log_scales: float32 [6, 128], replicated
Inputs may be any that keep to these rules, and one draw needn't show every extreme that they name: `adj_tiles`: every entry is 0 or 1. The live slots of a device are its first tile_count slots; at least one device holds 128 live slots. `tile_rows`: slots past a device's live count carry 0. `tile_cols`: slots past a device's live count carry 0. `tile_depth`: the value 6 + 1 marks a tile that takes path counts at every level.
All inputs are finite; a program needn't handle non-finite values.
Results may differ from a plain program's by a relative error of at most 0.0003.
Values may be sent and summed in bfloat16 or wider, within the bound.
No kernel may reach another device: no remote copies, remote signals or barrier semaphores. Data moves between devices by JAX's collectives and lax.ppermute only.
A program may use at most 64 MiB of HBM per device.

v0:
```python
import functools

import jax
import jax.numpy as jnp
from jax import lax
from jax.sharding import Mesh
from jax.sharding import PartitionSpec as P

TILE = 128
LEVELS = 6
ROW = ("row_0", "row_1", "row_2")
COL = ("col_0", "col_1")
ROW_COL = ("row_0", "row_1", "row_2", "col_0", "col_1")


EPSILON = 1e-06


def joined_along(parts, dim):
    lengths = list(parts.shape[1:])
    lengths[dim] *= parts.shape[0]
    return jnp.moveaxis(parts, 0, dim).reshape(lengths)


def copy_for_each(shard, axis):
    copies = jnp.broadcast_to(shard, (lax.axis_size(axis), *shard.shape))
    return lax.all_to_all(copies, axis, split_axis=0, concat_axis=0, tiled=True)


def collect(shard, axis, dim):
    return joined_along(copy_for_each(shard, axis), dim)


def cut_along(shard, dim, count):
    before, after = (shard.shape[:dim], shard.shape[dim + 1 :])
    return jnp.moveaxis(shard.reshape(*before, count, -1, *after), dim, 0)


def sent_and_summed(shard, axis, dim):
    count = lax.axis_size(axis)
    parts = lax.all_to_all(cut_along(shard, dim, count), axis, 0, 0, tiled=True)
    return jnp.sum(parts, axis=0)


def one_axis_at_a_time(shard, axes):
    return functools.reduce(lax.psum, axes, shard)


def tile_products(running, blocks, row_ids, col_ids, sources, base_tile, first_slot, end_slot):
    slot_total = blocks.shape[0]
    batch_size = min(16, slot_total)
    turn_count = (jnp.maximum(end_slot - first_slot, 0) + batch_size - 1) // batch_size

    def one_turn(turn_index, summed):
        wanted_start = first_slot + turn_index * batch_size
        window = jnp.minimum(wanted_start, slot_total - batch_size)
        part_blocks = lax.dynamic_slice_in_dim(blocks, window, batch_size, 0)
        part_rows = lax.dynamic_slice_in_dim(row_ids, window, batch_size, 0)
        part_cols = lax.dynamic_slice_in_dim(col_ids, window, batch_size, 0)
        slot_ids = window + jnp.arange(batch_size, dtype=jnp.int32)
        wanted = (slot_ids >= wanted_start) & (slot_ids < end_slot)
        local_cols = jnp.clip(part_cols - base_tile, 0, sources.shape[0] - 1)
        picked = jnp.take(sources, local_cols, axis=0)
        products = jnp.einsum(
            "gij,gjs->gis", part_blocks, picked, preferred_element_type=jnp.float32
        )
        return summed.at[part_rows].add(products * wanted.astype(jnp.float32)[:, None, None])

    return lax.fori_loop(0, turn_count, one_turn, running)


def local(adj_tiles, tile_rows, tile_cols, tile_count, tile_depth, source_ids):
    blocks = adj_tiles[0, 0]
    row_ids = tile_rows[0, 0]
    col_ids = tile_cols[0, 0]
    live_count = tile_count[0, 0]
    row_total = lax.axis_size(ROW)
    col_total = lax.axis_size(COL)
    piece_tiles = tile_depth.shape[0]
    panel_width = tile_depth.shape[1]
    piece_rows = piece_tiles * TILE
    dest_tiles = col_total * piece_tiles
    src_tiles = row_total * piece_tiles
    vertex_total = piece_rows * row_total * col_total
    position = lax.axis_index(ROW) * col_total + lax.axis_index(COL)
    vertex_ids = position * piece_rows + jnp.arange(piece_rows, dtype=jnp.int32)
    start_panel = (vertex_ids[:, None] == source_ids[None, :]).astype(jnp.float32)
    tile_lists = [(blocks, row_ids, col_ids, live_count)]
    zero_sums = jnp.zeros((dest_tiles, TILE, panel_width), jnp.float32)
    path_sums = start_panel
    frontier = start_panel.astype(jnp.bfloat16)
    log_scales = []
    for level_index in range(1, LEVELS + 1):
        gathered = collect(frontier, ROW, 0)
        sources = gathered.reshape(src_tiles, TILE, panel_width)
        partials = tuple(
            (
                tile_products(
                    zero_sums, tile_list[0], tile_list[1], tile_list[2], sources, 0, 0, tile_list[3]
                )
                for tile_list in tile_lists
            )
        )
        combined = partials[0]
        reduced = sent_and_summed(combined.reshape(dest_tiles * TILE, panel_width), COL, 0)
        reached = (tile_depth >= level_index).astype(jnp.float32)
        raw_paths = (reduced.reshape(piece_tiles, TILE, panel_width) * reached[:, None, :]).reshape(
            piece_rows, panel_width
        )
        squares = one_axis_at_a_time(jnp.sum(raw_paths * raw_paths, axis=0), ROW_COL)
        mean_square = squares / vertex_total + EPSILON
        scaled = raw_paths * lax.rsqrt(mean_square)
        path_sums = path_sums + scaled
        log_scales.append(0.5 * jnp.log(mean_square))
        frontier = scaled.astype(jnp.bfloat16)
    return (path_sums, jnp.stack(log_scales))


def solution(mesh):
    split = Mesh(mesh.devices.reshape(4, 2, 4, 4, 2), ("row_0", "row_1", "row_2", "col_0", "col_1"))
    in_specs = (
        P(ROW, COL, None, None, None),
        P(ROW, COL, None),
        P(ROW, COL, None),
        P(ROW, COL),
        P(ROW_COL, None),
        P(),
    )
    out_specs = (P(ROW_COL, None), P())
    return jax.shard_map(local, mesh=split, in_specs=in_specs, out_specs=out_specs, check_vma=False)
```

profile of v0, /device:TPU:1, one launch (start us, length us, event | category | flops | bytes accessed | tf_op | source)
XLA Modules:
  0.0 750.1 jit_solution(16349796312365457652)
XLA Ops:
  2.6 9.2 %all-to-all-start = ((bf16[32,128,128]{2,1,0:T(8,128)(2,1)}), bf16[32,128,128]{2,1,0:T(8,128)(2,1)S(1)}, u32[]{:S(2)}, u32[]{:S(2)}) async-start(bf16[32,128,128]{2,1,0:T(8,128)(2,1)} %broadcast_in_dim.46), calls=%async_computation | async-start | bytes 2097152 | tf_op jit(solution)/shard_map/all_to_all | solution.py:27
  12.5 14.9 %all-to-all-done = bf16[32,128,128]{2,1,0:T(8,128)(2,1)S(1)} async-done(((bf16[32,128,128]{2,1,0:T(8,128)(2,1)}), bf16[32,128,128]{2,1,0:T(8,128)(2,1)S(1)}, u32[]{:S(2)}, u32[]{:S(2)}) %all-to-all-start) | async-done | bytes 1048608 | tf_op jit(solution)/shard_map/all_to_all | solution.py:27
  28.2 22.6 %while.60 = (s32[]{:T(128)}, f32[8,128,128]{2,1,0:T(8,128)}, s32[]{:T(128)}, s32[128]{0:T(128)}, bf16[128,128,128]{2,1,0:T(8,128)(2,1)}, /*index=5*/s32[128]{0:T...) while((s32[]{:T(128)}, f32[8,128,128]{2,1,0:T(8,128)}, ...), condition=%wide.region_2.4_spmd, body=%wide.region_0.3_spmd.sunk | while | flops 67896568 | bytes 6296367 | solution.py:69
  50.8 42.2 %all-to-all-start.1 = ((f32[8,128,128]{2,1,0:T(8,128)}), f32[8,128,128]{2,1,0:T(8,128)S(1)}, u32[]{:S(2)}, u32[]{:S(2)}) async-start(f32[8,128,128]{2,1,0:T(8,128)} %get-tuple-element.261), calls=%async_computation.1 | async-start | bytes 1048576 | tf_op jit(solution)/shard_map/all_to_all | solution.py:41
  93.0 13.1 %all-to-all-done.1 = f32[8,128,128]{2,1,0:T(8,128)S(1)} async-done(((f32[8,128,128]{2,1,0:T(8,128)}), f32[8,128,128]{2,1,0:T(8,128)S(1)}, u32[]{:S(2)}, u32[]{:S(2)}) %all-to-all-start.1) | async-done | bytes 524320 | tf_op jit(solution)/shard_map/all_to_all | solution.py:41
  106.2 8.8 %psum.210 = f32[128]{0:T(128)S(1)} all-reduce(f32[128]{0:T(128)S(1)} %multiply_reduce_fusion.5), channel_id=1, replica_groups=mesh['row_0'=4,'row_1'=2,'row_2'=4,'col_0'=4,'col_1'=2] {'row_0'}, use_global_device_ids=true, to_apply=%region_5.7 | all-reduce | flops 128 | bytes 1024 | tf_op jit(solution)/shard_map/psum | solution.py:46
  115.0 4.7 psum.211
  119.8 9.3 %psum.212 = f32[128]{0:T(128)S(1)} all-reduce(f32[128]{0:T(128)S(1)} %psum.211), channel_id=1, replica_groups=mesh['row_0'=4,'row_1'=2,'row_2'=4,'col_0'=4,'col_1'=2] {'row_2'}, use_global_device_ids=true, to_apply=%region_7.9 | all-reduce | flops 128 | bytes 1024 | tf_op jit(solution)/shard_map/psum | solution.py:46
  129.0 7.8 %psum.213 = f32[128]{0:T(128)S(1)} all-reduce(f32[128]{0:T(128)S(1)} %psum.212), channel_id=1, replica_groups=mesh['row_0'=4,'row_1'=2,'row_2'=4,'col_0'=4,'col_1'=2] {'col_0'}, use_global_device_ids=true, to_apply=%region_8.10 | all-reduce | flops 128 | bytes 1024 | tf_op jit(solution)/shard_map/psum | solution.py:46
  136.8 10.7 %psum.214 = f32[128]{0:T(128)S(1)} all-reduce(f32[128]{0:T(128)S(1)} %psum.213), channel_id=1, replica_groups=mesh['row_0'=4,'row_1'=2,'row_2'=4,'col_0'=4,'col_1'=2] {'col_1'}, use_global_device_ids=true, to_apply=%region_9.11 | all-reduce | flops 128 | bytes 1024 | tf_op jit(solution)/shard_map/psum | solution.py:46
  148.8 3.9 all-to-all-start.2
  152.7 15.8 %all-to-all-done.2 = bf16[32,128,128]{2,1,0:T(8,128)(2,1)S(1)} async-done(((bf16[32,128,128]{2,1,0:T(8,128)(2,1)}), bf16[32,128,128]{2,1,0:T(8,128)(2,1)S(1)}, u32[]{:S(2)}, u32[]{:S(2)}) %all-to-all-start.2) | async-done | bytes 1048608 | tf_op jit(solution)/shard_map/all_to_all | solution.py:27
  168.6 15.6 %while.61 = (s32[]{:T(128)}, f32[8,128,128]{2,1,0:T(8,128)S(1)}, s32[]{:T(128)}, s32[128]{0:T(128)}, bf16[128,128,128]{2,1,0:T(8,128)(2,1)}, /*index=5*/s32[128]...) while((s32[]{:T(128)}, f32[8,128,128]{2,1,0:T(8,128)S(1)}, ...), condition=%wide.region_12.14_spmd, body=%wide.region_10.13_spmd.sunk | while | flops 67896568 | bytes 6296367 | solution.py:69
  184.2 44.0 %all_to_all.60 = f32[8,128,128]{2,1,0:T(8,128)S(1)} all-to-all(f32[8,128,128]{2,1,0:T(8,128)S(1)} %get-tuple-element.262), channel_id=1, replica_groups=mesh['row_0'=4,'row_1'=2,'row_2'=4,'col_0'=4,'col_1'=2] {'col_0','col_1'}, dimensions={0} | all-to-all | bytes 1048576 | tf_op jit(solution)/shard_map/all_to_all | solution.py:41
  228.2 8.5 %psum.215 = f32[128]{0:T(128)S(1)} all-reduce(f32[128]{0:T(128)S(1)} %multiply_reduce_fusion.4), channel_id=1, replica_groups=mesh['row_0'=4,'row_1'=2,'row_2'=4,'col_0'=4,'col_1'=2] {'row_0'}, use_global_device_ids=true, to_apply=%region_15.17 | all-reduce | flops 128 | bytes 1024 | tf_op jit(solution)/shard_map/psum | solution.py:46
  240.5 8.2 %psum.217 = f32[128]{0:T(128)S(1)} all-reduce(f32[128]{0:T(128)S(1)} %psum.216), channel_id=1, replica_groups=mesh['row_0'=4,'row_1'=2,'row_2'=4,'col_0'=4,'col_1'=2] {'row_2'}, use_global_device_ids=true, to_apply=%region_17.19 | all-reduce | flops 128 | bytes 1024 | tf_op jit(solution)/shard_map/psum | solution.py:46
  248.7 9.1 %psum.218 = f32[128]{0:T(128)S(1)} all-reduce(f32[128]{0:T(128)S(1)} %psum.217), channel_id=1, replica_groups=mesh['row_0'=4,'row_1'=2,'row_2'=4,'col_0'=4,'col_1'=2] {'col_0'}, use_global_device_ids=true, to_apply=%region_18.20 | all-reduce | flops 128 | bytes 1024 | tf_op jit(solution)/shard_map/psum | solution.py:46
  257.8 10.1 %psum.219 = f32[128]{0:T(128)S(1)} all-reduce(f32[128]{0:T(128)S(1)} %psum.218), channel_id=1, replica_groups=mesh['row_0'=4,'row_1'=2,'row_2'=4,'col_0'=4,'col_1'=2] {'col_1'}, use_global_device_ids=true, to_apply=%region_19.21 | all-reduce | flops 128 | bytes 1024 | tf_op jit(solution)/shard_map/psum | solution.py:46
  273.1 15.8 %all-to-all-done.4 = bf16[32,128,128]{2,1,0:T(8,128)(2,1)S(1)} async-done(((bf16[32,128,128]{2,1,0:T(8,128)(2,1)}), bf16[32,128,128]{2,1,0:T(8,128)(2,1)S(1)}, u32[]{:S(2)}, u32[]{:S(2)}) %all-to-all-start.4) | async-done | bytes 1048608 | tf_op jit(solution)/shard_map/all_to_all | solution.py:27
  289.0 15.6 %while.62 = (s32[]{:T(128)}, f32[8,128,128]{2,1,0:T(8,128)S(1)}, s32[]{:T(128)}, s32[128]{0:T(128)}, bf16[128,128,128]{2,1,0:T(8,128)(2,1)}, /*index=5*/s32[128]...) while((s32[]{:T(128)}, f32[8,128,128]{2,1,0:T(8,128)S(1)}, ...), condition=%wide.region_22.24_spmd, body=%wide.region_20.23_spmd.sunk | while | flops 67896568 | bytes 6296367 | solution.py:69
  304.5 43.4 %all_to_all.61 = f32[8,128,128]{2,1,0:T(8,128)S(1)} all-to-all(f32[8,128,128]{2,1,0:T(8,128)S(1)} %get-tuple-element.263), channel_id=1, replica_groups=mesh['row_0'=4,'row_1'=2,'row_2'=4,'col_0'=4,'col_1'=2] {'col_0','col_1'}, dimensions={0} | all-to-all | bytes 1048576 | tf_op jit(solution)/shard_map/all_to_all | solution.py:41
  348.0 8.6 %psum.220 = f32[128]{0:T(128)S(1)} all-reduce(f32[128]{0:T(128)S(1)} %multiply_reduce_fusion.3), channel_id=1, replica_groups=mesh['row_0'=4,'row_1'=2,'row_2'=4,'col_0'=4,'col_1'=2] {'row_0'}, use_global_device_ids=true, to_apply=%region_25.27 | all-reduce | flops 128 | bytes 1024 | tf_op jit(solution)/shard_map/psum | solution.py:46
  360.3 8.2 %psum.222 = f32[128]{0:T(128)S(1)} all-reduce(f32[128]{0:T(128)S(1)} %psum.221), channel_id=1, replica_groups=mesh['row_0'=4,'row_1'=2,'row_2'=4,'col_0'=4,'col_1'=2] {'row_2'}, use_global_device_ids=true, to_apply=%region_27.29 | all-reduce | flops 128 | bytes 1024 | tf_op jit(solution)/shard_map/psum | solution.py:46
  368.6 9.1 %psum.223 = f32[128]{0:T(128)S(1)} all-reduce(f32[128]{0:T(128)S(1)} %psum.222), channel_id=1, replica_groups=mesh['row_0'=4,'row_1'=2,'row_2'=4,'col_0'=4,'col_1'=2] {'col_0'}, use_global_device_ids=true, to_apply=%region_28.30 | all-reduce | flops 128 | bytes 1024 | tf_op jit(solution)/shard_map/psum | solution.py:46
  377.7 10.1 %psum.224 = f32[128]{0:T(128)S(1)} all-reduce(f32[128]{0:T(128)S(1)} %psum.223), channel_id=1, replica_groups=mesh['row_0'=4,'row_1'=2,'row_2'=4,'col_0'=4,'col_1'=2] {'col_1'}, use_global_device_ids=true, to_apply=%region_29.31 | all-reduce | flops 128 | bytes 1024 | tf_op jit(solution)/shard_map/psum | solution.py:46
  393.0 15.8 %all-to-all-done.6 = bf16[32,128,128]{2,1,0:T(8,128)(2,1)S(1)} async-done(((bf16[32,128,128]{2,1,0:T(8,128)(2,1)}), bf16[32,128,128]{2,1,0:T(8,128)(2,1)S(1)}, u32[]{:S(2)}, u32[]{:S(2)}) %all-to-all-start.6) | async-done | bytes 1048608 | tf_op jit(solution)/shard_map/all_to_all | solution.py:27
  408.8 15.6 %while.63 = (s32[]{:T(128)}, f32[8,128,128]{2,1,0:T(8,128)S(1)}, s32[]{:T(128)}, s32[128]{0:T(128)}, bf16[128,128,128]{2,1,0:T(8,128)(2,1)}, /*index=5*/s32[128]...) while((s32[]{:T(128)}, f32[8,128,128]{2,1,0:T(8,128)S(1)}, ...), condition=%wide.region_32.34_spmd, body=%wide.region_30.33_spmd.sunk | while | flops 67896568 | bytes 6296367 | solution.py:69
  424.4 43.4 %all_to_all.62 = f32[8,128,128]{2,1,0:T(8,128)S(1)} all-to-all(f32[8,128,128]{2,1,0:T(8,128)S(1)} %get-tuple-element.264), channel_id=1, replica_groups=mesh['row_0'=4,'row_1'=2,'row_2'=4,'col_0'=4,'col_1'=2] {'col_0','col_1'}, dimensions={0} | all-to-all | bytes 1048576 | tf_op jit(solution)/shard_map/all_to_all | solution.py:41
  467.9 8.5 %psum.225 = f32[128]{0:T(128)S(1)} all-reduce(f32[128]{0:T(128)S(1)} %multiply_reduce_fusion.2), channel_id=1, replica_groups=mesh['row_0'=4,'row_1'=2,'row_2'=4,'col_0'=4,'col_1'=2] {'row_0'}, use_global_device_ids=true, to_apply=%region_35.37 | all-reduce | flops 128 | bytes 1024 | tf_op jit(solution)/shard_map/psum | solution.py:46
  480.2 8.3 %psum.227 = f32[128]{0:T(128)S(1)} all-reduce(f32[128]{0:T(128)S(1)} %psum.226), channel_id=1, replica_groups=mesh['row_0'=4,'row_1'=2,'row_2'=4,'col_0'=4,'col_1'=2] {'row_2'}, use_global_device_ids=true, to_apply=%region_37.39 | all-reduce | flops 128 | bytes 1024 | tf_op jit(solution)/shard_map/psum | solution.py:46
  488.4 9.1 %psum.228 = f32[128]{0:T(128)S(1)} all-reduce(f32[128]{0:T(128)S(1)} %psum.227), channel_id=1, replica_groups=mesh['row_0'=4,'row_1'=2,'row_2'=4,'col_0'=4,'col_1'=2] {'col_0'}, use_global_device_ids=true, to_apply=%region_38.40 | all-reduce | flops 128 | bytes 1024 | tf_op jit(solution)/shard_map/psum | solution.py:46
  497.5 10.1 %psum.229 = f32[128]{0:T(128)S(1)} all-reduce(f32[128]{0:T(128)S(1)} %psum.228), channel_id=1, replica_groups=mesh['row_0'=4,'row_1'=2,'row_2'=4,'col_0'=4,'col_1'=2] {'col_1'}, use_global_device_ids=true, to_apply=%region_39.41 | all-reduce | flops 128 | bytes 1024 | tf_op jit(solution)/shard_map/psum | solution.py:46
  508.9 4.1 all-to-all-start.8
  513.0 15.8 %all-to-all-done.8 = bf16[32,128,128]{2,1,0:T(8,128)(2,1)S(1)} async-done(((bf16[32,128,128]{2,1,0:T(8,128)(2,1)}), bf16[32,128,128]{2,1,0:T(8,128)(2,1)S(1)}, u32[]{:S(2)}, u32[]{:S(2)}) %all-to-all-start.8) | async-done | bytes 1048608 | tf_op jit(solution)/shard_map/all_to_all | solution.py:27
  528.8 15.6 %while.64 = (s32[]{:T(128)}, f32[8,128,128]{2,1,0:T(8,128)S(1)}, s32[]{:T(128)}, s32[128]{0:T(128)}, bf16[128,128,128]{2,1,0:T(8,128)(2,1)}, /*index=5*/s32[128]...) while((s32[]{:T(128)}, f32[8,128,128]{2,1,0:T(8,128)S(1)}, ...), condition=%wide.region_42.44_spmd, body=%wide.region_40.43_spmd.sunk | while | flops 67896568 | bytes 6296367 | solution.py:69
  544.4 43.5 %all_to_all.63 = f32[8,128,128]{2,1,0:T(8,128)S(1)} all-to-all(f32[8,128,128]{2,1,0:T(8,128)S(1)} %get-tuple-element.265), channel_id=1, replica_groups=mesh['row_0'=4,'row_1'=2,'row_2'=4,'col_0'=4,'col_1'=2] {'col_0','col_1'}, dimensions={0} | all-to-all | bytes 1048576 | tf_op jit(solution)/shard_map/all_to_all | solution.py:41
  587.9 8.5 %psum.230 = f32[128]{0:T(128)S(1)} all-reduce(f32[128]{0:T(128)S(1)} %multiply_reduce_fusion.1), channel_id=1, replica_groups=mesh['row_0'=4,'row_1'=2,'row_2'=4,'col_0'=4,'col_1'=2] {'row_0'}, use_global_device_ids=true, to_apply=%region_45.47 | all-reduce | flops 128 | bytes 1024 | tf_op jit(solution)/shard_map/psum | solution.py:46
  600.2 8.3 %psum.232 = f32[128]{0:T(128)S(1)} all-reduce(f32[128]{0:T(128)S(1)} %psum.231), channel_id=1, replica_groups=mesh['row_0'=4,'row_1'=2,'row_2'=4,'col_0'=4,'col_1'=2] {'row_2'}, use_global_device_ids=true, to_apply=%region_47.49 | all-reduce | flops 128 | bytes 1024 | tf_op jit(solution)/shard_map/psum | solution.py:46
  608.5 9.1 %psum.233 = f32[128]{0:T(128)S(1)} all-reduce(f32[128]{0:T(128)S(1)} %psum.232), channel_id=1, replica_groups=mesh['row_0'=4,'row_1'=2,'row_2'=4,'col_0'=4,'col_1'=2] {'col_0'}, use_global_device_ids=true, to_apply=%region_48.50 | all-reduce | flops 128 | bytes 1024 | tf_op jit(solution)/shard_map/psum | solution.py:46
  617.5 10.1 %psum.234 = f32[128]{0:T(128)S(1)} all-reduce(f32[128]{0:T(128)S(1)} %psum.233), channel_id=1, replica_groups=mesh['row_0'=4,'row_1'=2,'row_2'=4,'col_0'=4,'col_1'=2] {'col_1'}, use_global_device_ids=true, to_apply=%region_49.51 | all-reduce | flops 128 | bytes 1024 | tf_op jit(solution)/shard_map/psum | solution.py:46
  629.5 3.9 all-to-all-start.10
  633.4 15.8 %all-to-all-done.10 = bf16[32,128,128]{2,1,0:T(8,128)(2,1)S(1)} async-done(((bf16[32,128,128]{2,1,0:T(8,128)(2,1)}), bf16[32,128,128]{2,1,0:T(8,128)(2,1)S(1)}, u32[]{:S(2)}, u32[]{:S(2)}) %all-to-all-start.10) | async-done | bytes 1048608 | tf_op jit(solution)/shard_map/all_to_all | solution.py:27
  649.3 15.6 %while.65 = (s32[]{:T(128)}, f32[8,128,128]{2,1,0:T(8,128)S(1)}, s32[]{:T(128)}, s32[128]{0:T(128)}, bf16[128,128,128]{2,1,0:T(8,128)(2,1)}, /*index=5*/s32[128]...) while((s32[]{:T(128)}, f32[8,128,128]{2,1,0:T(8,128)S(1)}, ...), condition=%wide.region_52.54_spmd, body=%wide.region_50.53_spmd.sunk | while | flops 67896568 | bytes 6296367 | solution.py:69
  664.9 43.4 %all_to_all.64 = f32[8,128,128]{2,1,0:T(8,128)S(1)} all-to-all(f32[8,128,128]{2,1,0:T(8,128)S(1)} %get-tuple-element.266), channel_id=1, replica_groups=mesh['row_0'=4,'row_1'=2,'row_2'=4,'col_0'=4,'col_1'=2] {'col_0','col_1'}, dimensions={0} | all-to-all | bytes 1048576 | tf_op jit(solution)/shard_map/all_to_all | solution.py:41
  708.4 8.5 %psum.235 = f32[128]{0:T(128)S(1)} all-reduce(f32[128]{0:T(128)S(1)} %multiply_reduce_fusion), channel_id=1, replica_groups=mesh['row_0'=4,'row_1'=2,'row_2'=4,'col_0'=4,'col_1'=2] {'row_0'}, use_global_device_ids=true, to_apply=%region_55.57 | all-reduce | flops 128 | bytes 1024 | tf_op jit(solution)/shard_map/psum | solution.py:46
  720.7 8.3 %psum.237 = f32[128]{0:T(128)S(1)} all-reduce(f32[128]{0:T(128)S(1)} %psum.236), channel_id=1, replica_groups=mesh['row_0'=4,'row_1'=2,'row_2'=4,'col_0'=4,'col_1'=2] {'row_2'}, use_global_device_ids=true, to_apply=%region_57.59 | all-reduce | flops 128 | bytes 1024 | tf_op jit(solution)/shard_map/psum | solution.py:46
  728.9 9.1 %psum.238 = f32[128]{0:T(128)S(1)} all-reduce(f32[128]{0:T(128)S(1)} %psum.237), channel_id=1, replica_groups=mesh['row_0'=4,'row_1'=2,'row_2'=4,'col_0'=4,'col_1'=2] {'col_0'}, use_global_device_ids=true, to_apply=%region_58.60 | all-reduce | flops 128 | bytes 1024 | tf_op jit(solution)/shard_map/psum | solution.py:46
  738.0 10.1 %psum.239 = f32[128]{0:T(128)S(1)} all-reduce(f32[128]{0:T(128)S(1)} %psum.238), channel_id=1, replica_groups=mesh['row_0'=4,'row_1'=2,'row_2'=4,'col_0'=4,'col_1'=2] {'col_1'}, use_global_device_ids=true, to_apply=%region_59.61 | all-reduce | flops 128 | bytes 1024 | tf_op jit(solution)/shard_map/psum | solution.py:46
  (161 shorter events, 138.5 us)
Async XLA Ops:
  2.6 24.7 %all-to-all-start = ((bf16[32,128,128]{2,1,0:T(8,128)(2,1)}), bf16[32,128,128]{2,1,0:T(8,128)(2,1)S(1)}, u32[]{:S(2)}, u32[]{:S(2)}) async-start(bf16[32,128,128]{2,1,0:T(8,128)(2,1)} %broadcast_in_dim.46), calls=%async_computation | async-start | bytes 2097152 | tf_op jit(solution)/shard_map/all_to_all | solution.py:27
  28.2 64.8 %copy-start.2 = (s32[1,128]{1,0:T(1,128)S(1)}, s32[1,128]{1,0:T(1,128)}, u32[]{:S(2)}) copy-start(s32[1,128]{1,0:T(1,128)} %param.24) | copy-start | bytes 1540
  50.8 117.7 %copy-start = (s32[128]{0:T(128)S(1)}, s32[128]{0:T(128)}, u32[]{:S(2)}) copy-start(s32[128]{0:T(128)} %get-tuple-element.981) | copy-start | bytes 1540
  50.8 55.3 %all-to-all-start.1 = ((f32[8,128,128]{2,1,0:T(8,128)}), f32[8,128,128]{2,1,0:T(8,128)S(1)}, u32[]{:S(2)}, u32[]{:S(2)}) async-start(f32[8,128,128]{2,1,0:T(8,128)} %get-tuple-element.261), calls=%async_computation.1 | async-start | bytes 1048576 | tf_op jit(solution)/shard_map/all_to_all | solution.py:41
  148.8 19.7 %all-to-all-start.2 = ((bf16[32,128,128]{2,1,0:T(8,128)(2,1)}), bf16[32,128,128]{2,1,0:T(8,128)(2,1)S(1)}, u32[]{:S(2)}, u32[]{:S(2)}) async-start(bf16[32,128,128]{2,1,0:T(8,128)(2,1)} %broadcast_in_dim.49), calls=%async_computation.2 | async-start | bytes 2097152 | tf_op jit(solution)/shard_map/all_to_all | solution.py:27
  269.2 19.7 %all-to-all-start.4 = ((bf16[32,128,128]{2,1,0:T(8,128)(2,1)}), bf16[32,128,128]{2,1,0:T(8,128)(2,1)S(1)}, u32[]{:S(2)}, u32[]{:S(2)}) async-start(bf16[32,128,128]{2,1,0:T(8,128)(2,1)} %broadcast_in_dim.50), calls=%async_computation.4 | async-start | bytes 2097152 | tf_op jit(solution)/shard_map/all_to_all | solution.py:27
  389.0 19.7 %all-to-all-start.6 = ((bf16[32,128,128]{2,1,0:T(8,128)(2,1)}), bf16[32,128,128]{2,1,0:T(8,128)(2,1)S(1)}, u32[]{:S(2)}, u32[]{:S(2)}) async-start(bf16[32,128,128]{2,1,0:T(8,128)(2,1)} %broadcast_in_dim.72), calls=%async_computation.6 | async-start | bytes 2097152 | tf_op jit(solution)/shard_map/all_to_all | solution.py:27
  508.9 19.9 %all-to-all-start.8 = ((bf16[32,128,128]{2,1,0:T(8,128)(2,1)}), bf16[32,128,128]{2,1,0:T(8,128)(2,1)S(1)}, u32[]{:S(2)}, u32[]{:S(2)}) async-start(bf16[32,128,128]{2,1,0:T(8,128)(2,1)} %broadcast_in_dim.73), calls=%async_computation.8 | async-start | bytes 2097152 | tf_op jit(solution)/shard_map/all_to_all | solution.py:27
  629.5 19.7 %all-to-all-start.10 = ((bf16[32,128,128]{2,1,0:T(8,128)(2,1)}), bf16[32,128,128]{2,1,0:T(8,128)(2,1)S(1)}, u32[]{:S(2)}, u32[]{:S(2)}) async-start(bf16[32,128,128]{2,1,0:T(8,128)(2,1)} %broadcast_in_dim.74), calls=%async_computation.10 | async-start | bytes 2097152 | tf_op jit(solution)/shard_map/all_to_all | solution.py:27
  649.3 98.9 %copy-start.1 = (s32[128]{0:T(128)S(1)}, s32[128]{0:T(128)}, u32[]{:S(2)}) copy-start(s32[128]{0:T(128)} %param.25) | copy-start | bytes 1540
where the time goes:
time: 750 us
  blocking collectives  458 us (61%)
  waiting for transfers between devices  107 us (14%)
  starting transfers between devices  71.2 us (9%)
  other arithmetic  65 us (9%)
  matrix products  25.5 us (3%)
  local copies, waits for them, and re-layouts  21.3 us (3%)
    psum x30, blocking collectives, one_axis_at_a_time(): return functools.reduce(lax.psum, axes, shard)  240 us
    all_to_all x5, blocking collectives, sent_and_summed(): parts = lax.all_to_all(cut_along(shard, dim, count), axis, 0, 0, tiled=True)  218 us
    all_to_all x6, waiting for transfers between devices, copy_for_each(): return lax.all_to_all(copies, axis, split_axis=0, concat_axis=0, tiled=True)  93.8 us
    all_to_all x1, starting transfers between devices, sent_and_summed(): parts = lax.all_to_all(cut_along(shard, dim, count), axis, 0, 0, tiled=True)  42.2 us
    scatter-add x18, other arithmetic, one_turn(): summed.at[part_rows]  34 us
    all_to_all x6, starting transfers between devices, copy_for_each(): return lax.all_to_all(copies, axis, split_axis=0, concat_axis=0, tiled=True)  29 us
    dot_general x18, matrix products, one_turn(): jnp.einsum('gij,gjs->gis', part_blocks, picked, preferred_element_type=jn...  25.5 us
    and x18, other arithmetic, one_turn(): picked = jnp.take(sources, local_cols, axis=0)  15.1 us
  transfers between devices with their start and end apart: 7, of which 7 were waited for; matrix products, arithmetic and copies ran while one was open for 0% of the time, Pallas kernels for 0%

commit v1 on v0

v1 whole, which is shorter than its diff:
```python
import jax
import jax.numpy as jnp
from jax import lax
from jax.experimental import pallas as pl
from jax.experimental.pallas import tpu as pltpu
from jax.sharding import Mesh
from jax.sharding import PartitionSpec as P

TILE = 128
PANEL = 128
LEVELS = 6
KMAX = 128
DEST_TILES = 8
SRC_TILES = 32
VERTICES = 32768
EPSILON = 1e-06
ROW = ("row_0", "row_1", "row_2")
COL = ("col_0", "col_1")
ROW_COL = ROW + COL
GROUP = 4
LIST_LEN = KMAX + DEST_TILES * GROUP
EXTRA = 8
ROWS = TILE + EXTRA


def f32(x):
    return x.astype(jnp.float32)


def sort_kernel(rows, cols, count, order, starts, fill):
    live = count[0]
    for d in range(DEST_TILES):
        fill[d] = 0

    def tally(k, carry):
        d = rows[k]
        fill[d] = fill[d] + 1
        return carry

    lax.fori_loop(0, live, tally, 0)
    first = jnp.int32(0)
    for d in range(DEST_TILES):
        held = fill[d]
        starts[d] = first
        fill[d] = first * GROUP
        first = first + (held + GROUP - 1) // GROUP
    starts[DEST_TILES] = first

    def blank(i, carry):
        order[i] = SRC_TILES * KMAX
        return carry

    lax.fori_loop(0, first * GROUP, blank, 0)

    def place(k, carry):
        d = rows[k]
        i = fill[d]
        order[i] = cols[k] * KMAX + k
        fill[d] = i + 1
        return carry

    lax.fori_loop(0, live, place, 0)


def sort_slots(rows, cols, count):
    smem = pl.BlockSpec(memory_space=pltpu.SMEM)
    return pl.pallas_call(
        sort_kernel,
        in_specs=[smem, smem, smem],
        out_specs=[smem, smem],
        out_shape=[
            jax.ShapeDtypeStruct((LIST_LEN,), jnp.int32),
            jax.ShapeDtypeStruct((16,), jnp.int32),
        ],
        scratch_shapes=[pltpu.SMEM((DEST_TILES,), jnp.int32)],
        name="sort_slots",
    )(rows, cols, count)


def product_kernel(order, starts, place, adj, sources, away, kept, held):
    c0, c1 = place[0], place[1]
    parts = jnp.sum(f32(sources[:, TILE:ROWS, :]), axis=0)
    squares = (parts[0:1] + parts[1:2]) + parts[2:3]
    row = lax.broadcasted_iota(jnp.int32, (EXTRA, PANEL), 0)
    extra = jnp.where(row == c0 * 2 + c1, jnp.broadcast_to(squares, (EXTRA, PANEL)), 0.0)
    for t in range(SRC_TILES):
        held[t] = sources[t, 0:TILE, :]
    held[SRC_TILES] = jnp.zeros((TILE, PANEL), jnp.bfloat16)

    for out, core in ((away, 1 - c1), (kept, c1)):
        for k in range(4):
            d = lax.rem(c0 + k, 4) * 2 + core

            def turn(g, total):
                lefts, rights = [], []
                for i in range(GROUP):
                    code = order[g * GROUP + i]
                    lefts.append(adj[code & (KMAX - 1)])
                    rights.append(held[lax.shift_right_logical(code, 7)])
                left = jnp.concatenate(lefts, axis=1)
                right = jnp.concatenate(rights, axis=0)
                return total + jnp.dot(left, right, preferred_element_type=jnp.float32)

            total = lax.fori_loop(
                starts[d], starts[d + 1], turn, jnp.zeros((TILE, PANEL), jnp.float32)
            )
            out[k, 0:TILE, :] = total
            out[k, TILE:ROWS, :] = extra


def products(order, starts, place, adj, sources):
    smem = pl.BlockSpec(memory_space=pltpu.SMEM)
    vmem = pl.BlockSpec(memory_space=pltpu.VMEM)
    chunk = jax.ShapeDtypeStruct((4, ROWS, PANEL), jnp.float32)
    return pl.pallas_call(
        product_kernel,
        in_specs=[smem, smem, smem, vmem, vmem],
        out_specs=[vmem, vmem],
        out_shape=[chunk, chunk],
        scratch_shapes=[pltpu.VMEM((SRC_TILES + 1, TILE, PANEL), jnp.bfloat16)],
        compiler_params=pltpu.CompilerParams(vmem_limit_bytes=16 * 1024 * 1024),
        name="products",
    )(order, starts, place, adj, sources)


def split3(x):
    high = x.astype(jnp.bfloat16)
    rest = x - f32(high)
    middle = rest.astype(jnp.bfloat16)
    low = (rest - f32(middle)).astype(jnp.bfloat16)
    return f32(high), f32(middle), f32(low)


def level_kernel(level, own, one, two, three, depth, raw_in, sums_in, sums, raw, squares, scale, spread):
    total = (own[...] + one[...]) + (two[...] + three[...])
    product = total[0:TILE]
    reached = depth[...] >= level
    if level == 1:
        sums[...] = sums_in[...]
        scale[...] = jnp.zeros((1, PANEL), jnp.float32)
    else:
        mean_square = jnp.sum(total[TILE:ROWS], axis=0, keepdims=True) / VERTICES + EPSILON
        scale[...] = mean_square
        inverse = lax.rsqrt(mean_square)
        sums[...] = sums_in[...] + raw_in[...] * inverse
        product = product * inverse
    paths = jnp.where(reached, product, 0.0)
    raw[...] = paths
    square = jnp.sum(paths * paths, axis=0, keepdims=True)
    squares[...] = square
    if level < LEVELS:
        sent = paths.astype(jnp.bfloat16)
        high, middle, low = split3(square)
        row = lax.broadcasted_iota(jnp.int32, (EXTRA, PANEL), 0)
        extra = jnp.where(
            row == 0, high, jnp.where(row == 1, middle, jnp.where(row == 2, low, 0.0))
        ).astype(jnp.bfloat16)
        for t in range(SRC_TILES):
            spread[t, 0:TILE, :] = sent
            spread[t, TILE:ROWS, :] = extra
    else:
        spread[...] = jnp.zeros(spread.shape, spread.dtype)


def finish_level(level, chunks, depth, raw, sums):
    vmem = pl.BlockSpec(memory_space=pltpu.VMEM)
    panel = jax.ShapeDtypeStruct((TILE, PANEL), jnp.float32)
    line = jax.ShapeDtypeStruct((1, PANEL), jnp.float32)
    spread_tiles = SRC_TILES if level < LEVELS else 1
    return pl.pallas_call(
        lambda *refs: level_kernel(level, *refs),
        in_specs=[vmem] * 7,
        out_specs=[vmem] * 5,
        out_shape=[
            panel,
            panel,
            line,
            line,
            jax.ShapeDtypeStruct((spread_tiles, ROWS, PANEL), jnp.bfloat16),
        ],
        compiler_params=pltpu.CompilerParams(vmem_limit_bytes=16 * 1024 * 1024),
        name=f"level_{level}",
    )(*chunks, depth, raw, sums)


def shifted(x, axis, count, step):
    return lax.ppermute(x, axis, [(i, (i + step) % count) for i in range(count)])


def summed_alike(x, axis, count):
    if count == 2:
        return x + shifted(x, axis, 2, 1)
    mine = jnp.arange(count, dtype=jnp.int32)[:, None] == lax.axis_index(axis)
    slots = jnp.where(mine, x, 0.0)
    slots = slots + sum(shifted(slots, axis, count, k) for k in range(1, count))
    return in_order(slots, count)


def in_order(slots, count):
    total = slots[0:1]
    for i in range(1, count):
        total = total + slots[i : i + 1]
    return total


def local(adj_tiles, tile_rows, tile_cols, tile_count, tile_depth, source_ids):
    adj = adj_tiles[0, 0]
    c0, c1 = lax.axis_index("col_0"), lax.axis_index("col_1")
    column = lax.axis_index(COL)
    position = lax.axis_index(ROW) * DEST_TILES + column
    order, starts = sort_slots(tile_rows[0, 0], tile_cols[0, 0], tile_count[0])
    place = jnp.stack([c0, c1]).astype(jnp.int32)
    vertex = position * TILE + jnp.arange(TILE, dtype=jnp.int32)
    sums = f32(vertex[:, None] == source_ids[None, :])
    raw = sums
    tile = jnp.arange(SRC_TILES, dtype=jnp.int32)[:, None, None]
    inner = jnp.arange(ROWS, dtype=jnp.int32)[None, :, None]
    vertex = jnp.where(inner < TILE, (tile * DEST_TILES + column) * TILE + inner, -1)
    sources = (vertex == source_ids[None, None, :]).astype(jnp.bfloat16)
    scales = []
    for level in range(1, LEVELS + 1):
        away, kept = products(order, starts, place, adj, sources)
        kept = kept + shifted(away, "col_1", 2, 1)
        moved = {k: shifted(kept[k], "col_0", 4, k) for k in (2, 1, 3)}
        chunks = (kept[0], moved[1], moved[2], moved[3])
        sums, raw, squares, scale, spread = finish_level(level, chunks, tile_depth, raw, sums)
        if level > 1:
            scales.append(scale)
        if level < LEVELS:
            sources = lax.all_to_all(spread, ROW, 0, 0, tiled=True)
    total = squares
    for axis, count in (("col_1", 2), ("col_0", 4), ("row_0", 4), ("row_1", 2), ("row_2", 4)):
        total = summed_alike(total, axis, count)
    mean_square = total / VERTICES + EPSILON
    scales.append(mean_square)
    path_sums = sums + raw * lax.rsqrt(mean_square)
    return path_sums, 0.5 * jnp.log(jnp.concatenate(scales, axis=0))


def solution(mesh):
    split = Mesh(mesh.devices.reshape(4, 2, 4, 4, 2), ROW_COL)
    in_specs = (
        P(ROW, COL, None, None, None),
        P(ROW, COL, None),
        P(ROW, COL, None),
        P(ROW, COL),
        P(ROW_COL, None),
        P(),
    )
    out_specs = (P(ROW_COL, None), P())
    return jax.shard_map(local, mesh=split, in_specs=in_specs, out_specs=out_specs, check_vma=False)
```

time: 750 us -> 290 us (0.39)
  blocking collectives: 458 us -> 105 us
  other arithmetic: 65 us -> 3.59 us
  Pallas kernels: 0 us -> 40.6 us
  waiting for transfers between devices: 107 us -> 69.5 us
  matrix products: 25.5 us -> 0 us
  local copies, waits for them, and re-layouts: 21.3 us -> 5.83 us
  starting transfers between devices: 71.2 us -> 61 us
    psum x30 -> x0, blocking collectives: 240 us -> none  [one_axis_at_a_time(): return functools.reduce(lax.psum, axes, shard)]
    all_to_all x5, blocking collectives: 218 us -> 105 us  [local(): sources = lax.all_to_all(spread, ROW, 0, 0, tiled=True)]
    all_to_all x7 -> x0, waiting for transfers between devices: 107 us -> none  [the longest x6 93.8 us: copy_for_each(): return lax.all_to_all(copies, axis, split_axis=0, concat_axis=0, tiled=True)]
    all_to_all x7 -> x0, starting transfers between devices: 71.2 us -> none  [the longest x1 42.2 us: sent_and_summed(): parts = lax.all_to_all(cut_along(shard, dim, count), axis, 0, 0, tiled=True)]
    ppermute x0 -> x35, waiting for transfers between devices: none -> 69.5 us  [shifted(): lax.ppermute(x, axis, [(i, (i + step) % count) for i in range(count)])]
    ppermute x0 -> x35, starting transfers between devices: none -> 61 us  [shifted(): lax.ppermute(x, axis, [(i, (i + step) % count) for i in range(count)])]
    pallas_call x0 -> x13, Pallas kernels: none -> 40.6 us  [the longest x6 33.4 us: products(): pl.pallas_call(product_kernel, in_specs=[smem, smem, smem, vmem, vmem], o...]
    scatter-add x18 -> x0, other arithmetic: 34 us -> none  [one_turn(): summed.at[part_rows]]
  transfers between devices with their start and end apart: 7 -> 35, of which waited for: 7 -> 24; matrix products, arithmetic and copies ran while one was open for 0% -> 0% of each run, Pallas kernels for 0% -> 0%
where the time goes in v1:
time: 290 us; the launch traced here: 287 us
  blocking collectives  105 us (36%)
  waiting for transfers between devices  69.5 us (24%)
  starting transfers between devices  61 us (21%)
  Pallas kernels  40.6 us (14%)
  local copies, waits for them, and re-layouts  5.83 us (2%)
  other arithmetic  3.59 us (1%)
    all_to_all x5, blocking collectives, local(): sources = lax.all_to_all(spread, ROW, 0, 0, tiled=True)  105 us
    ppermute x35, waiting for transfers between devices, shifted(): lax.ppermute(x, axis, [(i, (i + step) % count) for i in range(count)])  69.5 us
    ppermute x35, starting transfers between devices, shifted(): lax.ppermute(x, axis, [(i, (i + step) % count) for i in range(count)])  61 us
    pallas_call x6, Pallas kernels, products(): pl.pallas_call(product_kernel, in_specs=[smem, smem, smem, vmem, vmem], o...  33.4 us
  transfers between devices with their start and end apart: 35, of which 24 were waited for; matrix products, arithmetic and copies ran while one was open for 0% of the time, Pallas kernels for 0%

profile of v1, /device:TPU:1, one launch (start us, length us, event | category | flops | bytes accessed | tf_op | source)
XLA Modules:
  0.0 286.8 jit_solution(9022888265018825597)
XLA Ops:
  1.5 1.4 compare_convert_fusion.sources
  2.9 3.5 %sort_slots.1 = (s32[160]{0:T(256)}, s32[16]{0:T(128)}) custom-call(s32[128]{0:T(128)} %bitcast.69, s32[128]{0:T(128)} %bitcast.70, s32[1]{0:T(128)} %bitcast.62.count), custom_call_target="tpu_custom_call" | custom-call | tf_op jit(solution)/shard_map/sort_slots/pallas_call | solution.py:67
  6.4 2.2 copy-done
  9.9 5.6 %products.6 = (f32[4,136,128]{2,1,0:T(8,128)S(1)}, f32[4,136,128]{2,1,0:T(8,128)S(1)}) custom-call(s32[160]{0:T(256)S(1)} %copy-done.3, s32[16]{0:T(128)S(1)} %copy-done.6, s32[2]{0:T(128)S(1)} %pad_add_fusion.place, bf16[128,128,128]{2,1,0:T(8,128)(2,1)S(1)} %bitcast.63, bf16[32,136,128]{2,1,0:T(8,128)(2,1)S(1)} %compare_convert_fusion.sources), custom_call_target="tpu_custom_call" | custom-call | tf_op jit(solution)/shard_map/products/pallas_call | solution.py:115
  17.5 9.0 %collective-permute-start.3 = (f32[136,128]{1,0:T(8,128)S(1)}, f32[136,128]{1,0:T(8,128)S(1)}, u32[]{:S(2)}, u32[]{:S(2)}) collective-permute-start(f32[136,128]{1,0:T(8,128)S(1)} %get-tuple-element.98), channel_id=1, source_target_pairs={{0,6},{2,0},{4,2},{6,4},{1,7},{3,1},{5,3},{7,5},{8,14},{10,8},{12,... | collective-permute-start | bytes 208904 | tf_op jit(solution)/shard_map/ppermute | solution.py:187
  26.6 2.2 collective-permute-start.1
  28.8 7.6 %collective-permute-done.2.refs_2_ = f32[136,128]{1,0:T(8,128)S(1)} collective-permute-done((f32[136,128]{1,0:T(8,128)S(1)}, f32[136,128]{1,0:T(8,128)S(1)}, u32[]{:S(2)}, u32[]{:S(2)}) %collective-permute-start.2) | collective-permute-done | bytes 69664 | tf_op jit(solution)/shard_map/ppermute | solution.py:187
  37.0 23.1 %all_to_all.25.sources = bf16[32,136,128]{2,1,0:T(8,128)(2,1)S(1)} all-to-all(bf16[32,136,128]{2,1,0:T(8,128)(2,1)S(1)} %get-tuple-element.43), channel_id=1, replica_groups=mesh['row_0'=4,'row_1'=2,'row_2'=4,'col_0'=4,'col_1'=2] {'row_0','row_1'..., dimensions={0} | all-to-all | bytes 2228224 | tf_op jit(solution)/shard_map/all_to_all | solution.py:230
  60.1 2.2 copy-done.1
  62.3 5.6 %products.7 = (f32[4,136,128]{2,1,0:T(8,128)S(1)}, f32[4,136,128]{2,1,0:T(8,128)S(1)}) custom-call(s32[160]{0:T(256)S(1)} %copy-done.4, s32[16]{0:T(128)S(1)} %copy-done.7, s32[2]{0:T(128)S(1)} %pad_add_fusion.place, bf16[128,128,128]{2,1,0:T(8,128)(2,1)S(1)} %bitcast.64, bf16[32,136,128]{2,1,0:T(8,128)(2,1)S(1)} %all_to_all.25.sources), custom_call_target="tpu_custom_call" | custom-call | tf_op jit(solution)/shard_map/products/pallas_call | solution.py:115
  70.0 6.6 %collective-permute-start.7 = (f32[136,128]{1,0:T(8,128)S(1)}, f32[136,128]{1,0:T(8,128)S(1)}, u32[]{:S(2)}, u32[]{:S(2)}) collective-permute-start(f32[136,128]{1,0:T(8,128)S(1)} %get-tuple-element.94), channel_id=1, source_target_pairs={{0,6},{2,0},{4,2},{6,4},{1,7},{3,1},{5,3},{7,5},{8,14},{10,8},{12,... | collective-permute-start | bytes 208904 | tf_op jit(solution)/shard_map/ppermute | solution.py:187
  76.5 2.2 collective-permute-start.5
  78.7 2.5 collective-permute-done.7.refs_3_
  81.2 5.8 %collective-permute-done.6.refs_2_ = f32[136,128]{1,0:T(8,128)S(1)} collective-permute-done((f32[136,128]{1,0:T(8,128)S(1)}, f32[136,128]{1,0:T(8,128)S(1)}, u32[]{:S(2)}, u32[]{:S(2)}) %collective-permute-start.6) | collective-permute-done | bytes 69664 | tf_op jit(solution)/shard_map/ppermute | solution.py:187
  87.6 20.7 %all_to_all.26.sources = bf16[32,136,128]{2,1,0:T(8,128)(2,1)S(1)} all-to-all(bf16[32,136,128]{2,1,0:T(8,128)(2,1)S(1)} %get-tuple-element.48), channel_id=1, replica_groups=mesh['row_0'=4,'row_1'=2,'row_2'=4,'col_0'=4,'col_1'=2] {'row_0','row_1'..., dimensions={0} | all-to-all | bytes 2228224 | tf_op jit(solution)/shard_map/all_to_all | solution.py:230
  108.3 5.6 %products.8 = (f32[4,136,128]{2,1,0:T(8,128)S(1)}, f32[4,136,128]{2,1,0:T(8,128)S(1)}) custom-call(s32[160]{0:T(256)S(1)} %copy-done.4, s32[16]{0:T(128)S(1)} %copy-done.7, s32[2]{0:T(128)S(1)} %pad_add_fusion.place, bf16[128,128,128]{2,1,0:T(8,128)(2,1)S(1)} %bitcast.65, bf16[32,136,128]{2,1,0:T(8,128)(2,1)S(1)} %all_to_all.26.sources), custom_call_target="tpu_custom_call" | custom-call | tf_op jit(solution)/shard_map/products/pallas_call | solution.py:115
  114.2 1.3 collective-permute-done.8
  115.6 4.8 %collective-permute-start.11 = (f32[136,128]{1,0:T(8,128)S(1)}, f32[136,128]{1,0:T(8,128)S(1)}, u32[]{:S(2)}, u32[]{:S(2)}) collective-permute-start(f32[136,128]{1,0:T(8,128)S(1)} %get-tuple-element.90), channel_id=1, source_target_pairs={{0,6},{2,0},{4,2},{6,4},{1,7},{3,1},{5,3},{7,5},{8,14},{10,8},{12,... | collective-permute-start | bytes 208904 | tf_op jit(solution)/shard_map/ppermute | solution.py:187
  120.4 2.2 collective-permute-start.9
  122.5 2.5 collective-permute-done.11.refs_3_
  125.1 5.2 %collective-permute-done.10.refs_2_ = f32[136,128]{1,0:T(8,128)S(1)} collective-permute-done((f32[136,128]{1,0:T(8,128)S(1)}, f32[136,128]{1,0:T(8,128)S(1)}, u32[]{:S(2)}, u32[]{:S(2)}) %collective-permute-start.10) | collective-permute-done | bytes 69664 | tf_op jit(solution)/shard_map/ppermute | solution.py:187
  130.9 19.9 %all_to_all.27.sources = bf16[32,136,128]{2,1,0:T(8,128)(2,1)S(1)} all-to-all(bf16[32,136,128]{2,1,0:T(8,128)(2,1)S(1)} %get-tuple-element.53), channel_id=1, replica_groups=mesh['row_0'=4,'row_1'=2,'row_2'=4,'col_0'=4,'col_1'=2] {'row_0','row_1'..., dimensions={0} | all-to-all | bytes 2228224 | tf_op jit(solution)/shard_map/all_to_all | solution.py:230
  150.8 5.6 %products.9 = (f32[4,136,128]{2,1,0:T(8,128)S(1)}, f32[4,136,128]{2,1,0:T(8,128)S(1)}) custom-call(s32[160]{0:T(256)S(1)} %copy-done.4, s32[16]{0:T(128)S(1)} %copy-done.7, s32[2]{0:T(128)S(1)} %pad_add_fusion.place, bf16[128,128,128]{2,1,0:T(8,128)(2,1)S(1)} %bitcast.66, bf16[32,136,128]{2,1,0:T(8,128)(2,1)S(1)} %all_to_all.27.sources), custom_call_target="tpu_custom_call" | custom-call | tf_op jit(solution)/shard_map/products/pallas_call | solution.py:115
  157.6 1.2 collective-permute-done.12
  158.8 5.0 %collective-permute-start.15 = (f32[136,128]{1,0:T(8,128)S(1)}, f32[136,128]{1,0:T(8,128)S(1)}, u32[]{:S(2)}, u32[]{:S(2)}) collective-permute-start(f32[136,128]{1,0:T(8,128)S(1)} %get-tuple-element.86), channel_id=1, source_target_pairs={{0,6},{2,0},{4,2},{6,4},{1,7},{3,1},{5,3},{7,5},{8,14},{10,8},{12,... | collective-permute-start | bytes 208904 | tf_op jit(solution)/shard_map/ppermute | solution.py:187
  163.9 2.2 collective-permute-start.13
  166.0 2.4 collective-permute-done.15.refs_3_
  168.5 5.9 %collective-permute-done.14.refs_2_ = f32[136,128]{1,0:T(8,128)S(1)} collective-permute-done((f32[136,128]{1,0:T(8,128)S(1)}, f32[136,128]{1,0:T(8,128)S(1)}, u32[]{:S(2)}, u32[]{:S(2)}) %collective-permute-start.14) | collective-permute-done | bytes 69664 | tf_op jit(solution)/shard_map/ppermute | solution.py:187
  175.0 20.7 %all_to_all.28.sources = bf16[32,136,128]{2,1,0:T(8,128)(2,1)S(1)} all-to-all(bf16[32,136,128]{2,1,0:T(8,128)(2,1)S(1)} %get-tuple-element.58), channel_id=1, replica_groups=mesh['row_0'=4,'row_1'=2,'row_2'=4,'col_0'=4,'col_1'=2] {'row_0','row_1'..., dimensions={0} | all-to-all | bytes 2228224 | tf_op jit(solution)/shard_map/all_to_all | solution.py:230
  195.7 5.6 %products.10 = (f32[4,136,128]{2,1,0:T(8,128)S(1)}, f32[4,136,128]{2,1,0:T(8,128)S(1)}) custom-call(s32[160]{0:T(256)S(1)} %copy-done.4, s32[16]{0:T(128)S(1)} %copy-done.7, s32[2]{0:T(128)S(1)} %pad_add_fusion.place, bf16[128,128,128]{2,1,0:T(8,128)(2,1)S(1)} %bitcast.67, bf16[32,136,128]{2,1,0:T(8,128)(2,1)S(1)} %all_to_all.28.sources), custom_call_target="tpu_custom_call" | custom-call | tf_op jit(solution)/shard_map/products/pallas_call | solution.py:115
  201.6 1.3 collective-permute-done.16
  203.0 4.8 %collective-permute-start.19 = (f32[136,128]{1,0:T(8,128)S(1)}, f32[136,128]{1,0:T(8,128)S(1)}, u32[]{:S(2)}, u32[]{:S(2)}) collective-permute-start(f32[136,128]{1,0:T(8,128)S(1)} %get-tuple-element.82), channel_id=1, source_target_pairs={{0,6},{2,0},{4,2},{6,4},{1,7},{3,1},{5,3},{7,5},{8,14},{10,8},{12,... | collective-permute-start | bytes 208904 | tf_op jit(solution)/shard_map/ppermute | solution.py:187
  207.8 2.2 collective-permute-start.17
  210.0 2.6 collective-permute-done.19.refs_3_
  212.5 5.4 %collective-permute-done.18.refs_2_ = f32[136,128]{1,0:T(8,128)S(1)} collective-permute-done((f32[136,128]{1,0:T(8,128)S(1)}, f32[136,128]{1,0:T(8,128)S(1)}, u32[]{:S(2)}, u32[]{:S(2)}) %collective-permute-start.18) | collective-permute-done | bytes 69664 | tf_op jit(solution)/shard_map/ppermute | solution.py:187
  218.6 20.3 %all_to_all.29.sources = bf16[32,136,128]{2,1,0:T(8,128)(2,1)S(1)} all-to-all(bf16[32,136,128]{2,1,0:T(8,128)(2,1)S(1)} %get-tuple-element.63), channel_id=1, replica_groups=mesh['row_0'=4,'row_1'=2,'row_2'=4,'col_0'=4,'col_1'=2] {'row_0','row_1'..., dimensions={0} | all-to-all | bytes 2228224 | tf_op jit(solution)/shard_map/all_to_all | solution.py:230
  238.8 5.6 %products.11 = (f32[4,136,128]{2,1,0:T(8,128)S(1)}, f32[4,136,128]{2,1,0:T(8,128)S(1)}) custom-call(s32[160]{0:T(256)S(1)} %copy-done.4, s32[16]{0:T(128)S(1)} %copy-done.7, s32[2]{0:T(128)S(1)} %pad_add_fusion.place, bf16[128,128,128]{2,1,0:T(8,128)(2,1)S(1)} %bitcast.68, bf16[32,136,128]{2,1,0:T(8,128)(2,1)S(1)} %all_to_all.29.sources), custom_call_target="tpu_custom_call" | custom-call | tf_op jit(solution)/shard_map/products/pallas_call | solution.py:115
  246.5 4.9 %collective-permute-start.23 = (f32[136,128]{1,0:T(8,128)S(1)}, f32[136,128]{1,0:T(8,128)S(1)}, u32[]{:S(2)}, u32[]{:S(2)}) collective-permute-start(f32[136,128]{1,0:T(8,128)S(1)} %get-tuple-element.78), channel_id=1, source_target_pairs={{0,6},{2,0},{4,2},{6,4},{1,7},{3,1},{5,3},{7,5},{8,14},{10,8},{12,... | collective-permute-start | bytes 208904 | tf_op jit(solution)/shard_map/ppermute | solution.py:187
  251.4 2.2 collective-permute-start.21
  253.6 8.4 %collective-permute-done.22.refs_2_ = f32[136,128]{1,0:T(8,128)S(1)} collective-permute-done((f32[136,128]{1,0:T(8,128)S(1)}, f32[136,128]{1,0:T(8,128)S(1)}, u32[]{:S(2)}, u32[]{:S(2)}) %collective-permute-start.22) | collective-permute-done | bytes 69664 | tf_op jit(solution)/shard_map/ppermute | solution.py:187
  264.1 1.7 collective-permute-start.27
  266.2 1.8 collective-permute-start.25
  268.0 4.1 %collective-permute-done.26 = f32[4,128]{1,0:T(4,128)S(1)} collective-permute-done((f32[4,128]{1,0:T(4,128)S(1)}, f32[4,128]{1,0:T(4,128)S(1)}, u32[]{:S(2)}, u32[]{:S(2)}) %collective-permute-start.26) | collective-permute-done | bytes 2080 | tf_op jit(solution)/shard_map/ppermute | solution.py:187
  272.3 1.3 collective-permute-start.29
  274.7 1.6 collective-permute-done.29
  277.8 2.3 collective-permute-done.31
  280.2 1.3 collective-permute-start.34
  282.6 2.8 collective-permute-done.33
  (94 shorter events, 20.8 us)
Async XLA Ops:
  6.4 2.2 copy-start
  8.6 0.7 copy-start.3
  9.3 0.6 copy-start.6
  15.4 13.3 %copy-start.8 = (s32[128]{0:T(128)S(1)}, s32[128]{0:T(128)}, u32[]{:S(2)}) copy-start(s32[128]{0:T(128)} %param.11) | copy-start | bytes 1540
  15.5 21.0 %copy-start.5 = (s32[1,128]{1,0:T(1,128)S(1)}, s32[1,128]{1,0:T(1,128)}, u32[]{:S(2)}) copy-start(s32[1,128]{1,0:T(1,128)} %refs_4_.11) | copy-start | bytes 1540
  15.5 2.0 collective-permute-start
  17.5 11.3 %collective-permute-start.3 = (f32[136,128]{1,0:T(8,128)S(1)}, f32[136,128]{1,0:T(8,128)S(1)}, u32[]{:S(2)}, u32[]{:S(2)}) collective-permute-start(f32[136,128]{1,0:T(8,128)S(1)} %get-tuple-element.98), channel_id=1, source_target_pairs={{0,6},{2,0},{4,2},{6,4},{1,7},{3,1},{5,3},{7,5},{8,14},{10,8},{12,... | collective-permute-start | bytes 208904 | tf_op jit(solution)/shard_map/ppermute | solution.py:187
  26.6 9.9 %collective-permute-start.2 = (f32[136,128]{1,0:T(8,128)S(1)}, f32[136,128]{1,0:T(8,128)S(1)}, u32[]{:S(2)}, u32[]{:S(2)}) collective-permute-start(f32[136,128]{1,0:T(8,128)S(1)} %get-tuple-element.99), channel_id=1, source_target_pairs={{0,4},{2,6},{4,0},{6,2},{1,5},{3,7},{5,1},{7,3},{8,12},{10,14},{12... | collective-permute-start | bytes 208904 | tf_op jit(solution)/shard_map/ppermute | solution.py:187
  26.6 9.9 %collective-permute-start.1 = (f32[136,128]{1,0:T(8,128)S(1)}, f32[136,128]{1,0:T(8,128)S(1)}, u32[]{:S(2)}, u32[]{:S(2)}) collective-permute-start(f32[136,128]{1,0:T(8,128)S(1)} %get-tuple-element.100), channel_id=1, source_target_pairs={{0,2},{2,4},{4,6},{6,0},{1,3},{3,5},{5,7},{7,1},{8,10},{10,12},{12... | collective-permute-start | bytes 208904 | tf_op jit(solution)/shard_map/ppermute | solution.py:187
  37.0 23.1 %copy-start.4 = (s32[160]{0:T(256)S(1)}, s32[160]{0:T(256)}, u32[]{:S(2)}) copy-start(s32[160]{0:T(256)} %get-tuple-element.39.order) | copy-start | bytes 1924
  37.0 23.1 %copy-start.7 = (s32[16]{0:T(128)S(1)}, s32[16]{0:T(128)}, u32[]{:S(2)}) copy-start(s32[16]{0:T(128)} %get-tuple-element.40.starts) | copy-start | bytes 196
  60.1 2.2 copy-start.1
  62.3 46.0 %copy-start.2 = (bf16[1,1,128,128,128]{4,3,2,1,0:T(8,128)(2,1)S(1)}, bf16[1,1,128,128,128]{4,3,2,1,0:T(8,128)(2,1)}, u32[]{:S(2)}) copy-start(bf16[1,1,128,128,128]{4,3,2,1,0:T(8,128)(2,1)} %param.6) | copy-start | bytes 12582916
  67.9 2.0 collective-permute-start.4
  70.0 11.2 %collective-permute-start.7 = (f32[136,128]{1,0:T(8,128)S(1)}, f32[136,128]{1,0:T(8,128)S(1)}, u32[]{:S(2)}, u32[]{:S(2)}) collective-permute-start(f32[136,128]{1,0:T(8,128)S(1)} %get-tuple-element.94), channel_id=1, source_target_pairs={{0,6},{2,0},{4,2},{6,4},{1,7},{3,1},{5,3},{7,5},{8,14},{10,8},{12,... | collective-permute-start | bytes 208904 | tf_op jit(solution)/shard_map/ppermute | solution.py:187
  76.5 10.4 %collective-permute-start.6 = (f32[136,128]{1,0:T(8,128)S(1)}, f32[136,128]{1,0:T(8,128)S(1)}, u32[]{:S(2)}, u32[]{:S(2)}) collective-permute-start(f32[136,128]{1,0:T(8,128)S(1)} %get-tuple-element.95), channel_id=1, source_target_pairs={{0,4},{2,6},{4,0},{6,2},{1,5},{3,7},{5,1},{7,3},{8,12},{10,14},{12... | collective-permute-start | bytes 208904 | tf_op jit(solution)/shard_map/ppermute | solution.py:187
  76.5 10.4 %collective-permute-start.5 = (f32[136,128]{1,0:T(8,128)S(1)}, f32[136,128]{1,0:T(8,128)S(1)}, u32[]{:S(2)}, u32[]{:S(2)}) collective-permute-start(f32[136,128]{1,0:T(8,128)S(1)} %get-tuple-element.96), channel_id=1, source_target_pairs={{0,2},{2,4},{4,6},{6,0},{1,3},{3,5},{5,7},{7,1},{8,10},{10,12},{12... | collective-permute-start | bytes 208904 | tf_op jit(solution)/shard_map/ppermute | solution.py:187
  113.9 1.6 collective-permute-start.8
  115.6 9.5 %collective-permute-start.11 = (f32[136,128]{1,0:T(8,128)S(1)}, f32[136,128]{1,0:T(8,128)S(1)}, u32[]{:S(2)}, u32[]{:S(2)}) collective-permute-start(f32[136,128]{1,0:T(8,128)S(1)} %get-tuple-element.90), channel_id=1, source_target_pairs={{0,6},{2,0},{4,2},{6,4},{1,7},{3,1},{5,3},{7,5},{8,14},{10,8},{12,... | collective-permute-start | bytes 208904 | tf_op jit(solution)/shard_map/ppermute | solution.py:187
  120.4 9.9 %collective-permute-start.10 = (f32[136,128]{1,0:T(8,128)S(1)}, f32[136,128]{1,0:T(8,128)S(1)}, u32[]{:S(2)}, u32[]{:S(2)}) collective-permute-start(f32[136,128]{1,0:T(8,128)S(1)} %get-tuple-element.91), channel_id=1, source_target_pairs={{0,4},{2,6},{4,0},{6,2},{1,5},{3,7},{5,1},{7,3},{8,12},{10,14},{12... | collective-permute-start | bytes 208904 | tf_op jit(solution)/shard_map/ppermute | solution.py:187
  120.4 9.9 %collective-permute-start.9 = (f32[136,128]{1,0:T(8,128)S(1)}, f32[136,128]{1,0:T(8,128)S(1)}, u32[]{:S(2)}, u32[]{:S(2)}) collective-permute-start(f32[136,128]{1,0:T(8,128)S(1)} %get-tuple-element.92), channel_id=1, source_target_pairs={{0,2},{2,4},{4,6},{6,0},{1,3},{3,5},{5,7},{7,1},{8,10},{10,12},{12... | collective-permute-start | bytes 208904 | tf_op jit(solution)/shard_map/ppermute | solution.py:187
  156.4 2.4 collective-permute-start.12
  158.8 9.6 %collective-permute-start.15 = (f32[136,128]{1,0:T(8,128)S(1)}, f32[136,128]{1,0:T(8,128)S(1)}, u32[]{:S(2)}, u32[]{:S(2)}) collective-permute-start(f32[136,128]{1,0:T(8,128)S(1)} %get-tuple-element.86), channel_id=1, source_target_pairs={{0,6},{2,0},{4,2},{6,4},{1,7},{3,1},{5,3},{7,5},{8,14},{10,8},{12,... | collective-permute-start | bytes 208904 | tf_op jit(solution)/shard_map/ppermute | solution.py:187
  163.9 10.5 %collective-permute-start.14 = (f32[136,128]{1,0:T(8,128)S(1)}, f32[136,128]{1,0:T(8,128)S(1)}, u32[]{:S(2)}, u32[]{:S(2)}) collective-permute-start(f32[136,128]{1,0:T(8,128)S(1)} %get-tuple-element.87), channel_id=1, source_target_pairs={{0,4},{2,6},{4,0},{6,2},{1,5},{3,7},{5,1},{7,3},{8,12},{10,14},{12... | collective-permute-start | bytes 208904 | tf_op jit(solution)/shard_map/ppermute | solution.py:187
  163.9 10.5 %collective-permute-start.13 = (f32[136,128]{1,0:T(8,128)S(1)}, f32[136,128]{1,0:T(8,128)S(1)}, u32[]{:S(2)}, u32[]{:S(2)}) collective-permute-start(f32[136,128]{1,0:T(8,128)S(1)} %get-tuple-element.88), channel_id=1, source_target_pairs={{0,2},{2,4},{4,6},{6,0},{1,3},{3,5},{5,7},{7,1},{8,10},{10,12},{12... | collective-permute-start | bytes 208904 | tf_op jit(solution)/shard_map/ppermute | solution.py:187
  201.3 1.6 collective-permute-start.16
  203.0 9.5 %collective-permute-start.19 = (f32[136,128]{1,0:T(8,128)S(1)}, f32[136,128]{1,0:T(8,128)S(1)}, u32[]{:S(2)}, u32[]{:S(2)}) collective-permute-start(f32[136,128]{1,0:T(8,128)S(1)} %get-tuple-element.82), channel_id=1, source_target_pairs={{0,6},{2,0},{4,2},{6,4},{1,7},{3,1},{5,3},{7,5},{8,14},{10,8},{12,... | collective-permute-start | bytes 208904 | tf_op jit(solution)/shard_map/ppermute | solution.py:187
  207.8 10.2 %collective-permute-start.18 = (f32[136,128]{1,0:T(8,128)S(1)}, f32[136,128]{1,0:T(8,128)S(1)}, u32[]{:S(2)}, u32[]{:S(2)}) collective-permute-start(f32[136,128]{1,0:T(8,128)S(1)} %get-tuple-element.83), channel_id=1, source_target_pairs={{0,4},{2,6},{4,0},{6,2},{1,5},{3,7},{5,1},{7,3},{8,12},{10,14},{12... | collective-permute-start | bytes 208904 | tf_op jit(solution)/shard_map/ppermute | solution.py:187
  207.8 10.2 %collective-permute-start.17 = (f32[136,128]{1,0:T(8,128)S(1)}, f32[136,128]{1,0:T(8,128)S(1)}, u32[]{:S(2)}, u32[]{:S(2)}) collective-permute-start(f32[136,128]{1,0:T(8,128)S(1)} %get-tuple-element.84), channel_id=1, source_target_pairs={{0,2},{2,4},{4,6},{6,0},{1,3},{3,5},{5,7},{7,1},{8,10},{10,12},{12... | collective-permute-start | bytes 208904 | tf_op jit(solution)/shard_map/ppermute | solution.py:187
  244.4 2.0 collective-permute-start.20
  246.5 7.1 %collective-permute-start.23 = (f32[136,128]{1,0:T(8,128)S(1)}, f32[136,128]{1,0:T(8,128)S(1)}, u32[]{:S(2)}, u32[]{:S(2)}) collective-permute-start(f32[136,128]{1,0:T(8,128)S(1)} %get-tuple-element.78), channel_id=1, source_target_pairs={{0,6},{2,0},{4,2},{6,4},{1,7},{3,1},{5,3},{7,5},{8,14},{10,8},{12,... | collective-permute-start | bytes 208904 | tf_op jit(solution)/shard_map/ppermute | solution.py:187
  251.4 10.5 %collective-permute-start.22 = (f32[136,128]{1,0:T(8,128)S(1)}, f32[136,128]{1,0:T(8,128)S(1)}, u32[]{:S(2)}, u32[]{:S(2)}) collective-permute-start(f32[136,128]{1,0:T(8,128)S(1)} %get-tuple-element.79), channel_id=1, source_target_pairs={{0,4},{2,6},{4,0},{6,2},{1,5},{3,7},{5,1},{7,3},{8,12},{10,14},{12... | collective-permute-start | bytes 208904 | tf_op jit(solution)/shard_map/ppermute | solution.py:187
  251.4 10.5 %collective-permute-start.21 = (f32[136,128]{1,0:T(8,128)S(1)}, f32[136,128]{1,0:T(8,128)S(1)}, u32[]{:S(2)}, u32[]{:S(2)}) collective-permute-start(f32[136,128]{1,0:T(8,128)S(1)} %get-tuple-element.80), channel_id=1, source_target_pairs={{0,2},{2,4},{4,6},{6,0},{1,3},{3,5},{5,7},{7,1},{8,10},{10,12},{12... | collective-permute-start | bytes 208904 | tf_op jit(solution)/shard_map/ppermute | solution.py:187
  262.6 1.4 collective-permute-start.24
  264.1 4.0 %collective-permute-start.27 = (f32[4,128]{1,0:T(4,128)S(1)}, f32[4,128]{1,0:T(4,128)S(1)}, u32[]{:S(2)}, u32[]{:S(2)}) collective-permute-start(f32[4,128]{1,0:T(4,128)S(1)} %broadcast_select_fusion.2), channel_id=1, source_target_pairs={{0,6},{2,0},{4,2},{6,4},{1,7},{3,1},{5,3},{7,5},{8,14},{10,8},{12,... | collective-permute-start | bytes 6152 | tf_op jit(solution)/shard_map/ppermute | solution.py:187
  265.7 6.3 %collective-permute-start.26 = (f32[4,128]{1,0:T(4,128)S(1)}, f32[4,128]{1,0:T(4,128)S(1)}, u32[]{:S(2)}, u32[]{:S(2)}) collective-permute-start(f32[4,128]{1,0:T(4,128)S(1)} %broadcast_select_fusion.2), channel_id=1, source_target_pairs={{0,4},{2,6},{4,0},{6,2},{1,5},{3,7},{5,1},{7,3},{8,12},{10,14},{12... | collective-permute-start | bytes 6152 | tf_op jit(solution)/shard_map/ppermute | solution.py:187
  266.2 5.9 %collective-permute-start.25 = (f32[4,128]{1,0:T(4,128)S(1)}, f32[4,128]{1,0:T(4,128)S(1)}, u32[]{:S(2)}, u32[]{:S(2)}) collective-permute-start(f32[4,128]{1,0:T(4,128)S(1)} %broadcast_select_fusion.2), channel_id=1, source_target_pairs={{0,2},{2,4},{4,6},{6,0},{1,3},{3,5},{5,7},{7,1},{8,10},{10,12},{12... | collective-permute-start | bytes 6152 | tf_op jit(solution)/shard_map/ppermute | solution.py:187
  272.2 2.4 collective-permute-start.30
  272.3 4.0 %collective-permute-start.29 = (f32[4,128]{1,0:T(4,128)S(1)}, f32[4,128]{1,0:T(4,128)S(1)}, u32[]{:S(2)}, u32[]{:S(2)}) collective-permute-start(f32[4,128]{1,0:T(4,128)S(1)} %broadcast_select_fusion.1), channel_id=1, source_target_pairs={{0,128},{64,192},{128,0},{192,64},{1,129},{65,193},{129,1},{193,65... | collective-permute-start | bytes 6152 | tf_op jit(solution)/shard_map/ppermute | solution.py:187
  273.6 3.6 %collective-permute-start.28 = (f32[4,128]{1,0:T(4,128)S(1)}, f32[4,128]{1,0:T(4,128)S(1)}, u32[]{:S(2)}, u32[]{:S(2)}) collective-permute-start(f32[4,128]{1,0:T(4,128)S(1)} %broadcast_select_fusion.1), channel_id=1, source_target_pairs={{0,64},{64,128},{128,192},{192,0},{1,65},{65,129},{129,193},{193,1... | collective-permute-start | bytes 6152 | tf_op jit(solution)/shard_map/ppermute | solution.py:187
  277.3 2.7 collective-permute-start.31
  280.2 2.4 collective-permute-start.34
  281.5 3.9 %collective-permute-start.33 = (f32[4,128]{1,0:T(4,128)S(1)}, f32[4,128]{1,0:T(4,128)S(1)}, u32[]{:S(2)}, u32[]{:S(2)}) collective-permute-start(f32[4,128]{1,0:T(4,128)S(1)} %broadcast_select_fusion), channel_id=1, source_target_pairs={{0,16},{8,24},{16,0},{24,8},{1,17},{9,25},{17,1},{25,9},{2,18},{10... | collective-permute-start | bytes 6152 | tf_op jit(solution)/shard_map/ppermute | solution.py:187
  281.7 3.7 %collective-permute-start.32 = (f32[4,128]{1,0:T(4,128)S(1)}, f32[4,128]{1,0:T(4,128)S(1)}, u32[]{:S(2)}, u32[]{:S(2)}) collective-permute-start(f32[4,128]{1,0:T(4,128)S(1)} %broadcast_select_fusion), channel_id=1, source_target_pairs={{0,8},{8,16},{16,24},{24,0},{1,9},{9,17},{17,25},{25,1},{2,10},{10... | collective-permute-start | bytes 6152 | tf_op jit(solution)/shard_map/ppermute | solution.py:187

commit v2 on v1

v2 whole, which is shorter than its diff:
```python
import jax
import jax.numpy as jnp
from jax import lax
from jax.experimental import pallas as pl
from jax.experimental.pallas import tpu as pltpu
from jax.sharding import Mesh
from jax.sharding import PartitionSpec as P

TILE = 128
PANEL = 128
LEVELS = 6
KMAX = 128
DEST_TILES = 8
SRC_TILES = 32
VERTICES = 32768
EPSILON = 1e-06
ROW = ("row_0", "row_1", "row_2")
COL = ("col_0", "col_1")
ROW_COL = ROW + COL
HALF = TILE // 2
EXTRA = 8
ROWS = TILE + EXTRA
CODED = HALF + EXTRA
TOP = 65535.0
FETCH = 16
DEPTH = 1024
SMEM = pl.BlockSpec(memory_space=pltpu.SMEM)
VMEM = pl.BlockSpec(memory_space=pltpu.VMEM)
LIMIT = pltpu.CompilerParams(vmem_limit_bytes=24 * 1024 * 1024)


def f32(x):
    return x.astype(jnp.float32)


def multiply(dense, held, extra, out):
    for k in range(4):
        out[k, 0:TILE, :] = jnp.zeros((TILE, PANEL), jnp.float32)
        out[k, TILE:ROWS, :] = extra[...]

    def turn(n, carry):
        part = pl.ds(pl.multiple_of(n * DEPTH, DEPTH), DEPTH)
        product = jnp.dot(dense[:, part], held[part, :], preferred_element_type=jnp.float32)
        for k in range(4):
            out[k, 0:TILE, :] = out[k, 0:TILE, :] + product[k * TILE : (k + 1) * TILE]
        return carry

    lax.fori_loop(0, SRC_TILES * TILE // DEPTH, turn, 0)


def first_kernel(
    rows, cols, place, ids, adj, away_out, kept_out, away_dense, kept_dense,
    away, kept, staged, held, extra, sems, stores,
):
    live, c1 = place[0], place[2]

    def fetch(n):
        part = pl.ds(n * FETCH, FETCH)
        return pltpu.make_async_copy(adj.at[part], staged.at[part], sems.at[n])

    for n in range(KMAX // FETCH):

        @pl.when(n * FETCH < live)
        def _(n=n):
            fetch(n).start()

    def clear(i, carry):
        part = pl.ds(pl.multiple_of(i * TILE, TILE), TILE)
        blank = jnp.zeros((TILE, SRC_TILES * TILE), jnp.bfloat16)
        away[part, :] = blank
        kept[part, :] = blank
        return carry

    lax.fori_loop(0, DEST_TILES // 2, clear, 0)
    column = place[1] * 2 + c1
    inner = lax.broadcasted_iota(jnp.int32, (TILE, PANEL), 0)
    wanted = jnp.broadcast_to(ids[...], (TILE, PANEL)) - inner
    for t in range(SRC_TILES):
        hit = wanted == (t * DEST_TILES + column) * TILE
        held[t * TILE : (t + 1) * TILE, :] = jnp.where(hit, 1.0, 0.0).astype(jnp.bfloat16)
    extra[...] = jnp.zeros((EXTRA, PANEL), jnp.float32)

    def add(k, carry):
        d, u = rows[k], cols[k]
        down = pl.ds(pl.multiple_of((d >> 1) * TILE, TILE), TILE)
        across = pl.ds(pl.multiple_of(u * TILE, TILE), TILE)

        @pl.when((d & 1) == c1)
        def _():
            kept[down, across] = kept[down, across] + staged[k]

        @pl.when((d & 1) != c1)
        def _():
            away[down, across] = away[down, across] + staged[k]

        return carry

    for n in range(KMAX // FETCH):

        @pl.when(n * FETCH < live)
        def _(n=n):
            fetch(n).wait()
            lax.fori_loop(n * FETCH, jnp.minimum(live, (n + 1) * FETCH), add, 0)

    pairs = ((away, away_dense), (kept, kept_dense))
    copies = [pltpu.make_async_copy(v, h, stores.at[i]) for i, (v, h) in enumerate(pairs)]
    for copy in copies:
        copy.start()
    multiply(away, held, extra, away_out)
    multiply(kept, held, extra, kept_out)
    for copy in copies:
        copy.wait()


def first_products(rows, cols, place, ids, adj):
    hbm = pl.BlockSpec(memory_space=pltpu.HBM)
    half = (DEST_TILES // 2 * TILE, SRC_TILES * TILE)
    chunks = jax.ShapeDtypeStruct((4, ROWS, PANEL), jnp.float32)
    dense = jax.ShapeDtypeStruct(half, jnp.bfloat16)
    return pl.pallas_call(
        first_kernel,
        in_specs=[SMEM, SMEM, SMEM, VMEM, hbm],
        out_specs=[VMEM, VMEM, hbm, hbm],
        out_shape=[chunks, chunks, dense, dense],
        scratch_shapes=[
            pltpu.VMEM(half, jnp.bfloat16),
            pltpu.VMEM(half, jnp.bfloat16),
            pltpu.VMEM((KMAX, TILE, TILE), jnp.bfloat16),
            pltpu.VMEM((SRC_TILES * TILE, PANEL), jnp.bfloat16),
            pltpu.VMEM((EXTRA, PANEL), jnp.float32),
            pltpu.SemaphoreType.DMA((KMAX // FETCH,)),
            pltpu.SemaphoreType.DMA((2,)),
        ],
        compiler_params=LIMIT,
        name="first_products",
    )(rows, cols, place, ids, pltpu.with_memory_space_constraint(adj, pltpu.HBM))


def away_kernel(place, dense, sources, out, held, extra):
    parts = jnp.sum(f32(sources[:, TILE:ROWS, :]), axis=0)
    squares = (parts[0:1] + parts[1:2]) + parts[2:3]
    row = lax.broadcasted_iota(jnp.int32, (EXTRA, PANEL), 0)
    extra[...] = jnp.where(row == place[2], jnp.broadcast_to(squares, (EXTRA, PANEL)), 0.0)
    for t in range(SRC_TILES):
        held[t * TILE : (t + 1) * TILE, :] = sources[t, 0:TILE, :]
    multiply(dense, held, extra, out)


def away_products(place, dense, sources):
    return pl.pallas_call(
        away_kernel,
        in_specs=[SMEM, VMEM, VMEM],
        out_specs=[VMEM] * 3,
        out_shape=[
            jax.ShapeDtypeStruct((4, ROWS, PANEL), jnp.float32),
            jax.ShapeDtypeStruct((SRC_TILES * TILE, PANEL), jnp.bfloat16),
            jax.ShapeDtypeStruct((EXTRA, PANEL), jnp.float32),
        ],
        compiler_params=LIMIT,
        name="away_products",
    )(place, dense, sources)


def kept_products(dense, held, extra):
    return pl.pallas_call(
        multiply,
        in_specs=[VMEM] * 3,
        out_specs=VMEM,
        out_shape=jax.ShapeDtypeStruct((4, ROWS, PANEL), jnp.float32),
        compiler_params=LIMIT,
        name="kept_products",
    )(dense, held, extra)


def as_integers(x):
    x = jnp.maximum(x, 2.0**-80)
    exponent = jnp.floor(jnp.log2(x)) - 22.0
    return jnp.floor(x * jnp.exp2(-exponent) + 0.5), exponent


def encode_kernel(kept, away, coded):
    row = lax.broadcasted_iota(jnp.int32, (EXTRA, PANEL), 0)
    for k in range(4):
        total = kept[k] + away[k]
        sums = total[0:TILE]
        lines = list(as_integers(jnp.max(sums, axis=0, keepdims=True)))
        factor = TOP / (lines[0] * jnp.exp2(lines[1]))
        codes = jnp.minimum(jnp.floor(sums * factor + 0.5), TOP).astype(jnp.int32)
        coded[k, 0:HALF, :] = lax.shift_left(codes[0:HALF], 16) | codes[HALF:TILE]
        lines += as_integers(total[TILE : TILE + 1])
        lines += as_integers(total[TILE + 1 : TILE + 2])
        tail = jnp.zeros((EXTRA, PANEL), jnp.float32)
        for n, line in enumerate(lines):
            tail = jnp.where(row == n, jnp.broadcast_to(line, (EXTRA, PANEL)), tail)
        coded[k, HALF:CODED, :] = tail.astype(jnp.int32)


def encoded(kept, away):
    return pl.pallas_call(
        encode_kernel,
        in_specs=[VMEM] * 2,
        out_specs=VMEM,
        out_shape=jax.ShapeDtypeStruct((4, CODED, PANEL), jnp.int32),
        compiler_params=LIMIT,
        name="encoded",
    )(kept, away)


def split3(x):
    high = f32(x.astype(jnp.bfloat16))
    rest = x - high
    middle = f32(rest.astype(jnp.bfloat16))
    return high, middle, rest - middle


def level_kernel(level, coded, depth, raw_in, sums_in, sums, raw, squares, scale, *spread):
    highs = jnp.zeros((HALF, PANEL), jnp.float32)
    lows = jnp.zeros((HALF, PANEL), jnp.float32)
    mean_square = jnp.zeros((1, PANEL), jnp.float32)
    for k in range(4):
        tail = f32(coded[k, HALF:CODED, :])
        power = jnp.exp2(jnp.minimum(tail, 127.0))
        step = tail[0:1] * power[1:2] * (1.0 / TOP)
        mean_square = mean_square + tail[2:3] * power[3:4]
        mean_square = mean_square + tail[4:5] * power[5:6]
        codes = coded[k, 0:HALF, :]
        highs = highs + f32(lax.shift_right_logical(codes, 16)) * step
        lows = lows + f32(codes & 65535) * step
    product = jnp.concatenate([highs, lows], axis=0)
    reached = depth[...] >= level
    if level == 1:
        sums[...] = sums_in[...]
        scale[...] = jnp.zeros((1, PANEL), jnp.float32)
    else:
        mean_square = mean_square / VERTICES + EPSILON
        scale[...] = mean_square
        inverse = lax.rsqrt(mean_square)
        sums[...] = sums_in[...] + raw_in[...] * inverse
        product = product * inverse
    paths = jnp.where(reached, product, 0.0)
    raw[...] = paths
    square = jnp.sum(paths * paths, axis=0, keepdims=True)
    squares[...] = square
    if level < LEVELS:
        row = lax.broadcasted_iota(jnp.int32, (EXTRA, PANEL), 0)
        tail = jnp.zeros((EXTRA, PANEL), jnp.float32)
        for n, line in enumerate(split3(square)):
            tail = jnp.where(row == n, jnp.broadcast_to(line, (EXTRA, PANEL)), tail)
        sent, tail = paths.astype(jnp.bfloat16), tail.astype(jnp.bfloat16)
        for t in range(SRC_TILES):
            spread[0][t, 0:TILE, :] = sent
            spread[0][t, TILE:ROWS, :] = tail


def finish_level(level, chunks, depth, raw, sums):
    panel = jax.ShapeDtypeStruct((TILE, PANEL), jnp.float32)
    line = jax.ShapeDtypeStruct((1, PANEL), jnp.float32)
    spread = jax.ShapeDtypeStruct((SRC_TILES, ROWS, PANEL), jnp.bfloat16)
    shapes = [panel, panel, line, line] + ([spread] if level < LEVELS else [])
    return pl.pallas_call(
        lambda *refs: level_kernel(level, *refs),
        in_specs=[VMEM] * 4,
        out_specs=[VMEM] * len(shapes),
        out_shape=shapes,
        compiler_params=LIMIT,
        name=f"level_{level}",
    )(chunks, depth, raw, sums)


def from_partner(x):
    return lax.ppermute(x, "col_1", [(0, 1), (1, 0)])


def summed_alike(x, axes):
    copies = jnp.broadcast_to(x, (lax.axis_size(axes), EXTRA, PANEL))
    return jnp.sum(lax.all_to_all(copies, axes, 0, 0, tiled=True)[:, 0], axis=0, keepdims=True)


def local(adj_tiles, tile_rows, tile_cols, tile_count, tile_depth, source_ids):
    position = lax.axis_index(ROW) * DEST_TILES + lax.axis_index(COL)
    place = jnp.stack([tile_count[0, 0], lax.axis_index("col_0"), lax.axis_index("col_1")])
    away, kept, away_dense, kept_dense = first_products(
        tile_rows[0, 0], tile_cols[0, 0], place, source_ids[None, :], adj_tiles[0, 0]
    )
    vertex = position * TILE + jnp.arange(TILE, dtype=jnp.int32)
    sums = f32(vertex[:, None] == source_ids[None, :])
    raw = sums
    scales = []
    for level in range(1, LEVELS + 1):
        if level > 1:
            sources = lax.all_to_all(spread[0], ROW, 0, 0, tiled=True)
            away, held, extra = away_products(place, away_dense, sources)
            kept = kept_products(kept_dense, held, extra)
        coded = encoded(kept, from_partner(away))
        coded = lax.all_to_all(coded, "col_0", 0, 0, tiled=True)
        sums, raw, squares, scale, *spread = finish_level(level, coded, tile_depth, raw, sums)
        if level > 1:
            scales.append(scale)
    total = summed_alike(summed_alike(squares, ("row_1",) + COL), ("row_0", "row_2"))
    mean_square = total / VERTICES + EPSILON
    scales.append(mean_square)
    path_sums = sums + raw * lax.rsqrt(mean_square)
    return path_sums, 0.5 * jnp.log(jnp.concatenate(scales, axis=0))


def solution(mesh):
    split = Mesh(mesh.devices.reshape(4, 2, 4, 4, 2), ROW_COL)
    in_specs = (
        P(ROW, COL, None, None, None),
        P(ROW, COL, None),
        P(ROW, COL, None),
        P(ROW, COL),
        P(ROW_COL, None),
        P(),
    )
    out_specs = (P(ROW_COL, None), P())
    return jax.shard_map(local, mesh=split, in_specs=in_specs, out_specs=out_specs, check_vma=False)
```

time: 290 us -> 257 us (0.89); the launches traced: 287 us -> 257 us
  blocking collectives: 105 us -> 177 us
  waiting for transfers between devices: 69.5 us -> 8.49 us
  starting transfers between devices: 61 us -> 27.6 us
  Pallas kernels: 40.6 us -> 32.9 us
    all_to_all x5 -> x12, blocking collectives: 105 us -> 177 us  [the longest x5 102 us: local(): sources = lax.all_to_all(spread[0], ROW, 0, 0, tiled=True)]
    ppermute x35 -> x6, waiting for transfers between devices: 69.5 us -> 1.19 us  [from_partner(): return lax.ppermute(x, 'col_1', [(0, 1), (1, 0)])]
    ppermute x35 -> x6, starting transfers between devices: 61 us -> 21.4 us  [from_partner(): return lax.ppermute(x, 'col_1', [(0, 1), (1, 0)])]
    pallas_call x13 -> x23, Pallas kernels: 40.6 us -> 32.9 us  [the longest x5 12 us: away_products(): pl.pallas_call(away_kernel, in_specs=[SMEM, VMEM, VMEM], out_specs=[VMEM]...]
    all_to_all x0 -> x1, waiting for transfers between devices: none -> 7.3 us  [local(): coded = lax.all_to_all(coded, 'col_0', 0, 0, tiled=True)]
    all_to_all x0 -> x1, starting transfers between devices: none -> 6.27 us  [local(): coded = lax.all_to_all(coded, 'col_0', 0, 0, tiled=True)]
    unnamed x18 -> x20, local copies, waits for them, and re-layouts: 5.68 us -> 8.11 us
  transfers between devices with their start and end apart: 35 -> 7, of which waited for: 24 -> 2; matrix products, arithmetic and copies ran while one was open for 0% -> 0% of each run, Pallas kernels for 0% -> 3%
where the time goes in v2:
time: 257 us
  blocking collectives  177 us (69%)
  Pallas kernels  32.9 us (13%)
  starting transfers between devices  27.6 us (11%)
  waiting for transfers between devices  8.49 us (3%)
  local copies, waits for them, and re-layouts  8.16 us (3%)
    all_to_all x5, blocking collectives, local(): sources = lax.all_to_all(spread[0], ROW, 0, 0, tiled=True)  102 us
    all_to_all x5, blocking collectives, local(): coded = lax.all_to_all(coded, 'col_0', 0, 0, tiled=True)  53.5 us
    all_to_all x2, blocking collectives, summed_alike(): lax.all_to_all(copies, axes, 0, 0, tiled=True)[:, 0]  21.4 us
    ppermute x6, starting transfers between devices, from_partner(): return lax.ppermute(x, 'col_1', [(0, 1), (1, 0)])  21.4 us
    pallas_call x5, Pallas kernels, away_products(): pl.pallas_call(away_kernel, in_specs=[SMEM, VMEM, VMEM], out_specs=[VMEM]...  12 us
    pallas_call x5, Pallas kernels, kept_products(): pl.pallas_call(multiply, in_specs=[VMEM] * 3, out_specs=VMEM, out_shape=j...  8.99 us
    unnamed x20, local copies, waits for them, and re-layouts  8.11 us
    all_to_all x1, waiting for transfers between devices, local(): coded = lax.all_to_all(coded, 'col_0', 0, 0, tiled=True)  7.3 us
  transfers between devices with their start and end apart: 7, of which 2 were waited for; matrix products, arithmetic and copies ran while one was open for 0% of the time, Pallas kernels for 3%

profile of v2, /device:TPU:1, one launch (start us, length us, event | category | flops | bytes accessed | tf_op | source)
XLA Modules:
  0.0 257.0 jit_solution(4405240985323596939)
XLA Ops:
  1.4 0.7 copy-done.6
  2.0 0.7 copy-done.8
  2.7 0.7 copy-done.9
  3.3 7.2 %first_products.1 = (f32[4,136,128]{2,1,0:T(8,128)S(1)}, f32[4,136,128]{2,1,0:T(8,128)S(1)}, bf16[512,4096]{1,0:T(8,128)(2,1)S(1)}, bf16[512,4096]{1,0:T(8,128)(2,1)S(1)}) custom-call(s32[128]{0:T(128)S(1)} %bitcast.15, s32[128]{0:T(128)S(1)} %bitcast.16, s32[3]{0:T(128)S(1)} %pad_add_fusion.place, s32[1,128]{1,0:T(1,128)S(1)} %bitcast.13, ...), custom_call_target="tpu_custom_call" | custom-call | tf_op jit(solution)/shard_map/first_products/pallas_call | solution.py:120
  10.6 1.9 copy-done
  12.5 2.0 copy-done.2
  14.5 3.3 %collective-permute-start = (f32[4,136,128]{2,1,0:T(8,128)S(1)}, f32[4,136,128]{2,1,0:T(8,128)S(1)}, u32[]{:S(2)}, u32[]{:S(2)}) collective-permute-start(f32[4,136,128]{2,1,0:T(8,128)S(1)} %get-tuple-element.47), channel_id=1, source_target_pairs={{0,1},{1,0},{2,3},{3,2},{4,5},{5,4},{6,7},{7,6},{8,9},{9,8},{10,11... | collective-permute-start | bytes 835592 | tf_op jit(solution)/shard_map/ppermute | solution.py:271
  17.9 1.2 collective-permute-done.away
  19.0 0.8 encoded.6
  19.8 6.3 %all-to-all-start = ((s32[4,72,128]{2,1,0:T(8,128)}), s32[4,72,128]{2,1,0:T(8,128)S(1)}, u32[]{:S(2)}, u32[]{:S(2)}) async-start(s32[4,72,128]{2,1,0:T(8,128)} %encoded.6), calls=%async_computation | async-start | bytes 294912 | tf_op jit(solution)/shard_map/all_to_all | solution.py:295
  26.2 7.3 %all-to-all-done.refs_0_ = s32[4,72,128]{2,1,0:T(8,128)S(1)} async-done(((s32[4,72,128]{2,1,0:T(8,128)}), s32[4,72,128]{2,1,0:T(8,128)S(1)}, u32[]{:S(2)}, u32[]{:S(2)}) %all-to-all-start) | async-done | bytes 147488 | tf_op jit(solution)/shard_map/all_to_all | solution.py:295
  33.5 0.6 level_1.1
  34.1 25.6 %all_to_all.65.sources = bf16[32,136,128]{2,1,0:T(8,128)(2,1)S(1)} all-to-all(bf16[32,136,128]{2,1,0:T(8,128)(2,1)S(1)} %get-tuple-element.48), channel_id=1, replica_groups=mesh['row_0'=4,'row_1'=2,'row_2'=4,'col_0'=4,'col_1'=2] {'row_0','row_1'..., dimensions={0} | all-to-all | bytes 2228224 | tf_op jit(solution)/shard_map/all_to_all | solution.py:291
  59.7 2.2 copy-done.3
  61.9 2.4 away_products.5
  64.3 3.2 %collective-permute-start.1 = (f32[4,136,128]{2,1,0:T(8,128)S(1)}, f32[4,136,128]{2,1,0:T(8,128)S(1)}, u32[]{:S(2)}, u32[]{:S(2)}) collective-permute-start(f32[4,136,128]{2,1,0:T(8,128)S(1)} %get-tuple-element.51), channel_id=1, source_target_pairs={{0,1},{1,0},{2,3},{3,2},{4,5},{5,4},{6,7},{7,6},{8,9},{9,8},{10,11... | collective-permute-start | bytes 835592 | tf_op jit(solution)/shard_map/ppermute | solution.py:271
  67.5 1.8 kept_products.5.kept
  69.3 0.1 encoded.7
  69.5 10.5 %all_to_all.66.refs_0_ = s32[4,72,128]{2,1,0:T(8,128)S(1)} all-to-all(s32[4,72,128]{2,1,0:T(8,128)S(1)} %encoded.7), channel_id=1, replica_groups=mesh['row_0'=4,'row_1'=2,'row_2'=4,'col_0'=4,'col_1'=2] {'col_0'}, dimensions={0} | all-to-all | bytes 294912 | tf_op jit(solution)/shard_map/all_to_all | solution.py:295
  80.0 0.6 level_2.1
  80.7 18.9 %all_to_all.67.sources = bf16[32,136,128]{2,1,0:T(8,128)(2,1)S(1)} all-to-all(bf16[32,136,128]{2,1,0:T(8,128)(2,1)S(1)} %get-tuple-element.54), channel_id=1, replica_groups=mesh['row_0'=4,'row_1'=2,'row_2'=4,'col_0'=4,'col_1'=2] {'row_0','row_1'..., dimensions={0} | all-to-all | bytes 2228224 | tf_op jit(solution)/shard_map/all_to_all | solution.py:291
  99.5 2.4 away_products.6
  102.0 3.8 %collective-permute-start.2 = (f32[4,136,128]{2,1,0:T(8,128)S(1)}, f32[4,136,128]{2,1,0:T(8,128)S(1)}, u32[]{:S(2)}, u32[]{:S(2)}) collective-permute-start(f32[4,136,128]{2,1,0:T(8,128)S(1)} %get-tuple-element.57), channel_id=1, source_target_pairs={{0,1},{1,0},{2,3},{3,2},{4,5},{5,4},{6,7},{7,6},{8,9},{9,8},{10,11... | collective-permute-start | bytes 835592 | tf_op jit(solution)/shard_map/ppermute | solution.py:271
  105.8 1.8 kept_products.6.kept
  107.6 0.1 encoded.8
  107.8 10.8 %all_to_all.68.refs_0_ = s32[4,72,128]{2,1,0:T(8,128)S(1)} all-to-all(s32[4,72,128]{2,1,0:T(8,128)S(1)} %encoded.8), channel_id=1, replica_groups=mesh['row_0'=4,'row_1'=2,'row_2'=4,'col_0'=4,'col_1'=2] {'col_0'}, dimensions={0} | all-to-all | bytes 294912 | tf_op jit(solution)/shard_map/all_to_all | solution.py:295
  118.5 0.6 level_3.1
  119.1 19.0 %all_to_all.69.sources = bf16[32,136,128]{2,1,0:T(8,128)(2,1)S(1)} all-to-all(bf16[32,136,128]{2,1,0:T(8,128)(2,1)S(1)} %get-tuple-element.60), channel_id=1, replica_groups=mesh['row_0'=4,'row_1'=2,'row_2'=4,'col_0'=4,'col_1'=2] {'row_0','row_1'..., dimensions={0} | all-to-all | bytes 2228224 | tf_op jit(solution)/shard_map/all_to_all | solution.py:291
  138.2 2.4 away_products.7
  140.6 3.8 %collective-permute-start.3 = (f32[4,136,128]{2,1,0:T(8,128)S(1)}, f32[4,136,128]{2,1,0:T(8,128)S(1)}, u32[]{:S(2)}, u32[]{:S(2)}) collective-permute-start(f32[4,136,128]{2,1,0:T(8,128)S(1)} %get-tuple-element.63), channel_id=1, source_target_pairs={{0,1},{1,0},{2,3},{3,2},{4,5},{5,4},{6,7},{7,6},{8,9},{9,8},{10,11... | collective-permute-start | bytes 835592 | tf_op jit(solution)/shard_map/ppermute | solution.py:271
  144.3 1.8 kept_products.7.kept
  146.3 10.8 %all_to_all.70.refs_0_ = s32[4,72,128]{2,1,0:T(8,128)S(1)} all-to-all(s32[4,72,128]{2,1,0:T(8,128)S(1)} %encoded.9), channel_id=1, replica_groups=mesh['row_0'=4,'row_1'=2,'row_2'=4,'col_0'=4,'col_1'=2] {'col_0'}, dimensions={0} | all-to-all | bytes 294912 | tf_op jit(solution)/shard_map/all_to_all | solution.py:295
  157.1 0.6 level_4.1
  157.7 19.0 %all_to_all.71.sources = bf16[32,136,128]{2,1,0:T(8,128)(2,1)S(1)} all-to-all(bf16[32,136,128]{2,1,0:T(8,128)(2,1)S(1)} %get-tuple-element.66), channel_id=1, replica_groups=mesh['row_0'=4,'row_1'=2,'row_2'=4,'col_0'=4,'col_1'=2] {'row_0','row_1'..., dimensions={0} | all-to-all | bytes 2228224 | tf_op jit(solution)/shard_map/all_to_all | solution.py:291
  176.7 2.4 away_products.8
  179.1 3.8 %collective-permute-start.4 = (f32[4,136,128]{2,1,0:T(8,128)S(1)}, f32[4,136,128]{2,1,0:T(8,128)S(1)}, u32[]{:S(2)}, u32[]{:S(2)}) collective-permute-start(f32[4,136,128]{2,1,0:T(8,128)S(1)} %get-tuple-element.69), channel_id=1, source_target_pairs={{0,1},{1,0},{2,3},{3,2},{4,5},{5,4},{6,7},{7,6},{8,9},{9,8},{10,11... | collective-permute-start | bytes 835592 | tf_op jit(solution)/shard_map/ppermute | solution.py:271
  182.9 1.8 kept_products.8.kept
  184.8 10.8 %all_to_all.72.refs_0_ = s32[4,72,128]{2,1,0:T(8,128)S(1)} all-to-all(s32[4,72,128]{2,1,0:T(8,128)S(1)} %encoded.10), channel_id=1, replica_groups=mesh['row_0'=4,'row_1'=2,'row_2'=4,'col_0'=4,'col_1'=2] {'col_0'}, dimensions={0} | all-to-all | bytes 294912 | tf_op jit(solution)/shard_map/all_to_all | solution.py:295
  195.6 0.6 level_5.1
  196.2 19.4 %all_to_all.73.sources = bf16[32,136,128]{2,1,0:T(8,128)(2,1)S(1)} all-to-all(bf16[32,136,128]{2,1,0:T(8,128)(2,1)S(1)} %get-tuple-element.72), channel_id=1, replica_groups=mesh['row_0'=4,'row_1'=2,'row_2'=4,'col_0'=4,'col_1'=2] {'row_0','row_1'..., dimensions={0} | all-to-all | bytes 2228224 | tf_op jit(solution)/shard_map/all_to_all | solution.py:291
  215.7 2.4 away_products.9
  218.1 3.4 %collective-permute-start.5 = (f32[4,136,128]{2,1,0:T(8,128)S(1)}, f32[4,136,128]{2,1,0:T(8,128)S(1)}, u32[]{:S(2)}, u32[]{:S(2)}) collective-permute-start(f32[4,136,128]{2,1,0:T(8,128)S(1)} %get-tuple-element.75), channel_id=1, source_target_pairs={{0,1},{1,0},{2,3},{3,2},{4,5},{5,4},{6,7},{7,6},{8,9},{9,8},{10,11... | collective-permute-start | bytes 835592 | tf_op jit(solution)/shard_map/ppermute | solution.py:271
  221.5 1.8 kept_products.9.kept
  223.5 10.7 %all_to_all.74.refs_0_ = s32[4,72,128]{2,1,0:T(8,128)S(1)} all-to-all(s32[4,72,128]{2,1,0:T(8,128)S(1)} %encoded.11), channel_id=1, replica_groups=mesh['row_0'=4,'row_1'=2,'row_2'=4,'col_0'=4,'col_1'=2] {'col_0'}, dimensions={0} | all-to-all | bytes 294912 | tf_op jit(solution)/shard_map/all_to_all | solution.py:295
  234.2 12.2 %all_to_all.75 = f32[16,8,128]{2,1,0:T(8,128)S(1)} all-to-all(f32[16,8,128]{2,1,0:T(8,128)S(1)} %broadcast_in_dim.7), channel_id=1, replica_groups=mesh['row_0'=4,'row_1'=2,'row_2'=4,'col_0'=4,'col_1'=2] {'row_1','col_0'..., dimensions={0} | all-to-all | bytes 131072 | tf_op jit(solution)/shard_map/all_to_all | solution.py:276
  246.5 9.2 %all_to_all.76 = f32[16,8,128]{2,1,0:T(8,128)S(1)} all-to-all(f32[16,8,128]{2,1,0:T(8,128)S(1)} %broadcast_in_dim.8), channel_id=1, replica_groups=mesh['row_0'=4,'row_1'=2,'row_2'=4,'col_0'=4,'col_1'=2] {'row_0','row_2'}, dimensions={0} | all-to-all | bytes 131072 | tf_op jit(solution)/shard_map/all_to_all | solution.py:276
  255.7 0.6 log_multiply_fusion
  256.3 0.6 multiply_add_fusion
  (34 shorter events, 0.8 us)
Async XLA Ops:
  1.4 0.7 copy-start.6
  2.0 0.7 copy-start.8
  2.7 0.7 copy-start.9
  3.3 22.8 %copy-start.7 = (s32[128]{0:T(128)S(1)}, s32[128]{0:T(128)}, u32[]{:S(2)}) copy-start(s32[128]{0:T(128)} %param.11) | copy-start | bytes 1540
  3.3 30.2 %copy-start.5 = (s32[1,128]{1,0:T(1,128)S(1)}, s32[1,128]{1,0:T(1,128)}, u32[]{:S(2)}) copy-start(s32[1,128]{1,0:T(1,128)} %refs_1_.11) | copy-start | bytes 1540
  10.6 1.9 copy-start
  12.5 2.0 copy-start.2
  14.5 4.5 %collective-permute-start = (f32[4,136,128]{2,1,0:T(8,128)S(1)}, f32[4,136,128]{2,1,0:T(8,128)S(1)}, u32[]{:S(2)}, u32[]{:S(2)}) collective-permute-start(f32[4,136,128]{2,1,0:T(8,128)S(1)} %get-tuple-element.47), channel_id=1, source_target_pairs={{0,1},{1,0},{2,3},{3,2},{4,5},{5,4},{6,7},{7,6},{8,9},{9,8},{10,11... | collective-permute-start | bytes 835592 | tf_op jit(solution)/shard_map/ppermute | solution.py:271
  19.8 13.7 %all-to-all-start = ((s32[4,72,128]{2,1,0:T(8,128)}), s32[4,72,128]{2,1,0:T(8,128)S(1)}, u32[]{:S(2)}, u32[]{:S(2)}) async-start(s32[4,72,128]{2,1,0:T(8,128)} %encoded.6), calls=%async_computation | async-start | bytes 294912 | tf_op jit(solution)/shard_map/all_to_all | solution.py:295
  59.7 2.2 copy-start.3
  61.9 5.6 %copy-start.1 = (bf16[512,4096]{1,0:T(8,128)(2,1)S(1)}, bf16[512,4096]{1,0:T(8,128)(2,1)}, u32[]{:S(2)}) copy-start(bf16[512,4096]{1,0:T(8,128)(2,1)} %copy-done) | copy-start | bytes 12582916
  64.3 5.0 %collective-permute-start.1 = (f32[4,136,128]{2,1,0:T(8,128)S(1)}, f32[4,136,128]{2,1,0:T(8,128)S(1)}, u32[]{:S(2)}, u32[]{:S(2)}) collective-permute-start(f32[4,136,128]{2,1,0:T(8,128)S(1)} %get-tuple-element.51), channel_id=1, source_target_pairs={{0,1},{1,0},{2,3},{3,2},{4,5},{5,4},{6,7},{7,6},{8,9},{9,8},{10,11... | collective-permute-start | bytes 835592 | tf_op jit(solution)/shard_map/ppermute | solution.py:271
  67.5 32.0 %copy-start.4 = (bf16[512,4096]{1,0:T(8,128)(2,1)S(1)}, bf16[512,4096]{1,0:T(8,128)(2,1)}, u32[]{:S(2)}) copy-start(bf16[512,4096]{1,0:T(8,128)(2,1)} %copy-done.2) | copy-start | bytes 12582916
  102.0 5.7 %collective-permute-start.2 = (f32[4,136,128]{2,1,0:T(8,128)S(1)}, f32[4,136,128]{2,1,0:T(8,128)S(1)}, u32[]{:S(2)}, u32[]{:S(2)}) collective-permute-start(f32[4,136,128]{2,1,0:T(8,128)S(1)} %get-tuple-element.57), channel_id=1, source_target_pairs={{0,1},{1,0},{2,3},{3,2},{4,5},{5,4},{6,7},{7,6},{8,9},{9,8},{10,11... | collective-permute-start | bytes 835592 | tf_op jit(solution)/shard_map/ppermute | solution.py:271
  140.6 5.6 %collective-permute-start.3 = (f32[4,136,128]{2,1,0:T(8,128)S(1)}, f32[4,136,128]{2,1,0:T(8,128)S(1)}, u32[]{:S(2)}, u32[]{:S(2)}) collective-permute-start(f32[4,136,128]{2,1,0:T(8,128)S(1)} %get-tuple-element.63), channel_id=1, source_target_pairs={{0,1},{1,0},{2,3},{3,2},{4,5},{5,4},{6,7},{7,6},{8,9},{9,8},{10,11... | collective-permute-start | bytes 835592 | tf_op jit(solution)/shard_map/ppermute | solution.py:271
  179.1 5.6 %collective-permute-start.4 = (f32[4,136,128]{2,1,0:T(8,128)S(1)}, f32[4,136,128]{2,1,0:T(8,128)S(1)}, u32[]{:S(2)}, u32[]{:S(2)}) collective-permute-start(f32[4,136,128]{2,1,0:T(8,128)S(1)} %get-tuple-element.69), channel_id=1, source_target_pairs={{0,1},{1,0},{2,3},{3,2},{4,5},{5,4},{6,7},{7,6},{8,9},{9,8},{10,11... | collective-permute-start | bytes 835592 | tf_op jit(solution)/shard_map/ppermute | solution.py:271
  218.1 5.2 %collective-permute-start.5 = (f32[4,136,128]{2,1,0:T(8,128)S(1)}, f32[4,136,128]{2,1,0:T(8,128)S(1)}, u32[]{:S(2)}, u32[]{:S(2)}) collective-permute-start(f32[4,136,128]{2,1,0:T(8,128)S(1)} %get-tuple-element.75), channel_id=1, source_target_pairs={{0,1},{1,0},{2,3},{3,2},{4,5},{5,4},{6,7},{7,6},{8,9},{9,8},{10,11... | collective-permute-start | bytes 835592 | tf_op jit(solution)/shard_map/ppermute | solution.py:271

commit v3 on v2

v3 whole, which is shorter than its diff:
```python
import jax
import jax.numpy as jnp
from jax import lax
from jax.experimental import pallas as pl
from jax.experimental.pallas import tpu as pltpu
from jax.sharding import Mesh
from jax.sharding import PartitionSpec as P

TILE = 128
PANEL = 128
LEVELS = 6
KMAX = 128
DEST_TILES = 8
SRC_TILES = 32
VERTICES = 32768
EPSILON = 1e-06
ROW = ("row_0", "row_1", "row_2")
COL = ("col_0", "col_1")
ROW_COL = ROW + COL
SPLIT = (4, 2, 4, 4, 2)
HALF = TILE // 2
EXTRA = 8
ROWS = TILE + EXTRA
CODED = HALF + EXTRA
AWAY = DEST_TILES // 2 * TILE
TOP = 65535.0
ORDER = (1, 3, 2)
FETCH = 16
VMEM = pl.BlockSpec(memory_space=pltpu.VMEM)
WIDE = pltpu.CompilerParams(vmem_limit_bytes=16 * 1024 * 1024)
LIMIT = pltpu.CompilerParams(vmem_limit_bytes=4 * 1024 * 1024)


def f32(x):
    return x.astype(jnp.float32)


def multiply(dense, held, extra, out):
    product = jnp.dot(dense[...], held[...], preferred_element_type=jnp.float32)
    for k in range(4):
        out[k, 0:TILE, :] = product[k * TILE : (k + 1) * TILE]
        out[k, TILE:ROWS, :] = extra[...]


def first_kernel(
    count, rows_in, cols_in, ids_in, adj, away_out, kept_out, dense,
    rows, cols, ids, staged, held, extra, sems, stores,
):
    c1 = lax.axis_index("col_1")

    def fetch(n):
        part = pl.ds(n * FETCH, FETCH)
        return pltpu.make_async_copy(adj.at[part], staged.at[part], sems.at[n])

    small = [
        pltpu.make_async_copy(source, target, stores.at[i])
        for i, (source, target) in enumerate(((ids_in, ids), (rows_in, rows), (cols_in, cols)))
    ]
    for copy in small:
        copy.start()
    live = count[0, 0]
    for n in range(KMAX // FETCH):

        @pl.when(n * FETCH < live)
        def _(n=n):
            fetch(n).start()

    def clear(i, carry):
        part = pl.ds(pl.multiple_of(i * TILE, TILE), TILE)
        dense[part, :] = jnp.zeros((TILE, SRC_TILES * TILE), jnp.bfloat16)
        return carry

    lax.fori_loop(0, DEST_TILES, clear, 0)
    for copy in small:
        copy.wait()
    column = lax.axis_index("col_0") * 2 + c1
    inner = lax.broadcasted_iota(jnp.int32, (TILE, PANEL), 0)
    wanted = jnp.broadcast_to(ids[...], (TILE, PANEL)) - inner
    for t in range(SRC_TILES):
        hit = wanted == (t * DEST_TILES + column) * TILE
        held[t * TILE : (t + 1) * TILE, :] = jnp.where(hit, 1.0, 0.0).astype(jnp.bfloat16)
    extra[...] = jnp.zeros((EXTRA, PANEL), jnp.float32)

    def add(k, carry):
        d, u = rows[k], cols[k]
        block = ((d & 1) ^ c1) * (DEST_TILES // 2) + (d >> 1)
        down = pl.ds(pl.multiple_of(block * TILE, TILE), TILE)
        across = pl.ds(pl.multiple_of(u * TILE, TILE), TILE)
        dense[down, across] = dense[down, across] + staged[k]
        return carry

    for n in range(KMAX // FETCH):

        @pl.when(n * FETCH < live)
        def _(n=n):
            fetch(n).wait()
            lax.fori_loop(n * FETCH, jnp.minimum(live, (n + 1) * FETCH), add, 0)

    multiply(dense.at[pl.ds(AWAY, AWAY)], held, extra, away_out)
    multiply(dense.at[pl.ds(0, AWAY)], held, extra, kept_out)


def first_products(count, rows, cols, ids, adj):
    hbm = pl.BlockSpec(memory_space=pltpu.HBM)
    chunks = jax.ShapeDtypeStruct((4, ROWS, PANEL), jnp.float32)
    dense = jax.ShapeDtypeStruct((DEST_TILES * TILE, SRC_TILES * TILE), jnp.bfloat16)
    arrays = [pltpu.with_memory_space_constraint(x, pltpu.HBM) for x in (rows, cols, ids, adj)]
    return pl.pallas_call(
        first_kernel,
        in_specs=[pl.BlockSpec(memory_space=pltpu.SMEM)] + [hbm] * 4,
        out_specs=[VMEM] * 3,
        out_shape=[chunks, chunks, dense],
        scratch_shapes=[
            pltpu.SMEM((KMAX,), jnp.int32),
            pltpu.SMEM((KMAX,), jnp.int32),
            pltpu.VMEM((1, PANEL), jnp.int32),
            pltpu.VMEM((KMAX, TILE, TILE), jnp.bfloat16),
            pltpu.VMEM((SRC_TILES * TILE, PANEL), jnp.bfloat16),
            pltpu.VMEM((EXTRA, PANEL), jnp.float32),
            pltpu.SemaphoreType.DMA((KMAX // FETCH,)),
            pltpu.SemaphoreType.DMA((3,)),
        ],
        compiler_params=WIDE,
        name="first_products",
    )(count, *arrays)


def away_kernel(dense, sources, out, held, extra):
    parts = jnp.sum(f32(sources[:, TILE:ROWS, :]), axis=0)
    squares = (parts[0:1] + parts[1:2]) + parts[2:3]
    row = lax.broadcasted_iota(jnp.int32, (EXTRA, PANEL), 0)
    extra[...] = jnp.where(row == lax.axis_index("col_1"), jnp.broadcast_to(squares, (EXTRA, PANEL)), 0.0)
    for t in range(SRC_TILES):
        held[t * TILE : (t + 1) * TILE, :] = sources[t, 0:TILE, :]
    multiply(dense.at[pl.ds(AWAY, AWAY)], held, extra, out)


def away_products(dense, sources):
    return pl.pallas_call(
        away_kernel,
        in_specs=[VMEM, VMEM],
        out_specs=[VMEM] * 3,
        out_shape=[
            jax.ShapeDtypeStruct((4, ROWS, PANEL), jnp.float32),
            jax.ShapeDtypeStruct((SRC_TILES * TILE, PANEL), jnp.bfloat16),
            jax.ShapeDtypeStruct((EXTRA, PANEL), jnp.float32),
        ],
        compiler_params=LIMIT,
        name="away_products",
    )(dense, sources)


def kept_kernel(dense, held, extra, out):
    multiply(dense.at[pl.ds(0, AWAY)], held, extra, out)


def kept_products(dense, held, extra):
    return pl.pallas_call(
        kept_kernel,
        in_specs=[VMEM] * 3,
        out_specs=VMEM,
        out_shape=jax.ShapeDtypeStruct((4, ROWS, PANEL), jnp.float32),
        compiler_params=LIMIT,
        name="kept_products",
    )(dense, held, extra)


def as_integers(x):
    x = jnp.maximum(x, 2.0**-80)
    exponent = jnp.floor(jnp.log2(x)) - 22.0
    return jnp.floor(x * jnp.exp2(-exponent) + 0.5), exponent


def encode_kernel(kept, away, *outs):
    row = lax.broadcasted_iota(jnp.int32, (EXTRA, PANEL), 0)
    for k, coded in enumerate(outs):
        chunk = (lax.axis_index("col_0") + k) & 3
        total = kept[chunk] + away[chunk]
        sums = total[0:TILE]
        lines = list(as_integers(jnp.max(sums, axis=0, keepdims=True)))
        factor = TOP / (lines[0] * jnp.exp2(lines[1]))
        codes = jnp.minimum(jnp.floor(sums * factor + 0.5), TOP).astype(jnp.int32)
        coded[0:HALF, :] = lax.shift_left(codes[0:HALF], 16) | codes[HALF:TILE]
        lines += as_integers(total[TILE : TILE + 1])
        lines += as_integers(total[TILE + 1 : TILE + 2])
        tail = jnp.zeros((EXTRA, PANEL), jnp.float32)
        for n, line in enumerate(lines):
            tail = jnp.where(row == n, jnp.broadcast_to(line, (EXTRA, PANEL)), tail)
        coded[HALF:CODED, :] = tail.astype(jnp.int32)


def encoded(kept, away):
    return pl.pallas_call(
        encode_kernel,
        in_specs=[VMEM] * 2,
        out_specs=[VMEM] * 4,
        out_shape=[jax.ShapeDtypeStruct((CODED, PANEL), jnp.int32)] * 4,
        compiler_params=LIMIT,
        name="encoded",
    )(kept, away)


def split3(x):
    high = f32(x.astype(jnp.bfloat16))
    rest = x - high
    middle = f32(rest.astype(jnp.bfloat16))
    return high, middle, rest - middle


def decoded(chunks):
    highs = jnp.zeros((HALF, PANEL), jnp.float32)
    lows = jnp.zeros((HALF, PANEL), jnp.float32)
    shares = []
    for coded in chunks:
        tail = f32(coded[HALF:CODED, :])
        power = jnp.exp2(jnp.minimum(tail, 127.0))
        step = tail[0:1] * power[1:2] * (1.0 / TOP)
        shares.append(tail[2:3] * power[3:4] + tail[4:5] * power[5:6])
        codes = coded[0:HALF, :]
        highs = highs + f32(lax.shift_right_logical(codes, 16)) * step
        lows = lows + f32(codes & 65535) * step
    return jnp.concatenate([highs, lows], axis=0), shares


def outgoing(paths, out):
    square = jnp.sum(paths * paths, axis=0, keepdims=True)
    if out.shape[0] == 1:
        out[...] = square
        return
    row = lax.broadcasted_iota(jnp.int32, (EXTRA, PANEL), 0)
    tail = jnp.zeros((EXTRA, PANEL), jnp.float32)
    for n, line in enumerate(split3(square)):
        tail = jnp.where(row == n, jnp.broadcast_to(line, (EXTRA, PANEL)), tail)
    out[0:TILE, :] = paths.astype(jnp.bfloat16)
    out[TILE:ROWS, :] = tail.astype(jnp.bfloat16)


def start_piece(ids):
    position = jnp.int32(0)
    for axis, count in zip(ROW_COL, SPLIT):
        position = position * count + lax.axis_index(axis)
    vertex = position * TILE + lax.broadcasted_iota(jnp.int32, (TILE, PANEL), 0)
    return jnp.where(vertex == jnp.broadcast_to(ids[...], (TILE, PANEL)), 1.0, 0.0)


def first_level_kernel(own, one, three, two, depth, raw, out):
    product, _ = decoded((own, one, two, three))
    paths = jnp.where(depth[...] >= 1, product, 0.0)
    raw[...] = paths
    outgoing(paths, out)


def level_kernel(level, own, one, three, two, depth, raw_in, sums_in, raw, out, sums, scale):
    before = start_piece(sums_in) if level == 2 else sums_in[...]
    product, shares = decoded((own, one, two, three))
    mean_square = jnp.zeros((1, PANEL), jnp.float32)
    for j in range(4):
        for k, share in enumerate(shares):
            here = ((lax.axis_index("col_0") - j) & 3) == k
            mean_square = mean_square + jnp.where(here, share, 0.0)
    mean_square = mean_square / VERTICES + EPSILON
    scale[...] = mean_square
    inverse = lax.rsqrt(mean_square)
    sums[...] = before + raw_in[...] * inverse
    paths = jnp.where(depth[...] >= level, product * inverse, 0.0)
    raw[...] = paths
    outgoing(paths, out)


def finish_level(level, chunks, depth, raw, sums):
    panel = jax.ShapeDtypeStruct((TILE, PANEL), jnp.float32)
    line = jax.ShapeDtypeStruct((1, PANEL), jnp.float32)
    piece = jax.ShapeDtypeStruct((ROWS, PANEL), jnp.bfloat16)
    first = level == 1
    shapes = [panel, piece if level < LEVELS else line] + ([] if first else [panel, line])
    return pl.pallas_call(
        first_level_kernel if first else lambda *refs: level_kernel(level, *refs),
        in_specs=[VMEM] * (5 if first else 7),
        out_specs=[VMEM] * len(shapes),
        out_shape=shapes,
        compiler_params=LIMIT,
        name=f"level_{level}",
    )(*chunks, depth, *(() if first else (raw, sums)))


def from_partner(x):
    return lax.ppermute(x, "col_1", [(0, 1), (1, 0)])


def along_z(x, k):
    return lax.ppermute(x, "col_0", [(i, (i + k) % 4) for i in range(4)])


def exchanged(kept, away):
    chunks = encoded(kept, from_partner(away))
    moved = {k: along_z(chunks[k], k) for k in ORDER}
    return chunks[0], moved[1], moved[3], moved[2]


def summed_alike(x, axes):
    copies = jnp.broadcast_to(x, (lax.axis_size(axes), EXTRA, PANEL))
    return jnp.sum(lax.all_to_all(copies, axes, 0, 0, tiled=True)[:, 0], axis=0, keepdims=True)


def local(adj_tiles, tile_rows, tile_cols, tile_count, tile_depth, source_ids):
    away, kept, dense = first_products(
        tile_count, tile_rows[0, 0], tile_cols[0, 0], source_ids[None, :], adj_tiles[0, 0]
    )
    sums = source_ids[None, :]
    raw, piece, *_ = finish_level(1, exchanged(kept, away), tile_depth, None, None)
    scales = []
    for level in range(2, LEVELS + 1):
        spread = jnp.broadcast_to(piece, (SRC_TILES, ROWS, PANEL))
        sources = lax.all_to_all(spread, ROW, 0, 0, tiled=True)
        away, held, extra = away_products(dense, sources)
        chunks = exchanged(kept_products(dense, held, extra), away)
        raw, piece, sums, scale = finish_level(level, chunks, tile_depth, raw, sums)
        scales.append(scale)
    squares = piece
    total = summed_alike(summed_alike(squares, ("row_1",) + COL), ("row_0", "row_2"))
    mean_square = total / VERTICES + EPSILON
    scales.append(mean_square)
    path_sums = sums + raw * lax.rsqrt(mean_square)
    return path_sums, 0.5 * jnp.log(jnp.concatenate(scales, axis=0))


def solution(mesh):
    split = Mesh(mesh.devices.reshape(SPLIT), ROW_COL)
    in_specs = (
        P(ROW, COL, None, None, None),
        P(ROW, COL, None),
        P(ROW, COL, None),
        P(ROW, COL),
        P(ROW_COL, None),
        P(),
    )
    out_specs = (P(ROW_COL, None), P())
    return jax.shard_map(local, mesh=split, in_specs=in_specs, out_specs=out_specs, check_vma=False)
```

time: 257 us -> 236 us (0.918)
  blocking collectives: 177 us -> 128 us
  starting transfers between devices: 27.6 us -> 71.2 us
  Pallas kernels: 32.9 us -> 19.1 us
  local copies, waits for them, and re-layouts: 8.16 us -> 0.78 us
  waiting for transfers between devices: 8.49 us -> 14.2 us
    all_to_all x10 -> x5, blocking collectives: 155 us -> 103 us  [local(): sources = lax.all_to_all(spread, ROW, 0, 0, tiled=True)]
    ppermute x0 -> x18, starting transfers between devices: none -> 51.7 us  [along_z(): return lax.ppermute(x, 'col_0', [(i, (i + k) % 4) for i in range(4)])]
    pallas_call x23, Pallas kernels: 32.9 us -> 19.1 us  [the longest x5 6.65 us: away_products(): pl.pallas_call(away_kernel, in_specs=[VMEM, VMEM], out_specs=[VMEM] * 3,...]
    ppermute x0 -> x18, waiting for transfers between devices: none -> 13 us  [along_z(): return lax.ppermute(x, 'col_0', [(i, (i + k) % 4) for i in range(4)])]
    unnamed x20 -> x4, local copies, waits for them, and re-layouts: 8.11 us -> 0.01 us
    all_to_all x1 -> x0, waiting for transfers between devices: 7.3 us -> none  [local(): coded = lax.all_to_all(coded, 'col_0', 0, 0, tiled=True)]
    all_to_all x1 -> x0, starting transfers between devices: 6.27 us -> none  [local(): coded = lax.all_to_all(coded, 'col_0', 0, 0, tiled=True)]
    all_to_all x2, blocking collectives: 21.4 us -> 25.2 us  [summed_alike(): lax.all_to_all(copies, axes, 0, 0, tiled=True)[:, 0]]
  transfers between devices with their start and end apart: 7 -> 24, of which waited for: 2 -> 7; matrix products, arithmetic and copies ran while one was open for 0% -> 0% of each run, Pallas kernels for 3% -> 3%
where the time goes in v3:
time: 236 us
  blocking collectives  128 us (54%)
  starting transfers between devices  71.2 us (30%)
  Pallas kernels  19.1 us (8%)
  waiting for transfers between devices  14.2 us (6%)
    all_to_all x5, blocking collectives, local(): sources = lax.all_to_all(spread, ROW, 0, 0, tiled=True)  103 us
    ppermute x18, starting transfers between devices, along_z(): return lax.ppermute(x, 'col_0', [(i, (i + k) % 4) for i in range(4)])  51.7 us
    all_to_all x2, blocking collectives, summed_alike(): lax.all_to_all(copies, axes, 0, 0, tiled=True)[:, 0]  25.2 us
    ppermute x6, starting transfers between devices, from_partner(): return lax.ppermute(x, 'col_1', [(0, 1), (1, 0)])  19.5 us
    ppermute x18, waiting for transfers between devices, along_z(): return lax.ppermute(x, 'col_0', [(i, (i + k) % 4) for i in range(4)])  13 us
    pallas_call x5, Pallas kernels, away_products(): pl.pallas_call(away_kernel, in_specs=[VMEM, VMEM], out_specs=[VMEM] * 3,...  6.65 us
    pallas_call x5, Pallas kernels, kept_products(): pl.pallas_call(kept_kernel, in_specs=[VMEM] * 3, out_specs=VMEM, out_shap...  6.22 us
    pallas_call x1, Pallas kernels, first_products(): pl.pallas_call(first_kernel, in_specs=[pl.BlockSpec(memory_space=pltpu.SM...  4.86 us
  transfers between devices with their start and end apart: 24, of which 7 were waited for; matrix products, arithmetic and copies ran while one was open for 0% of the time, Pallas kernels for 3%

profile of v3, /device:TPU:1, one launch (start us, length us, event | category | flops | bytes accessed | tf_op | source)
XLA Modules:
  0.0 235.8 jit_solution(2788169246418133659)
XLA Ops:
  1.3 4.9 %first_products.1 = (f32[4,136,128]{2,1,0:T(8,128)S(1)}, f32[4,136,128]{2,1,0:T(8,128)S(1)}, bf16[1024,4096]{1,0:T(8,128)(2,1)S(1)}) custom-call(s32[1,1]{1,0:T(1,128)S(6)} %copy.10.count, s32[128]{0:T(128)} %bitcast.15, s32[128]{0:T(128)} %bitcast.16, s32[1,128]{1,0:T(1,128)} %bitcast.9, bf16[128,128,128]{2,1,0:T(8,128)(2,1)} %bitcast.12), custom_call_target="tpu_custom_call" | custom-call | tf_op jit(solution)/shard_map/first_products/pallas_call | solution.py:108
  6.2 3.4 %collective-permute-start = (f32[4,136,128]{2,1,0:T(8,128)S(1)}, f32[4,136,128]{2,1,0:T(8,128)S(1)}, u32[]{:S(2)}, u32[]{:S(2)}) collective-permute-start(f32[4,136,128]{2,1,0:T(8,128)S(1)} %get-tuple-element.68), channel_id=1, source_target_pairs={{0,1},{1,0},{2,3},{3,2},{4,5},{5,4},{6,7},{7,6},{8,9},{9,8},{10,11... | collective-permute-start | bytes 835592 | tf_op jit(solution)/shard_map/ppermute | solution.py:287
  10.8 1.4 collective-permute-start.1
  12.2 4.3 %collective-permute-start.2 = (s32[72,128]{1,0:T(8,128)S(1)}, s32[72,128]{1,0:T(8,128)S(1)}, u32[]{:S(2)}, u32[]{:S(2)}) collective-permute-start(s32[72,128]{1,0:T(8,128)S(1)} %get-tuple-element.71), channel_id=1, source_target_pairs={{0,6},{2,0},{4,2},{6,4},{1,7},{3,1},{5,3},{7,5},{8,14},{10,8},{12,... | collective-permute-start | bytes 110600 | tf_op jit(solution)/shard_map/ppermute | solution.py:291
  16.5 3.2 %collective-permute-start.3 = (s32[72,128]{1,0:T(8,128)S(1)}, s32[72,128]{1,0:T(8,128)S(1)}, u32[]{:S(2)}, u32[]{:S(2)}) collective-permute-start(s32[72,128]{1,0:T(8,128)S(1)} %get-tuple-element.72), channel_id=1, source_target_pairs={{0,4},{2,6},{4,0},{6,2},{1,5},{3,7},{5,1},{7,3},{8,12},{10,14},{12... | collective-permute-start | bytes 110600 | tf_op jit(solution)/shard_map/ppermute | solution.py:291
  19.7 3.5 %collective-permute-done.3.two = s32[72,128]{1,0:T(8,128)S(1)} collective-permute-done((s32[72,128]{1,0:T(8,128)S(1)}, s32[72,128]{1,0:T(8,128)S(1)}, u32[]{:S(2)}, u32[]{:S(2)}) %collective-permute-start.3) | collective-permute-done | bytes 36896 | tf_op jit(solution)/shard_map/ppermute | solution.py:291
  23.4 23.8 %all_to_all.35.sources = bf16[32,136,128]{2,1,0:T(8,128)(2,1)S(1)} all-to-all(bf16[32,136,128]{2,1,0:T(8,128)(2,1)S(1)} %broadcast_in_dim.32), channel_id=1, replica_groups=mesh['row_0'=4,'row_1'=2,'row_2'=4,'col_0'=4,'col_1'=2] {'row_0','row_1'..., dimensions={0} | all-to-all | bytes 2228224 | tf_op jit(solution)/shard_map/all_to_all | solution.py:314
  47.2 1.3 away_products.5
  48.5 3.2 %collective-permute-start.4 = (f32[4,136,128]{2,1,0:T(8,128)S(1)}, f32[4,136,128]{2,1,0:T(8,128)S(1)}, u32[]{:S(2)}, u32[]{:S(2)}) collective-permute-start(f32[4,136,128]{2,1,0:T(8,128)S(1)} %get-tuple-element.76), channel_id=1, source_target_pairs={{0,1},{1,0},{2,3},{3,2},{4,5},{5,4},{6,7},{7,6},{8,9},{9,8},{10,11... | collective-permute-start | bytes 835592 | tf_op jit(solution)/shard_map/ppermute | solution.py:287
  51.8 1.2 kept_products.5.kept
  53.2 1.3 collective-permute-start.5
  54.5 2.3 collective-permute-start.6
  56.8 4.5 %collective-permute-start.7 = (s32[72,128]{1,0:T(8,128)S(1)}, s32[72,128]{1,0:T(8,128)S(1)}, u32[]{:S(2)}, u32[]{:S(2)}) collective-permute-start(s32[72,128]{1,0:T(8,128)S(1)} %get-tuple-element.80), channel_id=1, source_target_pairs={{0,4},{2,6},{4,0},{6,2},{1,5},{3,7},{5,1},{7,3},{8,12},{10,14},{12... | collective-permute-start | bytes 110600 | tf_op jit(solution)/shard_map/ppermute | solution.py:291
  61.4 2.2 collective-permute-done.7.refs_3_
  63.8 19.8 %all_to_all.36.sources = bf16[32,136,128]{2,1,0:T(8,128)(2,1)S(1)} all-to-all(bf16[32,136,128]{2,1,0:T(8,128)(2,1)S(1)} %broadcast_in_dim.33), channel_id=1, replica_groups=mesh['row_0'=4,'row_1'=2,'row_2'=4,'col_0'=4,'col_1'=2] {'row_0','row_1'..., dimensions={0} | all-to-all | bytes 2228224 | tf_op jit(solution)/shard_map/all_to_all | solution.py:314
  83.6 1.3 away_products.6
  84.9 3.4 %collective-permute-start.8 = (f32[4,136,128]{2,1,0:T(8,128)S(1)}, f32[4,136,128]{2,1,0:T(8,128)S(1)}, u32[]{:S(2)}, u32[]{:S(2)}) collective-permute-start(f32[4,136,128]{2,1,0:T(8,128)S(1)} %get-tuple-element.85), channel_id=1, source_target_pairs={{0,1},{1,0},{2,3},{3,2},{4,5},{5,4},{6,7},{7,6},{8,9},{9,8},{10,11... | collective-permute-start | bytes 835592 | tf_op jit(solution)/shard_map/ppermute | solution.py:287
  88.3 1.2 kept_products.6.kept
  89.7 1.4 collective-permute-start.9
  91.1 2.2 collective-permute-start.10
  93.3 4.7 %collective-permute-start.11 = (s32[72,128]{1,0:T(8,128)S(1)}, s32[72,128]{1,0:T(8,128)S(1)}, u32[]{:S(2)}, u32[]{:S(2)}) collective-permute-start(s32[72,128]{1,0:T(8,128)S(1)} %get-tuple-element.89), channel_id=1, source_target_pairs={{0,4},{2,6},{4,0},{6,2},{1,5},{3,7},{5,1},{7,3},{8,12},{10,14},{12... | collective-permute-start | bytes 110600 | tf_op jit(solution)/shard_map/ppermute | solution.py:291
  98.0 2.0 collective-permute-done.11.refs_3_
  100.3 19.7 %all_to_all.37.sources = bf16[32,136,128]{2,1,0:T(8,128)(2,1)S(1)} all-to-all(bf16[32,136,128]{2,1,0:T(8,128)(2,1)S(1)} %broadcast_in_dim.34), channel_id=1, replica_groups=mesh['row_0'=4,'row_1'=2,'row_2'=4,'col_0'=4,'col_1'=2] {'row_0','row_1'..., dimensions={0} | all-to-all | bytes 2228224 | tf_op jit(solution)/shard_map/all_to_all | solution.py:314
  120.0 1.3 away_products.7
  121.3 3.1 %collective-permute-start.12 = (f32[4,136,128]{2,1,0:T(8,128)S(1)}, f32[4,136,128]{2,1,0:T(8,128)S(1)}, u32[]{:S(2)}, u32[]{:S(2)}) collective-permute-start(f32[4,136,128]{2,1,0:T(8,128)S(1)} %get-tuple-element.95), channel_id=1, source_target_pairs={{0,1},{1,0},{2,3},{3,2},{4,5},{5,4},{6,7},{7,6},{8,9},{9,8},{10,11... | collective-permute-start | bytes 835592 | tf_op jit(solution)/shard_map/ppermute | solution.py:287
  124.4 1.2 kept_products.7.kept
  125.9 1.5 collective-permute-start.13
  127.4 2.1 collective-permute-start.14
  129.5 4.9 %collective-permute-start.15 = (s32[72,128]{1,0:T(8,128)S(1)}, s32[72,128]{1,0:T(8,128)S(1)}, u32[]{:S(2)}, u32[]{:S(2)}) collective-permute-start(s32[72,128]{1,0:T(8,128)S(1)} %get-tuple-element.99), channel_id=1, source_target_pairs={{0,4},{2,6},{4,0},{6,2},{1,5},{3,7},{5,1},{7,3},{8,12},{10,14},{12... | collective-permute-start | bytes 110600 | tf_op jit(solution)/shard_map/ppermute | solution.py:291
  134.4 1.8 collective-permute-done.15.refs_3_
  136.5 19.7 %all_to_all.38.sources = bf16[32,136,128]{2,1,0:T(8,128)(2,1)S(1)} all-to-all(bf16[32,136,128]{2,1,0:T(8,128)(2,1)S(1)} %broadcast_in_dim.35), channel_id=1, replica_groups=mesh['row_0'=4,'row_1'=2,'row_2'=4,'col_0'=4,'col_1'=2] {'row_0','row_1'..., dimensions={0} | all-to-all | bytes 2228224 | tf_op jit(solution)/shard_map/all_to_all | solution.py:314
  156.2 1.3 away_products.8
  157.5 3.2 %collective-permute-start.16 = (f32[4,136,128]{2,1,0:T(8,128)S(1)}, f32[4,136,128]{2,1,0:T(8,128)S(1)}, u32[]{:S(2)}, u32[]{:S(2)}) collective-permute-start(f32[4,136,128]{2,1,0:T(8,128)S(1)} %get-tuple-element.105), channel_id=1, source_target_pairs={{0,1},{1,0},{2,3},{3,2},{4,5},{5,4},{6,7},{7,6},{8,9},{9,8},{10,11... | collective-permute-start | bytes 835592 | tf_op jit(solution)/shard_map/ppermute | solution.py:287
  160.7 1.2 kept_products.8.kept
  162.1 2.0 collective-permute-start.17
  164.1 1.9 collective-permute-start.18
  165.9 5.1 %collective-permute-start.19 = (s32[72,128]{1,0:T(8,128)S(1)}, s32[72,128]{1,0:T(8,128)S(1)}, u32[]{:S(2)}, u32[]{:S(2)}) collective-permute-start(s32[72,128]{1,0:T(8,128)S(1)} %get-tuple-element.109), channel_id=1, source_target_pairs={{0,4},{2,6},{4,0},{6,2},{1,5},{3,7},{5,1},{7,3},{8,12},{10,14},{12... | collective-permute-start | bytes 110600 | tf_op jit(solution)/shard_map/ppermute | solution.py:291
  171.0 1.7 collective-permute-done.19.refs_3_
  173.0 19.7 %all_to_all.39.sources = bf16[32,136,128]{2,1,0:T(8,128)(2,1)S(1)} all-to-all(bf16[32,136,128]{2,1,0:T(8,128)(2,1)S(1)} %broadcast_in_dim.36), channel_id=1, replica_groups=mesh['row_0'=4,'row_1'=2,'row_2'=4,'col_0'=4,'col_1'=2] {'row_0','row_1'..., dimensions={0} | all-to-all | bytes 2228224 | tf_op jit(solution)/shard_map/all_to_all | solution.py:314
  192.7 1.3 away_products.9
  194.0 3.3 %collective-permute-start.20 = (f32[4,136,128]{2,1,0:T(8,128)S(1)}, f32[4,136,128]{2,1,0:T(8,128)S(1)}, u32[]{:S(2)}, u32[]{:S(2)}) collective-permute-start(f32[4,136,128]{2,1,0:T(8,128)S(1)} %get-tuple-element.115), channel_id=1, source_target_pairs={{0,1},{1,0},{2,3},{3,2},{4,5},{5,4},{6,7},{7,6},{8,9},{9,8},{10,11... | collective-permute-start | bytes 835592 | tf_op jit(solution)/shard_map/ppermute | solution.py:287
  197.3 1.2 kept_products.9.kept
  198.7 2.2 collective-permute-start.21
  200.8 1.5 collective-permute-start.22
  202.3 5.1 %collective-permute-start.23 = (s32[72,128]{1,0:T(8,128)S(1)}, s32[72,128]{1,0:T(8,128)S(1)}, u32[]{:S(2)}, u32[]{:S(2)}) collective-permute-start(s32[72,128]{1,0:T(8,128)S(1)} %get-tuple-element.119), channel_id=1, source_target_pairs={{0,4},{2,6},{4,0},{6,2},{1,5},{3,7},{5,1},{7,3},{8,12},{10,14},{12... | collective-permute-start | bytes 110600 | tf_op jit(solution)/shard_map/ppermute | solution.py:291
  207.4 1.7 collective-permute-done.23.refs_3_
  209.3 16.1 %all_to_all.40 = f32[16,8,128]{2,1,0:T(8,128)S(1)} all-to-all(f32[16,8,128]{2,1,0:T(8,128)S(1)} %broadcast_in_dim.37), channel_id=1, replica_groups=mesh['row_0'=4,'row_1'=2,'row_2'=4,'col_0'=4,'col_1'=2] {'row_1','col_0'..., dimensions={0} | all-to-all | bytes 131072 | tf_op jit(solution)/shard_map/all_to_all | solution.py:302
  225.3 9.2 %all_to_all.41 = f32[16,8,128]{2,1,0:T(8,128)S(1)} all-to-all(f32[16,8,128]{2,1,0:T(8,128)S(1)} %broadcast_in_dim.38), channel_id=1, replica_groups=mesh['row_0'=4,'row_1'=2,'row_2'=4,'col_0'=4,'col_1'=2] {'row_0','row_2'}, dimensions={0} | all-to-all | bytes 131072 | tf_op jit(solution)/shard_map/all_to_all | solution.py:302
  (49 shorter events, 4.6 us)
Async XLA Ops:
  1.3 21.9 %copy-start = (s32[1,128]{1,0:T(1,128)S(1)}, s32[1,128]{1,0:T(1,128)}, u32[]{:S(2)}) copy-start(s32[1,128]{1,0:T(1,128)} %refs_4_.9) | copy-start | bytes 1540
  6.2 4.6 %collective-permute-start = (f32[4,136,128]{2,1,0:T(8,128)S(1)}, f32[4,136,128]{2,1,0:T(8,128)S(1)}, u32[]{:S(2)}, u32[]{:S(2)}) collective-permute-start(f32[4,136,128]{2,1,0:T(8,128)S(1)} %get-tuple-element.68), channel_id=1, source_target_pairs={{0,1},{1,0},{2,3},{3,2},{4,5},{5,4},{6,7},{7,6},{8,9},{9,8},{10,11... | collective-permute-start | bytes 835592 | tf_op jit(solution)/shard_map/ppermute | solution.py:287
  10.8 8.9 %collective-permute-start.1 = (s32[72,128]{1,0:T(8,128)S(1)}, s32[72,128]{1,0:T(8,128)S(1)}, u32[]{:S(2)}, u32[]{:S(2)}) collective-permute-start(s32[72,128]{1,0:T(8,128)S(1)} %get-tuple-element.70), channel_id=1, source_target_pairs={{0,2},{2,4},{4,6},{6,0},{1,3},{3,5},{5,7},{7,1},{8,10},{10,12},{12... | collective-permute-start | bytes 110600 | tf_op jit(solution)/shard_map/ppermute | solution.py:291
  12.2 7.5 %collective-permute-start.2 = (s32[72,128]{1,0:T(8,128)S(1)}, s32[72,128]{1,0:T(8,128)S(1)}, u32[]{:S(2)}, u32[]{:S(2)}) collective-permute-start(s32[72,128]{1,0:T(8,128)S(1)} %get-tuple-element.71), channel_id=1, source_target_pairs={{0,6},{2,0},{4,2},{6,4},{1,7},{3,1},{5,3},{7,5},{8,14},{10,8},{12,... | collective-permute-start | bytes 110600 | tf_op jit(solution)/shard_map/ppermute | solution.py:291
  16.5 6.7 %collective-permute-start.3 = (s32[72,128]{1,0:T(8,128)S(1)}, s32[72,128]{1,0:T(8,128)S(1)}, u32[]{:S(2)}, u32[]{:S(2)}) collective-permute-start(s32[72,128]{1,0:T(8,128)S(1)} %get-tuple-element.72), channel_id=1, source_target_pairs={{0,4},{2,6},{4,0},{6,2},{1,5},{3,7},{5,1},{7,3},{8,12},{10,14},{12... | collective-permute-start | bytes 110600 | tf_op jit(solution)/shard_map/ppermute | solution.py:291
  48.5 4.5 %collective-permute-start.4 = (f32[4,136,128]{2,1,0:T(8,128)S(1)}, f32[4,136,128]{2,1,0:T(8,128)S(1)}, u32[]{:S(2)}, u32[]{:S(2)}) collective-permute-start(f32[4,136,128]{2,1,0:T(8,128)S(1)} %get-tuple-element.76), channel_id=1, source_target_pairs={{0,1},{1,0},{2,3},{3,2},{4,5},{5,4},{6,7},{7,6},{8,9},{9,8},{10,11... | collective-permute-start | bytes 835592 | tf_op jit(solution)/shard_map/ppermute | solution.py:287
  51.8 11.8 %copy-start.1 = (s32[128]{0:T(128)S(1)}, s32[128]{0:T(128)}, u32[]{:S(2)}) copy-start(s32[128]{0:T(128)} %param.11) | copy-start | bytes 1540
  53.2 8.2 %collective-permute-start.5 = (s32[72,128]{1,0:T(8,128)S(1)}, s32[72,128]{1,0:T(8,128)S(1)}, u32[]{:S(2)}, u32[]{:S(2)}) collective-permute-start(s32[72,128]{1,0:T(8,128)S(1)} %get-tuple-element.78), channel_id=1, source_target_pairs={{0,2},{2,4},{4,6},{6,0},{1,3},{3,5},{5,7},{7,1},{8,10},{10,12},{12... | collective-permute-start | bytes 110600 | tf_op jit(solution)/shard_map/ppermute | solution.py:291
  54.5 6.9 %collective-permute-start.6 = (s32[72,128]{1,0:T(8,128)S(1)}, s32[72,128]{1,0:T(8,128)S(1)}, u32[]{:S(2)}, u32[]{:S(2)}) collective-permute-start(s32[72,128]{1,0:T(8,128)S(1)} %get-tuple-element.79), channel_id=1, source_target_pairs={{0,6},{2,0},{4,2},{6,4},{1,7},{3,1},{5,3},{7,5},{8,14},{10,8},{12,... | collective-permute-start | bytes 110600 | tf_op jit(solution)/shard_map/ppermute | solution.py:291
  56.8 6.7 %collective-permute-start.7 = (s32[72,128]{1,0:T(8,128)S(1)}, s32[72,128]{1,0:T(8,128)S(1)}, u32[]{:S(2)}, u32[]{:S(2)}) collective-permute-start(s32[72,128]{1,0:T(8,128)S(1)} %get-tuple-element.80), channel_id=1, source_target_pairs={{0,4},{2,6},{4,0},{6,2},{1,5},{3,7},{5,1},{7,3},{8,12},{10,14},{12... | collective-permute-start | bytes 110600 | tf_op jit(solution)/shard_map/ppermute | solution.py:291
  84.9 4.6 %collective-permute-start.8 = (f32[4,136,128]{2,1,0:T(8,128)S(1)}, f32[4,136,128]{2,1,0:T(8,128)S(1)}, u32[]{:S(2)}, u32[]{:S(2)}) collective-permute-start(f32[4,136,128]{2,1,0:T(8,128)S(1)} %get-tuple-element.85), channel_id=1, source_target_pairs={{0,1},{1,0},{2,3},{3,2},{4,5},{5,4},{6,7},{7,6},{8,9},{9,8},{10,11... | collective-permute-start | bytes 835592 | tf_op jit(solution)/shard_map/ppermute | solution.py:287
  89.7 8.3 %collective-permute-start.9 = (s32[72,128]{1,0:T(8,128)S(1)}, s32[72,128]{1,0:T(8,128)S(1)}, u32[]{:S(2)}, u32[]{:S(2)}) collective-permute-start(s32[72,128]{1,0:T(8,128)S(1)} %get-tuple-element.87), channel_id=1, source_target_pairs={{0,2},{2,4},{4,6},{6,0},{1,3},{3,5},{5,7},{7,1},{8,10},{10,12},{12... | collective-permute-start | bytes 110600 | tf_op jit(solution)/shard_map/ppermute | solution.py:291
  91.1 6.9 %collective-permute-start.10 = (s32[72,128]{1,0:T(8,128)S(1)}, s32[72,128]{1,0:T(8,128)S(1)}, u32[]{:S(2)}, u32[]{:S(2)}) collective-permute-start(s32[72,128]{1,0:T(8,128)S(1)} %get-tuple-element.88), channel_id=1, source_target_pairs={{0,6},{2,0},{4,2},{6,4},{1,7},{3,1},{5,3},{7,5},{8,14},{10,8},{12,... | collective-permute-start | bytes 110600 | tf_op jit(solution)/shard_map/ppermute | solution.py:291
  93.3 6.7 %collective-permute-start.11 = (s32[72,128]{1,0:T(8,128)S(1)}, s32[72,128]{1,0:T(8,128)S(1)}, u32[]{:S(2)}, u32[]{:S(2)}) collective-permute-start(s32[72,128]{1,0:T(8,128)S(1)} %get-tuple-element.89), channel_id=1, source_target_pairs={{0,4},{2,6},{4,0},{6,2},{1,5},{3,7},{5,1},{7,3},{8,12},{10,14},{12... | collective-permute-start | bytes 110600 | tf_op jit(solution)/shard_map/ppermute | solution.py:291
  121.3 4.4 %collective-permute-start.12 = (f32[4,136,128]{2,1,0:T(8,128)S(1)}, f32[4,136,128]{2,1,0:T(8,128)S(1)}, u32[]{:S(2)}, u32[]{:S(2)}) collective-permute-start(f32[4,136,128]{2,1,0:T(8,128)S(1)} %get-tuple-element.95), channel_id=1, source_target_pairs={{0,1},{1,0},{2,3},{3,2},{4,5},{5,4},{6,7},{7,6},{8,9},{9,8},{10,11... | collective-permute-start | bytes 835592 | tf_op jit(solution)/shard_map/ppermute | solution.py:287
  125.9 8.6 %collective-permute-start.13 = (s32[72,128]{1,0:T(8,128)S(1)}, s32[72,128]{1,0:T(8,128)S(1)}, u32[]{:S(2)}, u32[]{:S(2)}) collective-permute-start(s32[72,128]{1,0:T(8,128)S(1)} %get-tuple-element.97), channel_id=1, source_target_pairs={{0,2},{2,4},{4,6},{6,0},{1,3},{3,5},{5,7},{7,1},{8,10},{10,12},{12... | collective-permute-start | bytes 110600 | tf_op jit(solution)/shard_map/ppermute | solution.py:291
  127.4 7.1 %collective-permute-start.14 = (s32[72,128]{1,0:T(8,128)S(1)}, s32[72,128]{1,0:T(8,128)S(1)}, u32[]{:S(2)}, u32[]{:S(2)}) collective-permute-start(s32[72,128]{1,0:T(8,128)S(1)} %get-tuple-element.98), channel_id=1, source_target_pairs={{0,6},{2,0},{4,2},{6,4},{1,7},{3,1},{5,3},{7,5},{8,14},{10,8},{12,... | collective-permute-start | bytes 110600 | tf_op jit(solution)/shard_map/ppermute | solution.py:291
  129.5 6.7 %collective-permute-start.15 = (s32[72,128]{1,0:T(8,128)S(1)}, s32[72,128]{1,0:T(8,128)S(1)}, u32[]{:S(2)}, u32[]{:S(2)}) collective-permute-start(s32[72,128]{1,0:T(8,128)S(1)} %get-tuple-element.99), channel_id=1, source_target_pairs={{0,4},{2,6},{4,0},{6,2},{1,5},{3,7},{5,1},{7,3},{8,12},{10,14},{12... | collective-permute-start | bytes 110600 | tf_op jit(solution)/shard_map/ppermute | solution.py:291
  157.5 4.4 %collective-permute-start.16 = (f32[4,136,128]{2,1,0:T(8,128)S(1)}, f32[4,136,128]{2,1,0:T(8,128)S(1)}, u32[]{:S(2)}, u32[]{:S(2)}) collective-permute-start(f32[4,136,128]{2,1,0:T(8,128)S(1)} %get-tuple-element.105), channel_id=1, source_target_pairs={{0,1},{1,0},{2,3},{3,2},{4,5},{5,4},{6,7},{7,6},{8,9},{9,8},{10,11... | collective-permute-start | bytes 835592 | tf_op jit(solution)/shard_map/ppermute | solution.py:287
  162.1 9.0 %collective-permute-start.17 = (s32[72,128]{1,0:T(8,128)S(1)}, s32[72,128]{1,0:T(8,128)S(1)}, u32[]{:S(2)}, u32[]{:S(2)}) collective-permute-start(s32[72,128]{1,0:T(8,128)S(1)} %get-tuple-element.107), channel_id=1, source_target_pairs={{0,2},{2,4},{4,6},{6,0},{1,3},{3,5},{5,7},{7,1},{8,10},{10,12},{12... | collective-permute-start | bytes 110600 | tf_op jit(solution)/shard_map/ppermute | solution.py:291
  164.1 7.0 %collective-permute-start.18 = (s32[72,128]{1,0:T(8,128)S(1)}, s32[72,128]{1,0:T(8,128)S(1)}, u32[]{:S(2)}, u32[]{:S(2)}) collective-permute-start(s32[72,128]{1,0:T(8,128)S(1)} %get-tuple-element.108), channel_id=1, source_target_pairs={{0,6},{2,0},{4,2},{6,4},{1,7},{3,1},{5,3},{7,5},{8,14},{10,8},{12,... | collective-permute-start | bytes 110600 | tf_op jit(solution)/shard_map/ppermute | solution.py:291
  165.9 6.8 %collective-permute-start.19 = (s32[72,128]{1,0:T(8,128)S(1)}, s32[72,128]{1,0:T(8,128)S(1)}, u32[]{:S(2)}, u32[]{:S(2)}) collective-permute-start(s32[72,128]{1,0:T(8,128)S(1)} %get-tuple-element.109), channel_id=1, source_target_pairs={{0,4},{2,6},{4,0},{6,2},{1,5},{3,7},{5,1},{7,3},{8,12},{10,14},{12... | collective-permute-start | bytes 110600 | tf_op jit(solution)/shard_map/ppermute | solution.py:291
  194.0 4.5 %collective-permute-start.20 = (f32[4,136,128]{2,1,0:T(8,128)S(1)}, f32[4,136,128]{2,1,0:T(8,128)S(1)}, u32[]{:S(2)}, u32[]{:S(2)}) collective-permute-start(f32[4,136,128]{2,1,0:T(8,128)S(1)} %get-tuple-element.115), channel_id=1, source_target_pairs={{0,1},{1,0},{2,3},{3,2},{4,5},{5,4},{6,7},{7,6},{8,9},{9,8},{10,11... | collective-permute-start | bytes 835592 | tf_op jit(solution)/shard_map/ppermute | solution.py:287
  198.7 8.7 %collective-permute-start.21 = (s32[72,128]{1,0:T(8,128)S(1)}, s32[72,128]{1,0:T(8,128)S(1)}, u32[]{:S(2)}, u32[]{:S(2)}) collective-permute-start(s32[72,128]{1,0:T(8,128)S(1)} %get-tuple-element.117), channel_id=1, source_target_pairs={{0,2},{2,4},{4,6},{6,0},{1,3},{3,5},{5,7},{7,1},{8,10},{10,12},{12... | collective-permute-start | bytes 110600 | tf_op jit(solution)/shard_map/ppermute | solution.py:291
  200.8 6.6 %collective-permute-start.22 = (s32[72,128]{1,0:T(8,128)S(1)}, s32[72,128]{1,0:T(8,128)S(1)}, u32[]{:S(2)}, u32[]{:S(2)}) collective-permute-start(s32[72,128]{1,0:T(8,128)S(1)} %get-tuple-element.118), channel_id=1, source_target_pairs={{0,6},{2,0},{4,2},{6,4},{1,7},{3,1},{5,3},{7,5},{8,14},{10,8},{12,... | collective-permute-start | bytes 110600 | tf_op jit(solution)/shard_map/ppermute | solution.py:291
  202.3 6.8 %collective-permute-start.23 = (s32[72,128]{1,0:T(8,128)S(1)}, s32[72,128]{1,0:T(8,128)S(1)}, u32[]{:S(2)}, u32[]{:S(2)}) collective-permute-start(s32[72,128]{1,0:T(8,128)S(1)} %get-tuple-element.119), channel_id=1, source_target_pairs={{0,4},{2,6},{4,0},{6,2},{1,5},{3,7},{5,1},{7,3},{8,12},{10,14},{12... | collective-permute-start | bytes 110600 | tf_op jit(solution)/shard_map/ppermute | solution.py:291

commit v4 on v3

--- a/solution.py
+++ b/solution.py
@@ -24,8 +24,9 @@
 CODED = HALF + EXTRA
 AWAY = DEST_TILES // 2 * TILE
 TOP = 65535.0
-ORDER = (1, 3, 2)
+ORDER = (2, 1, 3)
 FETCH = 16
+TOGETHER = 8
 VMEM = pl.BlockSpec(memory_space=pltpu.VMEM)
 WIDE = pltpu.CompilerParams(vmem_limit_bytes=16 * 1024 * 1024)
 LIMIT = pltpu.CompilerParams(vmem_limit_bytes=4 * 1024 * 1024)
@@ -81,21 +82,32 @@
         held[t * TILE : (t + 1) * TILE, :] = jnp.where(hit, 1.0, 0.0).astype(jnp.bfloat16)
     extra[...] = jnp.zeros((EXTRA, PANEL), jnp.float32)
 
-    def add(k, carry):
+    def add(k):
         d, u = rows[k], cols[k]
         block = ((d & 1) ^ c1) * (DEST_TILES // 2) + (d >> 1)
         down = pl.ds(pl.multiple_of(block * TILE, TILE), TILE)
         across = pl.ds(pl.multiple_of(u * TILE, TILE), TILE)
         dense[down, across] = dense[down, across] + staged[k]
+
+    def add_some(g, carry):
+        for i in range(TOGETHER):
+            add(g * TOGETHER + i)
         return carry
 
+    def add_one(k, carry):
+        add(k)
+        return carry
+
+    whole = live // TOGETHER
     for n in range(KMAX // FETCH):
 
         @pl.when(n * FETCH < live)
         def _(n=n):
             fetch(n).wait()
-            lax.fori_loop(n * FETCH, jnp.minimum(live, (n + 1) * FETCH), add, 0)
-
+            step = FETCH // TOGETHER
+            lax.fori_loop(n * step, jnp.minimum(whole, (n + 1) * step), add_some, 0)
+
+    lax.fori_loop(whole * TOGETHER, live, add_one, 0)
     multiply(dense.at[pl.ds(AWAY, AWAY)], held, extra, away_out)
     multiply(dense.at[pl.ds(0, AWAY)], held, extra, kept_out)
 
@@ -178,8 +190,9 @@
         total = kept[chunk] + away[chunk]
         sums = total[0:TILE]
         lines = list(as_integers(jnp.max(sums, axis=0, keepdims=True)))
-        factor = TOP / (lines[0] * jnp.exp2(lines[1]))
-        codes = jnp.minimum(jnp.floor(sums * factor + 0.5), TOP).astype(jnp.int32)
+        factor = TOP / jnp.sqrt(jnp.sqrt(lines[0] * jnp.exp2(lines[1])))
+        codes = jnp.floor(jnp.sqrt(jnp.sqrt(sums)) * factor + 0.5)
+        codes = jnp.minimum(codes, TOP).astype(jnp.int32)
         coded[0:HALF, :] = lax.shift_left(codes[0:HALF], 16) | codes[HALF:TILE]
         lines += as_integers(total[TILE : TILE + 1])
         lines += as_integers(total[TILE + 1 : TILE + 2])
@@ -207,6 +220,11 @@
     return high, middle, rest - middle
 
 
+def fourth_power(codes):
+    root = f32(codes) * (1.0 / TOP)
+    return (root * root) * (root * root)
+
+
 def decoded(chunks):
     highs = jnp.zeros((HALF, PANEL), jnp.float32)
     lows = jnp.zeros((HALF, PANEL), jnp.float32)
@@ -214,11 +232,11 @@
     for coded in chunks:
         tail = f32(coded[HALF:CODED, :])
         power = jnp.exp2(jnp.minimum(tail, 127.0))
-        step = tail[0:1] * power[1:2] * (1.0 / TOP)
+        scale = tail[0:1] * power[1:2]
         shares.append(tail[2:3] * power[3:4] + tail[4:5] * power[5:6])
         codes = coded[0:HALF, :]
-        highs = highs + f32(lax.shift_right_logical(codes, 16)) * step
-        lows = lows + f32(codes & 65535) * step
+        highs = highs + fourth_power(lax.shift_right_logical(codes, 16)) * scale
+        lows = lows + fourth_power(codes & 65535) * scale
     return jnp.concatenate([highs, lows], axis=0), shares
 
 
@@ -243,14 +261,14 @@
     return jnp.where(vertex == jnp.broadcast_to(ids[...], (TILE, PANEL)), 1.0, 0.0)
 
 
-def first_level_kernel(own, one, three, two, depth, raw, out):
+def first_level_kernel(own, two, one, three, depth, raw, out):
     product, _ = decoded((own, one, two, three))
     paths = jnp.where(depth[...] >= 1, product, 0.0)
     raw[...] = paths
     outgoing(paths, out)
 
 
-def level_kernel(level, own, one, three, two, depth, raw_in, sums_in, raw, out, sums, scale):
+def level_kernel(level, own, two, one, three, depth, raw_in, sums_in, raw, out, sums, scale):
     before = start_piece(sums_in) if level == 2 else sums_in[...]
     product, shares = decoded((own, one, two, three))
     mean_square = jnp.zeros((1, PANEL), jnp.float32)
@@ -294,12 +312,38 @@
 def exchanged(kept, away):
     chunks = encoded(kept, from_partner(away))
     moved = {k: along_z(chunks[k], k) for k in ORDER}
-    return chunks[0], moved[1], moved[3], moved[2]
-
-
-def summed_alike(x, axes):
-    copies = jnp.broadcast_to(x, (lax.axis_size(axes), EXTRA, PANEL))
-    return jnp.sum(lax.all_to_all(copies, axes, 0, 0, tiled=True)[:, 0], axis=0, keepdims=True)
+    return (chunks[0], *(moved[k] for k in ORDER))
+
+
+def everywhere(line, axes):
+    copies = jnp.broadcast_to(line, (lax.axis_size(axes), EXTRA, PANEL))
+    return lax.all_to_all(copies, axes, 0, 0, tiled=True)
+
+
+def last_kernel(squares, raw, sums, *refs):
+    scales, (path_sums, log_scales) = refs[:-2], refs[-2:]
+    total = squares[0, 0:1, :]
+    for i in range(1, squares.shape[0]):
+        total = total + squares[i, 0:1, :]
+    mean_square = total / VERTICES + EPSILON
+    path_sums[...] = sums[...] + raw[...] * lax.rsqrt(mean_square)
+    for n, scale in enumerate(scales):
+        log_scales[n : n + 1, :] = 0.5 * jnp.log(scale[...])
+    log_scales[LEVELS - 1 : LEVELS, :] = 0.5 * jnp.log(mean_square)
+
+
+def last_level(squares, raw, sums, scales):
+    return pl.pallas_call(
+        last_kernel,
+        in_specs=[VMEM] * (3 + len(scales)),
+        out_specs=[VMEM] * 2,
+        out_shape=[
+            jax.ShapeDtypeStruct((TILE, PANEL), jnp.float32),
+            jax.ShapeDtypeStruct((LEVELS, PANEL), jnp.float32),
+        ],
+        compiler_params=LIMIT,
+        name="last_level",
+    )(squares, raw, sums, *scales)
 
 
 def local(adj_tiles, tile_rows, tile_cols, tile_count, tile_depth, source_ids):
@@ -316,12 +360,8 @@
         chunks = exchanged(kept_products(dense, held, extra), away)
         raw, piece, sums, scale = finish_level(level, chunks, tile_depth, raw, sums)
         scales.append(scale)
-    squares = piece
-    total = summed_alike(summed_alike(squares, ("row_1",) + COL), ("row_0", "row_2"))
-    mean_square = total / VERTICES + EPSILON
-    scales.append(mean_square)
-    path_sums = sums + raw * lax.rsqrt(mean_square)
-    return path_sums, 0.5 * jnp.log(jnp.concatenate(scales, axis=0))
+    squares = jnp.sum(everywhere(piece, ("row_1",) + COL)[:, 0], axis=0, keepdims=True)
+    return tuple(last_level(everywhere(squares, ("row_0", "row_2")), raw, sums, scales))
 
 
 def solution(mesh):

time: 236 us -> 228 us (0.966)
  starting transfers between devices: 71.2 us -> 58.3 us
  blocking collectives: 128 us -> 132 us
    ppermute x18, starting transfers between devices: 51.7 us -> 41.7 us  [along_z(): return lax.ppermute(x, 'col_0', [(i, (i + k) % 4) for i in range(4)])]
    all_to_all x5, blocking collectives: 103 us -> 108 us  [local(): sources = lax.all_to_all(spread, ROW, 0, 0, tiled=True)]
    ppermute x6, starting transfers between devices: 19.5 us -> 16.6 us  [from_partner(): return lax.ppermute(x, 'col_1', [(0, 1), (1, 0)])]
  transfers between devices with their start and end apart: 24 -> 24, of which waited for: 7 -> 17; matrix products, arithmetic and copies ran while one was open for 0% -> 0% of each run, Pallas kernels for 3% -> 3%
where the time goes in v4:
time: 228 us
  blocking collectives  132 us (58%)
  starting transfers between devices  58.3 us (26%)
  Pallas kernels  20.1 us (9%)
  waiting for transfers between devices  15.4 us (7%)
    all_to_all x5, blocking collectives, local(): sources = lax.all_to_all(spread, ROW, 0, 0, tiled=True)  108 us
    ppermute x18, starting transfers between devices, along_z(): return lax.ppermute(x, 'col_0', [(i, (i + k) % 4) for i in range(4)])  41.7 us
    all_to_all x2, blocking collectives, everywhere(): return lax.all_to_all(copies, axes, 0, 0, tiled=True)  23.7 us
    ppermute x6, starting transfers between devices, from_partner(): return lax.ppermute(x, 'col_1', [(0, 1), (1, 0)])  16.6 us
    ppermute x18, waiting for transfers between devices, along_z(): return lax.ppermute(x, 'col_0', [(i, (i + k) % 4) for i in range(4)])  14.2 us
    pallas_call x5, Pallas kernels, away_products(): pl.pallas_call(away_kernel, in_specs=[VMEM, VMEM], out_specs=[VMEM] * 3,...  6.65 us
    pallas_call x5, Pallas kernels, kept_products(): pl.pallas_call(kept_kernel, in_specs=[VMEM] * 3, out_specs=VMEM, out_shap...  6.22 us
  transfers between devices with their start and end apart: 24, of which 17 were waited for; matrix products, arithmetic and copies ran while one was open for 0% of the time, Pallas kernels for 3%

profile of v4, /device:TPU:1, one launch (start us, length us, event | category | flops | bytes accessed | tf_op | source)
XLA Modules:
  0.0 228.3 jit_solution(16267938473141126263)
XLA Ops:
  1.3 4.3 %first_products.1 = (f32[4,136,128]{2,1,0:T(8,128)S(1)}, f32[4,136,128]{2,1,0:T(8,128)S(1)}, bf16[1024,4096]{1,0:T(8,128)(2,1)S(1)}) custom-call(s32[1,1]{1,0:T(1,128)S(6)} %copy.9.count, s32[128]{0:T(128)} %bitcast.11, s32[128]{0:T(128)} %bitcast.12, s32[1,128]{1,0:T(1,128)} %bitcast.6, bf16[128,128,128]{2,1,0:T(8,128)(2,1)} %bitcast.9), custom_call_target="tpu_custom_call" | custom-call | tf_op jit(solution)/shard_map/first_products/pallas_call | solution.py:120
  5.6 3.3 %collective-permute-start = (f32[4,136,128]{2,1,0:T(8,128)S(1)}, f32[4,136,128]{2,1,0:T(8,128)S(1)}, u32[]{:S(2)}, u32[]{:S(2)}) collective-permute-start(f32[4,136,128]{2,1,0:T(8,128)S(1)} %get-tuple-element.68), channel_id=1, source_target_pairs={{0,1},{1,0},{2,3},{3,2},{4,5},{5,4},{6,7},{7,6},{8,9},{9,8},{10,11... | collective-permute-start | bytes 835592 | tf_op jit(solution)/shard_map/ppermute | solution.py:305
  8.9 1.2 collective-permute-done.away
  10.4 5.3 %collective-permute-start.1 = (s32[72,128]{1,0:T(8,128)S(1)}, s32[72,128]{1,0:T(8,128)S(1)}, u32[]{:S(2)}, u32[]{:S(2)}) collective-permute-start(s32[72,128]{1,0:T(8,128)S(1)} %get-tuple-element.70), channel_id=1, source_target_pairs={{0,4},{2,6},{4,0},{6,2},{1,5},{3,7},{5,1},{7,3},{8,12},{10,14},{12... | collective-permute-start | bytes 110600 | tf_op jit(solution)/shard_map/ppermute | solution.py:309
  15.7 1.2 collective-permute-start.2
  16.9 2.3 %collective-permute-start.3 = (s32[72,128]{1,0:T(8,128)S(1)}, s32[72,128]{1,0:T(8,128)S(1)}, u32[]{:S(2)}, u32[]{:S(2)}) collective-permute-start(s32[72,128]{1,0:T(8,128)S(1)} %get-tuple-element.72), channel_id=1, source_target_pairs={{0,6},{2,0},{4,2},{6,4},{1,7},{3,1},{5,3},{7,5},{8,14},{10,8},{12,... | collective-permute-start | bytes 110600 | tf_op jit(solution)/shard_map/ppermute | solution.py:309
  19.2 1.3 collective-permute-done.2.one
  20.9 25.0 %all_to_all.35.sources = bf16[32,136,128]{2,1,0:T(8,128)(2,1)S(1)} all-to-all(bf16[32,136,128]{2,1,0:T(8,128)(2,1)S(1)} %broadcast_in_dim.31), channel_id=1, replica_groups=mesh['row_0'=4,'row_1'=2,'row_2'=4,'col_0'=4,'col_1'=2] {'row_0','row_1'..., dimensions={0} | all-to-all | bytes 2228224 | tf_op jit(solution)/shard_map/all_to_all | solution.py:358
  45.8 1.3 away_products.5
  47.2 3.3 %collective-permute-start.4 = (f32[4,136,128]{2,1,0:T(8,128)S(1)}, f32[4,136,128]{2,1,0:T(8,128)S(1)}, u32[]{:S(2)}, u32[]{:S(2)}) collective-permute-start(f32[4,136,128]{2,1,0:T(8,128)S(1)} %get-tuple-element.76), channel_id=1, source_target_pairs={{0,1},{1,0},{2,3},{3,2},{4,5},{5,4},{6,7},{7,6},{8,9},{9,8},{10,11... | collective-permute-start | bytes 835592 | tf_op jit(solution)/shard_map/ppermute | solution.py:305
  50.5 1.2 kept_products.5.kept
  52.0 2.9 %collective-permute-start.5 = (s32[72,128]{1,0:T(8,128)S(1)}, s32[72,128]{1,0:T(8,128)S(1)}, u32[]{:S(2)}, u32[]{:S(2)}) collective-permute-start(s32[72,128]{1,0:T(8,128)S(1)} %get-tuple-element.78), channel_id=1, source_target_pairs={{0,4},{2,6},{4,0},{6,2},{1,5},{3,7},{5,1},{7,3},{8,12},{10,14},{12... | collective-permute-start | bytes 110600 | tf_op jit(solution)/shard_map/ppermute | solution.py:309
  54.9 3.0 %collective-permute-start.6 = (s32[72,128]{1,0:T(8,128)S(1)}, s32[72,128]{1,0:T(8,128)S(1)}, u32[]{:S(2)}, u32[]{:S(2)}) collective-permute-start(s32[72,128]{1,0:T(8,128)S(1)} %get-tuple-element.79), channel_id=1, source_target_pairs={{0,2},{2,4},{4,6},{6,0},{1,3},{3,5},{5,7},{7,1},{8,10},{10,12},{12... | collective-permute-start | bytes 110600 | tf_op jit(solution)/shard_map/ppermute | solution.py:309
  59.0 2.2 collective-permute-done.6.refs_2_
  61.2 0.8 collective-permute-done.7.refs_3_
  62.3 19.4 %all_to_all.36.sources = bf16[32,136,128]{2,1,0:T(8,128)(2,1)S(1)} all-to-all(bf16[32,136,128]{2,1,0:T(8,128)(2,1)S(1)} %broadcast_in_dim.32), channel_id=1, replica_groups=mesh['row_0'=4,'row_1'=2,'row_2'=4,'col_0'=4,'col_1'=2] {'row_0','row_1'..., dimensions={0} | all-to-all | bytes 2228224 | tf_op jit(solution)/shard_map/all_to_all | solution.py:358
  81.7 1.3 away_products.6
  83.1 3.3 %collective-permute-start.8 = (f32[4,136,128]{2,1,0:T(8,128)S(1)}, f32[4,136,128]{2,1,0:T(8,128)S(1)}, u32[]{:S(2)}, u32[]{:S(2)}) collective-permute-start(f32[4,136,128]{2,1,0:T(8,128)S(1)} %get-tuple-element.85), channel_id=1, source_target_pairs={{0,1},{1,0},{2,3},{3,2},{4,5},{5,4},{6,7},{7,6},{8,9},{9,8},{10,11... | collective-permute-start | bytes 835592 | tf_op jit(solution)/shard_map/ppermute | solution.py:305
  86.3 1.2 kept_products.6.kept
  87.9 3.0 %collective-permute-start.9 = (s32[72,128]{1,0:T(8,128)S(1)}, s32[72,128]{1,0:T(8,128)S(1)}, u32[]{:S(2)}, u32[]{:S(2)}) collective-permute-start(s32[72,128]{1,0:T(8,128)S(1)} %get-tuple-element.87), channel_id=1, source_target_pairs={{0,4},{2,6},{4,0},{6,2},{1,5},{3,7},{5,1},{7,3},{8,12},{10,14},{12... | collective-permute-start | bytes 110600 | tf_op jit(solution)/shard_map/ppermute | solution.py:309
  90.8 1.4 collective-permute-start.10
  92.2 2.2 collective-permute-start.11
  94.8 2.0 collective-permute-done.10.refs_2_
  97.1 21.7 %all_to_all.37.sources = bf16[32,136,128]{2,1,0:T(8,128)(2,1)S(1)} all-to-all(bf16[32,136,128]{2,1,0:T(8,128)(2,1)S(1)} %broadcast_in_dim.33), channel_id=1, replica_groups=mesh['row_0'=4,'row_1'=2,'row_2'=4,'col_0'=4,'col_1'=2] {'row_0','row_1'..., dimensions={0} | all-to-all | bytes 2228224 | tf_op jit(solution)/shard_map/all_to_all | solution.py:358
  118.7 1.3 away_products.7
  120.1 2.1 collective-permute-start.12
  122.2 1.2 kept_products.7.kept
  123.7 3.0 %collective-permute-start.13 = (s32[72,128]{1,0:T(8,128)S(1)}, s32[72,128]{1,0:T(8,128)S(1)}, u32[]{:S(2)}, u32[]{:S(2)}) collective-permute-start(s32[72,128]{1,0:T(8,128)S(1)} %get-tuple-element.97), channel_id=1, source_target_pairs={{0,4},{2,6},{4,0},{6,2},{1,5},{3,7},{5,1},{7,3},{8,12},{10,14},{12... | collective-permute-start | bytes 110600 | tf_op jit(solution)/shard_map/ppermute | solution.py:309
  126.7 1.0 collective-permute-start.14
  127.7 2.6 %collective-permute-start.15 = (s32[72,128]{1,0:T(8,128)S(1)}, s32[72,128]{1,0:T(8,128)S(1)}, u32[]{:S(2)}, u32[]{:S(2)}) collective-permute-start(s32[72,128]{1,0:T(8,128)S(1)} %get-tuple-element.99), channel_id=1, source_target_pairs={{0,6},{2,0},{4,2},{6,4},{1,7},{3,1},{5,3},{7,5},{8,14},{10,8},{12,... | collective-permute-start | bytes 110600 | tf_op jit(solution)/shard_map/ppermute | solution.py:309
  130.6 1.1 collective-permute-done.14.refs_2_
  132.8 20.9 %all_to_all.38.sources = bf16[32,136,128]{2,1,0:T(8,128)(2,1)S(1)} all-to-all(bf16[32,136,128]{2,1,0:T(8,128)(2,1)S(1)} %broadcast_in_dim.34), channel_id=1, replica_groups=mesh['row_0'=4,'row_1'=2,'row_2'=4,'col_0'=4,'col_1'=2] {'row_0','row_1'..., dimensions={0} | all-to-all | bytes 2228224 | tf_op jit(solution)/shard_map/all_to_all | solution.py:358
  153.6 1.3 away_products.8
  155.0 2.6 %collective-permute-start.16 = (f32[4,136,128]{2,1,0:T(8,128)S(1)}, f32[4,136,128]{2,1,0:T(8,128)S(1)}, u32[]{:S(2)}, u32[]{:S(2)}) collective-permute-start(f32[4,136,128]{2,1,0:T(8,128)S(1)} %get-tuple-element.105), channel_id=1, source_target_pairs={{0,1},{1,0},{2,3},{3,2},{4,5},{5,4},{6,7},{7,6},{8,9},{9,8},{10,11... | collective-permute-start | bytes 835592 | tf_op jit(solution)/shard_map/ppermute | solution.py:305
  157.6 1.2 kept_products.8.kept
  159.1 3.0 %collective-permute-start.17 = (s32[72,128]{1,0:T(8,128)S(1)}, s32[72,128]{1,0:T(8,128)S(1)}, u32[]{:S(2)}, u32[]{:S(2)}) collective-permute-start(s32[72,128]{1,0:T(8,128)S(1)} %get-tuple-element.107), channel_id=1, source_target_pairs={{0,4},{2,6},{4,0},{6,2},{1,5},{3,7},{5,1},{7,3},{8,12},{10,14},{12... | collective-permute-start | bytes 110600 | tf_op jit(solution)/shard_map/ppermute | solution.py:309
  162.0 2.0 collective-permute-start.18
  164.0 1.6 collective-permute-start.19
  166.0 2.1 collective-permute-done.18.refs_2_
  168.7 21.6 %all_to_all.39.sources = bf16[32,136,128]{2,1,0:T(8,128)(2,1)S(1)} all-to-all(bf16[32,136,128]{2,1,0:T(8,128)(2,1)S(1)} %broadcast_in_dim.35), channel_id=1, replica_groups=mesh['row_0'=4,'row_1'=2,'row_2'=4,'col_0'=4,'col_1'=2] {'row_0','row_1'..., dimensions={0} | all-to-all | bytes 2228224 | tf_op jit(solution)/shard_map/all_to_all | solution.py:358
  190.2 1.3 away_products.9
  191.6 2.1 collective-permute-start.20
  193.6 1.2 kept_products.9.kept
  195.2 3.1 %collective-permute-start.21 = (s32[72,128]{1,0:T(8,128)S(1)}, s32[72,128]{1,0:T(8,128)S(1)}, u32[]{:S(2)}, u32[]{:S(2)}) collective-permute-start(s32[72,128]{1,0:T(8,128)S(1)} %get-tuple-element.117), channel_id=1, source_target_pairs={{0,4},{2,6},{4,0},{6,2},{1,5},{3,7},{5,1},{7,3},{8,12},{10,14},{12... | collective-permute-start | bytes 110600 | tf_op jit(solution)/shard_map/ppermute | solution.py:309
  198.9 2.9 %collective-permute-start.23 = (s32[72,128]{1,0:T(8,128)S(1)}, s32[72,128]{1,0:T(8,128)S(1)}, u32[]{:S(2)}, u32[]{:S(2)}) collective-permute-start(s32[72,128]{1,0:T(8,128)S(1)} %get-tuple-element.119), channel_id=1, source_target_pairs={{0,6},{2,0},{4,2},{6,4},{1,7},{3,1},{5,3},{7,5},{8,14},{10,8},{12,... | collective-permute-start | bytes 110600 | tf_op jit(solution)/shard_map/ppermute | solution.py:309
  202.1 1.5 collective-permute-done.22.refs_2_
  203.8 14.5 %all_to_all.40 = f32[16,8,128]{2,1,0:T(8,128)S(1)} all-to-all(f32[16,8,128]{2,1,0:T(8,128)S(1)} %broadcast_in_dim.36), channel_id=1, replica_groups=mesh['row_0'=4,'row_1'=2,'row_2'=4,'col_0'=4,'col_1'=2] {'row_1','col_0'..., dimensions={0} | all-to-all | bytes 131072 | tf_op jit(solution)/shard_map/all_to_all | solution.py:320
  218.4 9.2 %all_to_all.41.squares = f32[16,8,128]{2,1,0:T(8,128)S(1)} all-to-all(f32[16,8,128]{2,1,0:T(8,128)S(1)} %broadcast_in_dim.37), channel_id=1, replica_groups=mesh['row_0'=4,'row_1'=2,'row_2'=4,'col_0'=4,'col_1'=2] {'row_0','row_2'}, dimensions={0} | all-to-all | bytes 131072 | tf_op jit(solution)/shard_map/all_to_all | solution.py:320
  (44 shorter events, 8.0 us)
Async XLA Ops:
  1.3 19.4 %copy-start = (s32[1,128]{1,0:T(1,128)S(1)}, s32[1,128]{1,0:T(1,128)}, u32[]{:S(2)}) copy-start(s32[1,128]{1,0:T(1,128)} %refs_4_.9) | copy-start | bytes 1540
  5.6 4.5 %collective-permute-start = (f32[4,136,128]{2,1,0:T(8,128)S(1)}, f32[4,136,128]{2,1,0:T(8,128)S(1)}, u32[]{:S(2)}, u32[]{:S(2)}) collective-permute-start(f32[4,136,128]{2,1,0:T(8,128)S(1)} %get-tuple-element.68), channel_id=1, source_target_pairs={{0,1},{1,0},{2,3},{3,2},{4,5},{5,4},{6,7},{7,6},{8,9},{9,8},{10,11... | collective-permute-start | bytes 835592 | tf_op jit(solution)/shard_map/ppermute | solution.py:305
  10.4 8.9 %collective-permute-start.1 = (s32[72,128]{1,0:T(8,128)S(1)}, s32[72,128]{1,0:T(8,128)S(1)}, u32[]{:S(2)}, u32[]{:S(2)}) collective-permute-start(s32[72,128]{1,0:T(8,128)S(1)} %get-tuple-element.70), channel_id=1, source_target_pairs={{0,4},{2,6},{4,0},{6,2},{1,5},{3,7},{5,1},{7,3},{8,12},{10,14},{12... | collective-permute-start | bytes 110600 | tf_op jit(solution)/shard_map/ppermute | solution.py:309
  15.7 4.9 %collective-permute-start.2 = (s32[72,128]{1,0:T(8,128)S(1)}, s32[72,128]{1,0:T(8,128)S(1)}, u32[]{:S(2)}, u32[]{:S(2)}) collective-permute-start(s32[72,128]{1,0:T(8,128)S(1)} %get-tuple-element.71), channel_id=1, source_target_pairs={{0,2},{2,4},{4,6},{6,0},{1,3},{3,5},{5,7},{7,1},{8,10},{10,12},{12... | collective-permute-start | bytes 110600 | tf_op jit(solution)/shard_map/ppermute | solution.py:309
  16.9 3.8 %collective-permute-start.3 = (s32[72,128]{1,0:T(8,128)S(1)}, s32[72,128]{1,0:T(8,128)S(1)}, u32[]{:S(2)}, u32[]{:S(2)}) collective-permute-start(s32[72,128]{1,0:T(8,128)S(1)} %get-tuple-element.72), channel_id=1, source_target_pairs={{0,6},{2,0},{4,2},{6,4},{1,7},{3,1},{5,3},{7,5},{8,14},{10,8},{12,... | collective-permute-start | bytes 110600 | tf_op jit(solution)/shard_map/ppermute | solution.py:309
  47.2 4.6 %collective-permute-start.4 = (f32[4,136,128]{2,1,0:T(8,128)S(1)}, f32[4,136,128]{2,1,0:T(8,128)S(1)}, u32[]{:S(2)}, u32[]{:S(2)}) collective-permute-start(f32[4,136,128]{2,1,0:T(8,128)S(1)} %get-tuple-element.76), channel_id=1, source_target_pairs={{0,1},{1,0},{2,3},{3,2},{4,5},{5,4},{6,7},{7,6},{8,9},{9,8},{10,11... | collective-permute-start | bytes 835592 | tf_op jit(solution)/shard_map/ppermute | solution.py:305
  50.5 11.5 %copy-start.1 = (s32[128]{0:T(128)S(1)}, s32[128]{0:T(128)}, u32[]{:S(2)}) copy-start(s32[128]{0:T(128)} %param.11) | copy-start | bytes 1540
  52.0 6.9 %collective-permute-start.5 = (s32[72,128]{1,0:T(8,128)S(1)}, s32[72,128]{1,0:T(8,128)S(1)}, u32[]{:S(2)}, u32[]{:S(2)}) collective-permute-start(s32[72,128]{1,0:T(8,128)S(1)} %get-tuple-element.78), channel_id=1, source_target_pairs={{0,4},{2,6},{4,0},{6,2},{1,5},{3,7},{5,1},{7,3},{8,12},{10,14},{12... | collective-permute-start | bytes 110600 | tf_op jit(solution)/shard_map/ppermute | solution.py:309
  54.9 6.3 %collective-permute-start.6 = (s32[72,128]{1,0:T(8,128)S(1)}, s32[72,128]{1,0:T(8,128)S(1)}, u32[]{:S(2)}, u32[]{:S(2)}) collective-permute-start(s32[72,128]{1,0:T(8,128)S(1)} %get-tuple-element.79), channel_id=1, source_target_pairs={{0,2},{2,4},{4,6},{6,0},{1,3},{3,5},{5,7},{7,1},{8,10},{10,12},{12... | collective-permute-start | bytes 110600 | tf_op jit(solution)/shard_map/ppermute | solution.py:309
  57.9 4.1 %collective-permute-start.7 = (s32[72,128]{1,0:T(8,128)S(1)}, s32[72,128]{1,0:T(8,128)S(1)}, u32[]{:S(2)}, u32[]{:S(2)}) collective-permute-start(s32[72,128]{1,0:T(8,128)S(1)} %get-tuple-element.80), channel_id=1, source_target_pairs={{0,6},{2,0},{4,2},{6,4},{1,7},{3,1},{5,3},{7,5},{8,14},{10,8},{12,... | collective-permute-start | bytes 110600 | tf_op jit(solution)/shard_map/ppermute | solution.py:309
  83.1 4.5 %collective-permute-start.8 = (f32[4,136,128]{2,1,0:T(8,128)S(1)}, f32[4,136,128]{2,1,0:T(8,128)S(1)}, u32[]{:S(2)}, u32[]{:S(2)}) collective-permute-start(f32[4,136,128]{2,1,0:T(8,128)S(1)} %get-tuple-element.85), channel_id=1, source_target_pairs={{0,1},{1,0},{2,3},{3,2},{4,5},{5,4},{6,7},{7,6},{8,9},{9,8},{10,11... | collective-permute-start | bytes 835592 | tf_op jit(solution)/shard_map/ppermute | solution.py:305
  87.9 6.9 %collective-permute-start.9 = (s32[72,128]{1,0:T(8,128)S(1)}, s32[72,128]{1,0:T(8,128)S(1)}, u32[]{:S(2)}, u32[]{:S(2)}) collective-permute-start(s32[72,128]{1,0:T(8,128)S(1)} %get-tuple-element.87), channel_id=1, source_target_pairs={{0,4},{2,6},{4,0},{6,2},{1,5},{3,7},{5,1},{7,3},{8,12},{10,14},{12... | collective-permute-start | bytes 110600 | tf_op jit(solution)/shard_map/ppermute | solution.py:309
  90.8 6.0 %collective-permute-start.10 = (s32[72,128]{1,0:T(8,128)S(1)}, s32[72,128]{1,0:T(8,128)S(1)}, u32[]{:S(2)}, u32[]{:S(2)}) collective-permute-start(s32[72,128]{1,0:T(8,128)S(1)} %get-tuple-element.88), channel_id=1, source_target_pairs={{0,2},{2,4},{4,6},{6,0},{1,3},{3,5},{5,7},{7,1},{8,10},{10,12},{12... | collective-permute-start | bytes 110600 | tf_op jit(solution)/shard_map/ppermute | solution.py:309
  92.2 4.6 %collective-permute-start.11 = (s32[72,128]{1,0:T(8,128)S(1)}, s32[72,128]{1,0:T(8,128)S(1)}, u32[]{:S(2)}, u32[]{:S(2)}) collective-permute-start(s32[72,128]{1,0:T(8,128)S(1)} %get-tuple-element.89), channel_id=1, source_target_pairs={{0,6},{2,0},{4,2},{6,4},{1,7},{3,1},{5,3},{7,5},{8,14},{10,8},{12,... | collective-permute-start | bytes 110600 | tf_op jit(solution)/shard_map/ppermute | solution.py:309
  120.1 3.3 %collective-permute-start.12 = (f32[4,136,128]{2,1,0:T(8,128)S(1)}, f32[4,136,128]{2,1,0:T(8,128)S(1)}, u32[]{:S(2)}, u32[]{:S(2)}) collective-permute-start(f32[4,136,128]{2,1,0:T(8,128)S(1)} %get-tuple-element.95), channel_id=1, source_target_pairs={{0,1},{1,0},{2,3},{3,2},{4,5},{5,4},{6,7},{7,6},{8,9},{9,8},{10,11... | collective-permute-start | bytes 835592 | tf_op jit(solution)/shard_map/ppermute | solution.py:305
  123.7 6.9 %collective-permute-start.13 = (s32[72,128]{1,0:T(8,128)S(1)}, s32[72,128]{1,0:T(8,128)S(1)}, u32[]{:S(2)}, u32[]{:S(2)}) collective-permute-start(s32[72,128]{1,0:T(8,128)S(1)} %get-tuple-element.97), channel_id=1, source_target_pairs={{0,4},{2,6},{4,0},{6,2},{1,5},{3,7},{5,1},{7,3},{8,12},{10,14},{12... | collective-permute-start | bytes 110600 | tf_op jit(solution)/shard_map/ppermute | solution.py:309
  126.7 5.0 %collective-permute-start.14 = (s32[72,128]{1,0:T(8,128)S(1)}, s32[72,128]{1,0:T(8,128)S(1)}, u32[]{:S(2)}, u32[]{:S(2)}) collective-permute-start(s32[72,128]{1,0:T(8,128)S(1)} %get-tuple-element.98), channel_id=1, source_target_pairs={{0,2},{2,4},{4,6},{6,0},{1,3},{3,5},{5,7},{7,1},{8,10},{10,12},{12... | collective-permute-start | bytes 110600 | tf_op jit(solution)/shard_map/ppermute | solution.py:309
  127.7 4.8 %collective-permute-start.15 = (s32[72,128]{1,0:T(8,128)S(1)}, s32[72,128]{1,0:T(8,128)S(1)}, u32[]{:S(2)}, u32[]{:S(2)}) collective-permute-start(s32[72,128]{1,0:T(8,128)S(1)} %get-tuple-element.99), channel_id=1, source_target_pairs={{0,6},{2,0},{4,2},{6,4},{1,7},{3,1},{5,3},{7,5},{8,14},{10,8},{12,... | collective-permute-start | bytes 110600 | tf_op jit(solution)/shard_map/ppermute | solution.py:309
  155.0 3.8 %collective-permute-start.16 = (f32[4,136,128]{2,1,0:T(8,128)S(1)}, f32[4,136,128]{2,1,0:T(8,128)S(1)}, u32[]{:S(2)}, u32[]{:S(2)}) collective-permute-start(f32[4,136,128]{2,1,0:T(8,128)S(1)} %get-tuple-element.105), channel_id=1, source_target_pairs={{0,1},{1,0},{2,3},{3,2},{4,5},{5,4},{6,7},{7,6},{8,9},{9,8},{10,11... | collective-permute-start | bytes 835592 | tf_op jit(solution)/shard_map/ppermute | solution.py:305
  159.1 6.9 %collective-permute-start.17 = (s32[72,128]{1,0:T(8,128)S(1)}, s32[72,128]{1,0:T(8,128)S(1)}, u32[]{:S(2)}, u32[]{:S(2)}) collective-permute-start(s32[72,128]{1,0:T(8,128)S(1)} %get-tuple-element.107), channel_id=1, source_target_pairs={{0,4},{2,6},{4,0},{6,2},{1,5},{3,7},{5,1},{7,3},{8,12},{10,14},{12... | collective-permute-start | bytes 110600 | tf_op jit(solution)/shard_map/ppermute | solution.py:309
  162.0 6.1 %collective-permute-start.18 = (s32[72,128]{1,0:T(8,128)S(1)}, s32[72,128]{1,0:T(8,128)S(1)}, u32[]{:S(2)}, u32[]{:S(2)}) collective-permute-start(s32[72,128]{1,0:T(8,128)S(1)} %get-tuple-element.108), channel_id=1, source_target_pairs={{0,2},{2,4},{4,6},{6,0},{1,3},{3,5},{5,7},{7,1},{8,10},{10,12},{12... | collective-permute-start | bytes 110600 | tf_op jit(solution)/shard_map/ppermute | solution.py:309
  164.0 4.4 %collective-permute-start.19 = (s32[72,128]{1,0:T(8,128)S(1)}, s32[72,128]{1,0:T(8,128)S(1)}, u32[]{:S(2)}, u32[]{:S(2)}) collective-permute-start(s32[72,128]{1,0:T(8,128)S(1)} %get-tuple-element.109), channel_id=1, source_target_pairs={{0,6},{2,0},{4,2},{6,4},{1,7},{3,1},{5,3},{7,5},{8,14},{10,8},{12,... | collective-permute-start | bytes 110600 | tf_op jit(solution)/shard_map/ppermute | solution.py:309
  191.6 3.3 %collective-permute-start.20 = (f32[4,136,128]{2,1,0:T(8,128)S(1)}, f32[4,136,128]{2,1,0:T(8,128)S(1)}, u32[]{:S(2)}, u32[]{:S(2)}) collective-permute-start(f32[4,136,128]{2,1,0:T(8,128)S(1)} %get-tuple-element.115), channel_id=1, source_target_pairs={{0,1},{1,0},{2,3},{3,2},{4,5},{5,4},{6,7},{7,6},{8,9},{9,8},{10,11... | collective-permute-start | bytes 835592 | tf_op jit(solution)/shard_map/ppermute | solution.py:305
  195.2 6.9 %collective-permute-start.21 = (s32[72,128]{1,0:T(8,128)S(1)}, s32[72,128]{1,0:T(8,128)S(1)}, u32[]{:S(2)}, u32[]{:S(2)}) collective-permute-start(s32[72,128]{1,0:T(8,128)S(1)} %get-tuple-element.117), channel_id=1, source_target_pairs={{0,4},{2,6},{4,0},{6,2},{1,5},{3,7},{5,1},{7,3},{8,12},{10,14},{12... | collective-permute-start | bytes 110600 | tf_op jit(solution)/shard_map/ppermute | solution.py:309
  198.3 5.3 %collective-permute-start.22 = (s32[72,128]{1,0:T(8,128)S(1)}, s32[72,128]{1,0:T(8,128)S(1)}, u32[]{:S(2)}, u32[]{:S(2)}) collective-permute-start(s32[72,128]{1,0:T(8,128)S(1)} %get-tuple-element.118), channel_id=1, source_target_pairs={{0,2},{2,4},{4,6},{6,0},{1,3},{3,5},{5,7},{7,1},{8,10},{10,12},{12... | collective-permute-start | bytes 110600 | tf_op jit(solution)/shard_map/ppermute | solution.py:309
  198.9 4.8 %collective-permute-start.23 = (s32[72,128]{1,0:T(8,128)S(1)}, s32[72,128]{1,0:T(8,128)S(1)}, u32[]{:S(2)}, u32[]{:S(2)}) collective-permute-start(s32[72,128]{1,0:T(8,128)S(1)} %get-tuple-element.119), channel_id=1, source_target_pairs={{0,6},{2,0},{4,2},{6,4},{1,7},{3,1},{5,3},{7,5},{8,14},{10,8},{12,... | collective-permute-start | bytes 110600 | tf_op jit(solution)/shard_map/ppermute | solution.py:309

commit v5 on v4

--- a/solution.py
+++ b/solution.py
@@ -24,7 +24,6 @@
 CODED = HALF + EXTRA
 AWAY = DEST_TILES // 2 * TILE
 TOP = 65535.0
-ORDER = (2, 1, 3)
 FETCH = 16
 TOGETHER = 8
 VMEM = pl.BlockSpec(memory_space=pltpu.VMEM)
@@ -74,7 +73,8 @@
     lax.fori_loop(0, DEST_TILES, clear, 0)
     for copy in small:
         copy.wait()
-    column = lax.axis_index("col_0") * 2 + c1
+    c0 = lax.axis_index("col_0")
+    column = c0 * 2 + c1
     inner = lax.broadcasted_iota(jnp.int32, (TILE, PANEL), 0)
     wanted = jnp.broadcast_to(ids[...], (TILE, PANEL)) - inner
     for t in range(SRC_TILES):
@@ -84,7 +84,11 @@
 
     def add(k):
         d, u = rows[k], cols[k]
-        block = ((d & 1) ^ c1) * (DEST_TILES // 2) + (d >> 1)
+        step = ((d >> 1) - c0) & 3
+        beside = (step & 1) == 1
+        owner = jnp.where(beside, step >> 1, d & 1)
+        spot = jnp.where(beside, (d & 1) ^ owner, 3 - (step >> 1))
+        block = (owner ^ c1) * (DEST_TILES // 2) + spot
         down = pl.ds(pl.multiple_of(block * TILE, TILE), TILE)
         across = pl.ds(pl.multiple_of(u * TILE, TILE), TILE)
         dense[down, across] = dense[down, across] + staged[k]
@@ -183,11 +187,10 @@
     return jnp.floor(x * jnp.exp2(-exponent) + 0.5), exponent
 
 
-def encode_kernel(kept, away, *outs):
+def encode_kernel(kept, away, beside, far, own):
     row = lax.broadcasted_iota(jnp.int32, (EXTRA, PANEL), 0)
-    for k, coded in enumerate(outs):
-        chunk = (lax.axis_index("col_0") + k) & 3
-        total = kept[chunk] + away[chunk]
+    for k, coded in enumerate((beside.at[0], beside.at[1], far, own)):
+        total = kept[k] + away[k]
         sums = total[0:TILE]
         lines = list(as_integers(jnp.max(sums, axis=0, keepdims=True)))
         factor = TOP / jnp.sqrt(jnp.sqrt(lines[0] * jnp.exp2(lines[1])))
@@ -206,8 +209,12 @@
     return pl.pallas_call(
         encode_kernel,
         in_specs=[VMEM] * 2,
-        out_specs=[VMEM] * 4,
-        out_shape=[jax.ShapeDtypeStruct((CODED, PANEL), jnp.int32)] * 4,
+        out_specs=[VMEM] * 3,
+        out_shape=[
+            jax.ShapeDtypeStruct((2, CODED, PANEL), jnp.int32),
+            jax.ShapeDtypeStruct((CODED, PANEL), jnp.int32),
+            jax.ShapeDtypeStruct((CODED, PANEL), jnp.int32),
+        ],
         compiler_params=LIMIT,
         name="encoded",
     )(kept, away)
@@ -261,19 +268,21 @@
     return jnp.where(vertex == jnp.broadcast_to(ids[...], (TILE, PANEL)), 1.0, 0.0)
 
 
-def first_level_kernel(own, two, one, three, depth, raw, out):
-    product, _ = decoded((own, one, two, three))
+def first_level_kernel(own, heard, handed, far, depth, raw, out):
+    product, _ = decoded((own, heard.at[0], handed, far))
     paths = jnp.where(depth[...] >= 1, product, 0.0)
     raw[...] = paths
     outgoing(paths, out)
 
 
-def level_kernel(level, own, two, one, three, depth, raw_in, sums_in, raw, out, sums, scale):
+def level_kernel(level, own, heard, handed, far, depth, raw_in, sums_in, raw, out, sums, scale):
     before = start_piece(sums_in) if level == 2 else sums_in[...]
-    product, shares = decoded((own, one, two, three))
+    product, shares = decoded((own, heard.at[0], handed, far))
     mean_square = jnp.zeros((1, PANEL), jnp.float32)
+    turned = 2 * lax.axis_index("col_1")
+    back = (0, 1 + turned, 3 - turned, 2)
     for j in range(4):
-        for k, share in enumerate(shares):
+        for k, share in zip(back, shares):
             here = ((lax.axis_index("col_0") - j) & 3) == k
             mean_square = mean_square + jnp.where(here, share, 0.0)
     mean_square = mean_square / VERTICES + EPSILON
@@ -305,14 +314,14 @@
     return lax.ppermute(x, "col_1", [(0, 1), (1, 0)])
 
 
-def along_z(x, k):
-    return lax.ppermute(x, "col_0", [(i, (i + k) % 4) for i in range(4)])
-
-
 def exchanged(kept, away):
-    chunks = encoded(kept, from_partner(away))
-    moved = {k: along_z(chunks[k], k) for k in ORDER}
-    return (chunks[0], *(moved[k] for k in ORDER))
+    beside, far, own = encoded(kept, from_partner(away))
+    forward = [(2 * i, 2 * ((i + 1) % 4)) for i in range(4)]
+    backward = [(2 * i + 1, 2 * ((i - 1) % 4) + 1) for i in range(4)]
+    heard = lax.ppermute(beside, COL, forward + backward)
+    handed = from_partner(heard[1])
+    far = lax.ppermute(far, "col_0", [(i, (i + 2) % 4) for i in range(4)])
+    return own, heard, handed, far
 
 
 def everywhere(line, axes):

time: 228 us -> 225 us (0.987)
  starting transfers between devices: 58.3 us -> 50.7 us
  waiting for transfers between devices: 15.4 us -> 20.5 us
    ppermute x18 -> x12, starting transfers between devices: 41.7 us -> 27 us  [the longest x6 14.6 us: exchanged(): far = lax.ppermute(far, 'col_0', [(i, (i + 2) % 4) for i in range(4)])]
    ppermute x6 -> x12, starting transfers between devices: 16.6 us -> 23.8 us  [from_partner(): return lax.ppermute(x, 'col_1', [(0, 1), (1, 0)])]
    ppermute x18 -> x12, waiting for transfers between devices: 14.2 us -> 18.8 us  [the longest x6 12.4 us: exchanged(): far = lax.ppermute(far, 'col_0', [(i, (i + 2) % 4) for i in range(4)])]
  transfers between devices with their start and end apart: 24 -> 24, of which waited for: 17 -> 12; matrix products, arithmetic and copies ran while one was open for 0% -> 0% of each run, Pallas kernels for 3% -> 3%
where the time goes in v5:
time: 225 us
  blocking collectives  131 us (58%)
  starting transfers between devices  50.7 us (23%)
  waiting for transfers between devices  20.5 us (9%)
  Pallas kernels  20.4 us (9%)
    all_to_all x5, blocking collectives, local(): sources = lax.all_to_all(spread, ROW, 0, 0, tiled=True)  109 us
    ppermute x12, starting transfers between devices, from_partner(): return lax.ppermute(x, 'col_1', [(0, 1), (1, 0)])  23.8 us
    all_to_all x2, blocking collectives, everywhere(): return lax.all_to_all(copies, axes, 0, 0, tiled=True)  22.1 us
    ppermute x6, starting transfers between devices, exchanged(): far = lax.ppermute(far, 'col_0', [(i, (i + 2) % 4) for i in range(4)])  14.6 us
    ppermute x6, waiting for transfers between devices, exchanged(): far = lax.ppermute(far, 'col_0', [(i, (i + 2) % 4) for i in range(4)])  12.4 us
    ppermute x6, starting transfers between devices, exchanged(): heard = lax.ppermute(beside, COL, forward + backward)  12.4 us
    pallas_call x5, Pallas kernels, away_products(): pl.pallas_call(away_kernel, in_specs=[VMEM, VMEM], out_specs=[VMEM] * 3,...  6.65 us
    ppermute x6, waiting for transfers between devices, exchanged(): heard = lax.ppermute(beside, COL, forward + backward)  6.46 us
  transfers between devices with their start and end apart: 24, of which 12 were waited for; matrix products, arithmetic and copies ran while one was open for 0% of the time, Pallas kernels for 3%

profile of v5, /device:TPU:1, one launch (start us, length us, event | category | flops | bytes accessed | tf_op | source)
XLA Modules:
  0.0 224.8 jit_solution(4068598234171169454)
XLA Ops:
  1.3 4.8 %first_products.1 = (f32[4,136,128]{2,1,0:T(8,128)S(1)}, f32[4,136,128]{2,1,0:T(8,128)S(1)}, bf16[1024,4096]{1,0:T(8,128)(2,1)S(1)}) custom-call(s32[1,1]{1,0:T(1,128)S(6)} %copy.9.count, s32[128]{0:T(128)} %bitcast.23, s32[128]{0:T(128)} %bitcast.24, s32[1,128]{1,0:T(1,128)} %bitcast.18, bf16[128,128,128]{2,1,0:T(8,128)(2,1)} %bitcast.21), custom_call_target="tpu_custom_call" | custom-call | tf_op jit(solution)/shard_map/first_products/pallas_call | solution.py:124
  6.1 3.3 %collective-permute-start = (f32[4,136,128]{2,1,0:T(8,128)S(1)}, f32[4,136,128]{2,1,0:T(8,128)S(1)}, u32[]{:S(2)}, u32[]{:S(2)}) collective-permute-start(f32[4,136,128]{2,1,0:T(8,128)S(1)} %get-tuple-element.62), channel_id=1, source_target_pairs={{0,1},{1,0},{2,3},{3,2},{4,5},{5,4},{6,7},{7,6},{8,9},{9,8},{10,11... | collective-permute-start | bytes 835592 | tf_op jit(solution)/shard_map/ppermute | solution.py:314
  9.3 1.2 collective-permute-done.away
  10.8 5.1 %collective-permute-start.1 = (s32[2,72,128]{2,1,0:T(8,128)S(1)}, s32[2,72,128]{2,1,0:T(8,128)S(1)}, u32[]{:S(2)}, u32[]{:S(2)}) collective-permute-start(s32[2,72,128]{2,1,0:T(8,128)S(1)} %get-tuple-element.64), channel_id=1, source_target_pairs={{0,2},{2,4},{4,6},{6,0},{1,7},{3,1},{5,3},{7,5},{8,10},{10,12},{12... | collective-permute-start | bytes 221192 | tf_op jit(solution)/shard_map/ppermute | solution.py:321
  15.9 1.4 collective-permute-done.1.heard
  17.3 1.8 collective-permute-start.2
  19.1 4.6 %collective-permute-done.3.far = s32[72,128]{1,0:T(8,128)S(1)} collective-permute-done((s32[72,128]{1,0:T(8,128)S(1)}, s32[72,128]{1,0:T(8,128)S(1)}, u32[]{:S(2)}, u32[]{:S(2)}) %collective-permute-start.3) | collective-permute-done | bytes 36896 | tf_op jit(solution)/shard_map/ppermute | solution.py:323
  24.0 24.5 %all_to_all.35.sources = bf16[32,136,128]{2,1,0:T(8,128)(2,1)S(1)} all-to-all(bf16[32,136,128]{2,1,0:T(8,128)(2,1)S(1)} %broadcast_in_dim.31), channel_id=1, replica_groups=mesh['row_0'=4,'row_1'=2,'row_2'=4,'col_0'=4,'col_1'=2] {'row_0','row_1'..., dimensions={0} | all-to-all | bytes 2228224 | tf_op jit(solution)/shard_map/all_to_all | solution.py:367
  48.5 1.3 away_products.5
  49.8 1.6 collective-permute-start.4
  51.4 1.2 kept_products.5.kept
  52.9 1.8 collective-permute-start.5
  54.7 1.8 collective-permute-start.7
  56.6 1.3 collective-permute-done.5.refs_1_
  57.9 2.0 collective-permute-start.6
  59.9 1.9 collective-permute-done.7.refs_3_
  62.1 21.3 %all_to_all.36.sources = bf16[32,136,128]{2,1,0:T(8,128)(2,1)S(1)} all-to-all(bf16[32,136,128]{2,1,0:T(8,128)(2,1)S(1)} %broadcast_in_dim.32), channel_id=1, replica_groups=mesh['row_0'=4,'row_1'=2,'row_2'=4,'col_0'=4,'col_1'=2] {'row_0','row_1'..., dimensions={0} | all-to-all | bytes 2228224 | tf_op jit(solution)/shard_map/all_to_all | solution.py:367
  83.4 1.3 away_products.6
  84.7 1.6 collective-permute-start.8
  86.3 1.2 kept_products.6.kept
  87.8 2.3 %collective-permute-start.9 = (s32[2,72,128]{2,1,0:T(8,128)S(1)}, s32[2,72,128]{2,1,0:T(8,128)S(1)}, u32[]{:S(2)}, u32[]{:S(2)}) collective-permute-start(s32[2,72,128]{2,1,0:T(8,128)S(1)} %get-tuple-element.79), channel_id=1, source_target_pairs={{0,2},{2,4},{4,6},{6,0},{1,7},{3,1},{5,3},{7,5},{8,10},{10,12},{12... | collective-permute-start | bytes 221192 | tf_op jit(solution)/shard_map/ppermute | solution.py:321
  90.1 1.4 collective-permute-start.11
  91.4 1.4 collective-permute-done.9.refs_1_
  92.8 2.4 %collective-permute-start.10 = (s32[72,128]{1,0:T(8,128)S(1)}, s32[72,128]{1,0:T(8,128)S(1)}, u32[]{:S(2)}, u32[]{:S(2)}) collective-permute-start(s32[72,128]{1,0:T(8,128)S(1)} %slice_bitcast_fusion.3), channel_id=1, source_target_pairs={{0,1},{1,0},{2,3},{3,2},{4,5},{5,4},{6,7},{7,6},{8,9},{9,8},{10,11... | collective-permute-start | bytes 110600 | tf_op jit(solution)/shard_map/ppermute | solution.py:314
  95.2 2.0 collective-permute-done.11.refs_3_
  97.4 21.6 %all_to_all.37.sources = bf16[32,136,128]{2,1,0:T(8,128)(2,1)S(1)} all-to-all(bf16[32,136,128]{2,1,0:T(8,128)(2,1)S(1)} %broadcast_in_dim.33), channel_id=1, replica_groups=mesh['row_0'=4,'row_1'=2,'row_2'=4,'col_0'=4,'col_1'=2] {'row_0','row_1'..., dimensions={0} | all-to-all | bytes 2228224 | tf_op jit(solution)/shard_map/all_to_all | solution.py:367
  119.0 1.3 away_products.7
  120.4 1.1 collective-permute-start.12
  121.5 1.2 kept_products.7.kept
  123.7 2.6 %collective-permute-start.15 = (s32[72,128]{1,0:T(8,128)S(1)}, s32[72,128]{1,0:T(8,128)S(1)}, u32[]{:S(2)}, u32[]{:S(2)}) collective-permute-start(s32[72,128]{1,0:T(8,128)S(1)} %get-tuple-element.89), channel_id=1, source_target_pairs={{0,4},{2,6},{4,0},{6,2},{1,5},{3,7},{5,1},{7,3},{8,12},{10,14},{12... | collective-permute-start | bytes 110600 | tf_op jit(solution)/shard_map/ppermute | solution.py:323
  126.3 2.4 %collective-permute-done.13.refs_1_ = s32[2,72,128]{2,1,0:T(8,128)S(1)} collective-permute-done((s32[2,72,128]{2,1,0:T(8,128)S(1)}, s32[2,72,128]{2,1,0:T(8,128)S(1)}, u32[]{:S(2)}, u32[]{:S(2)}) %collective-permute-start.13) | collective-permute-done | bytes 73760 | tf_op jit(solution)/shard_map/ppermute | solution.py:321
  128.7 1.2 collective-permute-start.14
  131.1 21.2 %all_to_all.38.sources = bf16[32,136,128]{2,1,0:T(8,128)(2,1)S(1)} all-to-all(bf16[32,136,128]{2,1,0:T(8,128)(2,1)S(1)} %broadcast_in_dim.34), channel_id=1, replica_groups=mesh['row_0'=4,'row_1'=2,'row_2'=4,'col_0'=4,'col_1'=2] {'row_0','row_1'..., dimensions={0} | all-to-all | bytes 2228224 | tf_op jit(solution)/shard_map/all_to_all | solution.py:367
  152.2 1.3 away_products.8
  153.6 2.4 %collective-permute-start.16 = (f32[4,136,128]{2,1,0:T(8,128)S(1)}, f32[4,136,128]{2,1,0:T(8,128)S(1)}, u32[]{:S(2)}, u32[]{:S(2)}) collective-permute-start(f32[4,136,128]{2,1,0:T(8,128)S(1)} %get-tuple-element.95), channel_id=1, source_target_pairs={{0,1},{1,0},{2,3},{3,2},{4,5},{5,4},{6,7},{7,6},{8,9},{9,8},{10,11... | collective-permute-start | bytes 835592 | tf_op jit(solution)/shard_map/ppermute | solution.py:314
  156.0 1.2 kept_products.8.kept
  157.9 5.5 %collective-permute-start.19 = (s32[72,128]{1,0:T(8,128)S(1)}, s32[72,128]{1,0:T(8,128)S(1)}, u32[]{:S(2)}, u32[]{:S(2)}) collective-permute-start(s32[72,128]{1,0:T(8,128)S(1)} %get-tuple-element.98), channel_id=1, source_target_pairs={{0,4},{2,6},{4,0},{6,2},{1,5},{3,7},{5,1},{7,3},{8,12},{10,14},{12... | collective-permute-start | bytes 110600 | tf_op jit(solution)/shard_map/ppermute | solution.py:323
  163.3 1.0 collective-permute-start.18
  165.4 20.2 %all_to_all.39.sources = bf16[32,136,128]{2,1,0:T(8,128)(2,1)S(1)} all-to-all(bf16[32,136,128]{2,1,0:T(8,128)(2,1)S(1)} %broadcast_in_dim.35), channel_id=1, replica_groups=mesh['row_0'=4,'row_1'=2,'row_2'=4,'col_0'=4,'col_1'=2] {'row_0','row_1'..., dimensions={0} | all-to-all | bytes 2228224 | tf_op jit(solution)/shard_map/all_to_all | solution.py:367
  185.7 1.3 away_products.9
  187.0 3.5 %collective-permute-start.20 = (f32[4,136,128]{2,1,0:T(8,128)S(1)}, f32[4,136,128]{2,1,0:T(8,128)S(1)}, u32[]{:S(2)}, u32[]{:S(2)}) collective-permute-start(f32[4,136,128]{2,1,0:T(8,128)S(1)} %get-tuple-element.104), channel_id=1, source_target_pairs={{0,1},{1,0},{2,3},{3,2},{4,5},{5,4},{6,7},{7,6},{8,9},{9,8},{10,11... | collective-permute-start | bytes 835592 | tf_op jit(solution)/shard_map/ppermute | solution.py:314
  190.5 1.2 kept_products.9.kept
  192.0 2.0 collective-permute-start.21
  194.0 3.3 %collective-permute-start.23 = (s32[72,128]{1,0:T(8,128)S(1)}, s32[72,128]{1,0:T(8,128)S(1)}, u32[]{:S(2)}, u32[]{:S(2)}) collective-permute-start(s32[72,128]{1,0:T(8,128)S(1)} %get-tuple-element.107), channel_id=1, source_target_pairs={{0,4},{2,6},{4,0},{6,2},{1,5},{3,7},{5,1},{7,3},{8,12},{10,14},{12... | collective-permute-start | bytes 110600 | tf_op jit(solution)/shard_map/ppermute | solution.py:323
  197.4 1.9 collective-permute-start.22
  199.3 2.6 %collective-permute-done.23.refs_3_ = s32[72,128]{1,0:T(8,128)S(1)} collective-permute-done((s32[72,128]{1,0:T(8,128)S(1)}, s32[72,128]{1,0:T(8,128)S(1)}, u32[]{:S(2)}, u32[]{:S(2)}) %collective-permute-start.23) | collective-permute-done | bytes 36896 | tf_op jit(solution)/shard_map/ppermute | solution.py:323
  202.0 12.8 %all_to_all.40 = f32[16,8,128]{2,1,0:T(8,128)S(1)} all-to-all(f32[16,8,128]{2,1,0:T(8,128)S(1)} %broadcast_in_dim.36), channel_id=1, replica_groups=mesh['row_0'=4,'row_1'=2,'row_2'=4,'col_0'=4,'col_1'=2] {'row_1','col_0'..., dimensions={0} | all-to-all | bytes 131072 | tf_op jit(solution)/shard_map/all_to_all | solution.py:329
  214.8 9.3 %all_to_all.41.squares = f32[16,8,128]{2,1,0:T(8,128)S(1)} all-to-all(f32[16,8,128]{2,1,0:T(8,128)S(1)} %broadcast_in_dim.37), channel_id=1, replica_groups=mesh['row_0'=4,'row_1'=2,'row_2'=4,'col_0'=4,'col_1'=2] {'row_0','row_2'}, dimensions={0} | all-to-all | bytes 131072 | tf_op jit(solution)/shard_map/all_to_all | solution.py:329
  (50 shorter events, 6.5 us)
Async XLA Ops:
  1.3 22.5 %copy-start = (s32[1,128]{1,0:T(1,128)S(1)}, s32[1,128]{1,0:T(1,128)}, u32[]{:S(2)}) copy-start(s32[1,128]{1,0:T(1,128)} %refs_4_.9) | copy-start | bytes 1540
  6.1 4.5 %collective-permute-start = (f32[4,136,128]{2,1,0:T(8,128)S(1)}, f32[4,136,128]{2,1,0:T(8,128)S(1)}, u32[]{:S(2)}, u32[]{:S(2)}) collective-permute-start(f32[4,136,128]{2,1,0:T(8,128)S(1)} %get-tuple-element.62), channel_id=1, source_target_pairs={{0,1},{1,0},{2,3},{3,2},{4,5},{5,4},{6,7},{7,6},{8,9},{9,8},{10,11... | collective-permute-start | bytes 835592 | tf_op jit(solution)/shard_map/ppermute | solution.py:314
  10.8 6.5 %collective-permute-start.1 = (s32[2,72,128]{2,1,0:T(8,128)S(1)}, s32[2,72,128]{2,1,0:T(8,128)S(1)}, u32[]{:S(2)}, u32[]{:S(2)}) collective-permute-start(s32[2,72,128]{2,1,0:T(8,128)S(1)} %get-tuple-element.64), channel_id=1, source_target_pairs={{0,2},{2,4},{4,6},{6,0},{1,7},{3,1},{5,3},{7,5},{8,10},{10,12},{12... | collective-permute-start | bytes 221192 | tf_op jit(solution)/shard_map/ppermute | solution.py:321
  15.9 7.9 %collective-permute-start.3 = (s32[72,128]{1,0:T(8,128)S(1)}, s32[72,128]{1,0:T(8,128)S(1)}, u32[]{:S(2)}, u32[]{:S(2)}) collective-permute-start(s32[72,128]{1,0:T(8,128)S(1)} %get-tuple-element.65), channel_id=1, source_target_pairs={{0,4},{2,6},{4,0},{6,2},{1,5},{3,7},{5,1},{7,3},{8,12},{10,14},{12... | collective-permute-start | bytes 110600 | tf_op jit(solution)/shard_map/ppermute | solution.py:323
  17.3 6.5 %collective-permute-start.2 = (s32[72,128]{1,0:T(8,128)S(1)}, s32[72,128]{1,0:T(8,128)S(1)}, u32[]{:S(2)}, u32[]{:S(2)}) collective-permute-start(s32[72,128]{1,0:T(8,128)S(1)} %slice_bitcast_fusion.5), channel_id=1, source_target_pairs={{0,1},{1,0},{2,3},{3,2},{4,5},{5,4},{6,7},{7,6},{8,9},{9,8},{10,11... | collective-permute-start | bytes 110600 | tf_op jit(solution)/shard_map/ppermute | solution.py:314
  49.8 2.8 %collective-permute-start.4 = (f32[4,136,128]{2,1,0:T(8,128)S(1)}, f32[4,136,128]{2,1,0:T(8,128)S(1)}, u32[]{:S(2)}, u32[]{:S(2)}) collective-permute-start(f32[4,136,128]{2,1,0:T(8,128)S(1)} %get-tuple-element.69), channel_id=1, source_target_pairs={{0,1},{1,0},{2,3},{3,2},{4,5},{5,4},{6,7},{7,6},{8,9},{9,8},{10,11... | collective-permute-start | bytes 835592 | tf_op jit(solution)/shard_map/ppermute | solution.py:314
  51.4 10.4 %copy-start.1 = (s32[128]{0:T(128)S(1)}, s32[128]{0:T(128)}, u32[]{:S(2)}) copy-start(s32[128]{0:T(128)} %param.11) | copy-start | bytes 1540
  52.9 5.0 %collective-permute-start.5 = (s32[2,72,128]{2,1,0:T(8,128)S(1)}, s32[2,72,128]{2,1,0:T(8,128)S(1)}, u32[]{:S(2)}, u32[]{:S(2)}) collective-permute-start(s32[2,72,128]{2,1,0:T(8,128)S(1)} %get-tuple-element.71), channel_id=1, source_target_pairs={{0,2},{2,4},{4,6},{6,0},{1,7},{3,1},{5,3},{7,5},{8,10},{10,12},{12... | collective-permute-start | bytes 221192 | tf_op jit(solution)/shard_map/ppermute | solution.py:321
  54.7 7.1 %collective-permute-start.7 = (s32[72,128]{1,0:T(8,128)S(1)}, s32[72,128]{1,0:T(8,128)S(1)}, u32[]{:S(2)}, u32[]{:S(2)}) collective-permute-start(s32[72,128]{1,0:T(8,128)S(1)} %get-tuple-element.72), channel_id=1, source_target_pairs={{0,4},{2,6},{4,0},{6,2},{1,5},{3,7},{5,1},{7,3},{8,12},{10,14},{12... | collective-permute-start | bytes 110600 | tf_op jit(solution)/shard_map/ppermute | solution.py:323
  57.9 3.9 %collective-permute-start.6 = (s32[72,128]{1,0:T(8,128)S(1)}, s32[72,128]{1,0:T(8,128)S(1)}, u32[]{:S(2)}, u32[]{:S(2)}) collective-permute-start(s32[72,128]{1,0:T(8,128)S(1)} %slice_bitcast_fusion.4), channel_id=1, source_target_pairs={{0,1},{1,0},{2,3},{3,2},{4,5},{5,4},{6,7},{7,6},{8,9},{9,8},{10,11... | collective-permute-start | bytes 110600 | tf_op jit(solution)/shard_map/ppermute | solution.py:314
  84.7 2.8 %collective-permute-start.8 = (f32[4,136,128]{2,1,0:T(8,128)S(1)}, f32[4,136,128]{2,1,0:T(8,128)S(1)}, u32[]{:S(2)}, u32[]{:S(2)}) collective-permute-start(f32[4,136,128]{2,1,0:T(8,128)S(1)} %get-tuple-element.77), channel_id=1, source_target_pairs={{0,1},{1,0},{2,3},{3,2},{4,5},{5,4},{6,7},{7,6},{8,9},{9,8},{10,11... | collective-permute-start | bytes 835592 | tf_op jit(solution)/shard_map/ppermute | solution.py:314
  87.8 5.0 %collective-permute-start.9 = (s32[2,72,128]{2,1,0:T(8,128)S(1)}, s32[2,72,128]{2,1,0:T(8,128)S(1)}, u32[]{:S(2)}, u32[]{:S(2)}) collective-permute-start(s32[2,72,128]{2,1,0:T(8,128)S(1)} %get-tuple-element.79), channel_id=1, source_target_pairs={{0,2},{2,4},{4,6},{6,0},{1,7},{3,1},{5,3},{7,5},{8,10},{10,12},{12... | collective-permute-start | bytes 221192 | tf_op jit(solution)/shard_map/ppermute | solution.py:321
  90.1 7.1 %collective-permute-start.11 = (s32[72,128]{1,0:T(8,128)S(1)}, s32[72,128]{1,0:T(8,128)S(1)}, u32[]{:S(2)}, u32[]{:S(2)}) collective-permute-start(s32[72,128]{1,0:T(8,128)S(1)} %get-tuple-element.80), channel_id=1, source_target_pairs={{0,4},{2,6},{4,0},{6,2},{1,5},{3,7},{5,1},{7,3},{8,12},{10,14},{12... | collective-permute-start | bytes 110600 | tf_op jit(solution)/shard_map/ppermute | solution.py:323
  92.8 4.4 %collective-permute-start.10 = (s32[72,128]{1,0:T(8,128)S(1)}, s32[72,128]{1,0:T(8,128)S(1)}, u32[]{:S(2)}, u32[]{:S(2)}) collective-permute-start(s32[72,128]{1,0:T(8,128)S(1)} %slice_bitcast_fusion.3), channel_id=1, source_target_pairs={{0,1},{1,0},{2,3},{3,2},{4,5},{5,4},{6,7},{7,6},{8,9},{9,8},{10,11... | collective-permute-start | bytes 110600 | tf_op jit(solution)/shard_map/ppermute | solution.py:314
  120.4 2.4 %collective-permute-start.12 = (f32[4,136,128]{2,1,0:T(8,128)S(1)}, f32[4,136,128]{2,1,0:T(8,128)S(1)}, u32[]{:S(2)}, u32[]{:S(2)}) collective-permute-start(f32[4,136,128]{2,1,0:T(8,128)S(1)} %get-tuple-element.86), channel_id=1, source_target_pairs={{0,1},{1,0},{2,3},{3,2},{4,5},{5,4},{6,7},{7,6},{8,9},{9,8},{10,11... | collective-permute-start | bytes 835592 | tf_op jit(solution)/shard_map/ppermute | solution.py:314
  123.0 5.7 %collective-permute-start.13 = (s32[2,72,128]{2,1,0:T(8,128)S(1)}, s32[2,72,128]{2,1,0:T(8,128)S(1)}, u32[]{:S(2)}, u32[]{:S(2)}) collective-permute-start(s32[2,72,128]{2,1,0:T(8,128)S(1)} %get-tuple-element.88), channel_id=1, source_target_pairs={{0,2},{2,4},{4,6},{6,0},{1,7},{3,1},{5,3},{7,5},{8,10},{10,12},{12... | collective-permute-start | bytes 221192 | tf_op jit(solution)/shard_map/ppermute | solution.py:321
  123.7 7.1 %collective-permute-start.15 = (s32[72,128]{1,0:T(8,128)S(1)}, s32[72,128]{1,0:T(8,128)S(1)}, u32[]{:S(2)}, u32[]{:S(2)}) collective-permute-start(s32[72,128]{1,0:T(8,128)S(1)} %get-tuple-element.89), channel_id=1, source_target_pairs={{0,4},{2,6},{4,0},{6,2},{1,5},{3,7},{5,1},{7,3},{8,12},{10,14},{12... | collective-permute-start | bytes 110600 | tf_op jit(solution)/shard_map/ppermute | solution.py:323
  128.7 2.1 collective-permute-start.14
  153.6 3.6 %collective-permute-start.16 = (f32[4,136,128]{2,1,0:T(8,128)S(1)}, f32[4,136,128]{2,1,0:T(8,128)S(1)}, u32[]{:S(2)}, u32[]{:S(2)}) collective-permute-start(f32[4,136,128]{2,1,0:T(8,128)S(1)} %get-tuple-element.95), channel_id=1, source_target_pairs={{0,1},{1,0},{2,3},{3,2},{4,5},{5,4},{6,7},{7,6},{8,9},{9,8},{10,11... | collective-permute-start | bytes 835592 | tf_op jit(solution)/shard_map/ppermute | solution.py:314
  157.5 5.9 %collective-permute-start.17 = (s32[2,72,128]{2,1,0:T(8,128)S(1)}, s32[2,72,128]{2,1,0:T(8,128)S(1)}, u32[]{:S(2)}, u32[]{:S(2)}) collective-permute-start(s32[2,72,128]{2,1,0:T(8,128)S(1)} %get-tuple-element.97), channel_id=1, source_target_pairs={{0,2},{2,4},{4,6},{6,0},{1,7},{3,1},{5,3},{7,5},{8,10},{10,12},{12... | collective-permute-start | bytes 221192 | tf_op jit(solution)/shard_map/ppermute | solution.py:321
  157.9 6.8 %collective-permute-start.19 = (s32[72,128]{1,0:T(8,128)S(1)}, s32[72,128]{1,0:T(8,128)S(1)}, u32[]{:S(2)}, u32[]{:S(2)}) collective-permute-start(s32[72,128]{1,0:T(8,128)S(1)} %get-tuple-element.98), channel_id=1, source_target_pairs={{0,4},{2,6},{4,0},{6,2},{1,5},{3,7},{5,1},{7,3},{8,12},{10,14},{12... | collective-permute-start | bytes 110600 | tf_op jit(solution)/shard_map/ppermute | solution.py:323
  163.3 1.8 collective-permute-start.18
  187.0 4.7 %collective-permute-start.20 = (f32[4,136,128]{2,1,0:T(8,128)S(1)}, f32[4,136,128]{2,1,0:T(8,128)S(1)}, u32[]{:S(2)}, u32[]{:S(2)}) collective-permute-start(f32[4,136,128]{2,1,0:T(8,128)S(1)} %get-tuple-element.104), channel_id=1, source_target_pairs={{0,1},{1,0},{2,3},{3,2},{4,5},{5,4},{6,7},{7,6},{8,9},{9,8},{10,11... | collective-permute-start | bytes 835592 | tf_op jit(solution)/shard_map/ppermute | solution.py:314
  192.0 5.4 %collective-permute-start.21 = (s32[2,72,128]{2,1,0:T(8,128)S(1)}, s32[2,72,128]{2,1,0:T(8,128)S(1)}, u32[]{:S(2)}, u32[]{:S(2)}) collective-permute-start(s32[2,72,128]{2,1,0:T(8,128)S(1)} %get-tuple-element.106), channel_id=1, source_target_pairs={{0,2},{2,4},{4,6},{6,0},{1,7},{3,1},{5,3},{7,5},{8,10},{10,12},{12... | collective-permute-start | bytes 221192 | tf_op jit(solution)/shard_map/ppermute | solution.py:321
  194.0 7.8 %collective-permute-start.23 = (s32[72,128]{1,0:T(8,128)S(1)}, s32[72,128]{1,0:T(8,128)S(1)}, u32[]{:S(2)}, u32[]{:S(2)}) collective-permute-start(s32[72,128]{1,0:T(8,128)S(1)} %get-tuple-element.107), channel_id=1, source_target_pairs={{0,4},{2,6},{4,0},{6,2},{1,5},{3,7},{5,1},{7,3},{8,12},{10,14},{12... | collective-permute-start | bytes 110600 | tf_op jit(solution)/shard_map/ppermute | solution.py:323
  197.4 4.5 %collective-permute-start.22 = (s32[72,128]{1,0:T(8,128)S(1)}, s32[72,128]{1,0:T(8,128)S(1)}, u32[]{:S(2)}, u32[]{:S(2)}) collective-permute-start(s32[72,128]{1,0:T(8,128)S(1)} %slice_bitcast_fusion), channel_id=1, source_target_pairs={{0,1},{1,0},{2,3},{3,2},{4,5},{5,4},{6,7},{7,6},{8,9},{9,8},{10,11... | collective-permute-start | bytes 110600 | tf_op jit(solution)/shard_map/ppermute | solution.py:314

commit v6 on v5

--- a/solution.py
+++ b/solution.py
@@ -5,6 +5,7 @@
 from jax.experimental.pallas import tpu as pltpu
 from jax.sharding import Mesh
 from jax.sharding import PartitionSpec as P
+
 
 TILE = 128
 PANEL = 128
@@ -268,19 +269,19 @@
     return jnp.where(vertex == jnp.broadcast_to(ids[...], (TILE, PANEL)), 1.0, 0.0)
 
 
-def first_level_kernel(own, heard, handed, far, depth, raw, out):
-    product, _ = decoded((own, heard.at[0], handed, far))
+def first_level_kernel(own, far, heard, handed, depth, raw, out):
+    product, _ = decoded((own, far, heard.at[0], handed))
     paths = jnp.where(depth[...] >= 1, product, 0.0)
     raw[...] = paths
     outgoing(paths, out)
 
 
-def level_kernel(level, own, heard, handed, far, depth, raw_in, sums_in, raw, out, sums, scale):
+def level_kernel(level, own, far, heard, handed, depth, raw_in, sums_in, raw, out, sums, scale):
     before = start_piece(sums_in) if level == 2 else sums_in[...]
-    product, shares = decoded((own, heard.at[0], handed, far))
+    product, shares = decoded((own, far, heard.at[0], handed))
     mean_square = jnp.zeros((1, PANEL), jnp.float32)
     turned = 2 * lax.axis_index("col_1")
-    back = (0, 1 + turned, 3 - turned, 2)
+    back = (0, 2, 1 + turned, 3 - turned)
     for j in range(4):
         for k, share in zip(back, shares):
             here = ((lax.axis_index("col_0") - j) & 3) == k
@@ -306,7 +307,6 @@
         out_specs=[VMEM] * len(shapes),
         out_shape=shapes,
         compiler_params=LIMIT,
-        name=f"level_{level}",
     )(*chunks, depth, *(() if first else (raw, sums)))
 
 
@@ -316,12 +316,11 @@
 
 def exchanged(kept, away):
     beside, far, own = encoded(kept, from_partner(away))
+    far = lax.ppermute(far, "col_0", [(i, (i + 2) % 4) for i in range(4)])
     forward = [(2 * i, 2 * ((i + 1) % 4)) for i in range(4)]
     backward = [(2 * i + 1, 2 * ((i - 1) % 4) + 1) for i in range(4)]
     heard = lax.ppermute(beside, COL, forward + backward)
-    handed = from_partner(heard[1])
-    far = lax.ppermute(far, "col_0", [(i, (i + 2) % 4) for i in range(4)])
-    return own, heard, handed, far
+    return own, far, heard, from_partner(heard[1])
 
 
 def everywhere(line, axes):

time: 225 us -> 224 us (level)
  transfers between devices with their start and end apart: 24 -> 24, of which waited for: 12 -> 13; matrix products, arithmetic and copies ran while one was open for 0% -> 0% of each run, Pallas kernels for 3% -> 3%
where the time goes in v6:
time: 224 us
  blocking collectives  132 us (59%)
  starting transfers between devices  49.9 us (22%)
  Pallas kernels  20 us (9%)
  waiting for transfers between devices  19.8 us (9%)
    all_to_all x5, blocking collectives, local(): sources = lax.all_to_all(spread, ROW, 0, 0, tiled=True)  109 us
    ppermute x12, starting transfers between devices, from_partner(): return lax.ppermute(x, 'col_1', [(0, 1), (1, 0)])  24.5 us
    all_to_all x2, blocking collectives, everywhere(): return lax.all_to_all(copies, axes, 0, 0, tiled=True)  22.9 us
    ppermute x6, starting transfers between devices, exchanged(): far = lax.ppermute(far, 'col_0', [(i, (i + 2) % 4) for i in range(4)])  13.5 us
    ppermute x6, waiting for transfers between devices, exchanged(): far = lax.ppermute(far, 'col_0', [(i, (i + 2) % 4) for i in range(4)])  12.2 us
    ppermute x6, starting transfers between devices, exchanged(): heard = lax.ppermute(beside, COL, forward + backward)  11.9 us
    pallas_call x5, Pallas kernels, away_products(): pl.pallas_call(away_kernel, in_specs=[VMEM, VMEM], out_specs=[VMEM] * 3,...  6.65 us
    ppermute x6, waiting for transfers between devices, exchanged(): heard = lax.ppermute(beside, COL, forward + backward)  6.36 us
  transfers between devices with their start and end apart: 24, of which 13 were waited for; matrix products, arithmetic and copies ran while one was open for 0% of the time, Pallas kernels for 3%

profile of v6, /device:TPU:1, one launch (start us, length us, event | category | flops | bytes accessed | tf_op | source)
XLA Modules:
  0.0 223.7 jit_solution(7946317133652337694)
XLA Ops:
  1.3 4.3 %first_products.1 = (f32[4,136,128]{2,1,0:T(8,128)S(1)}, f32[4,136,128]{2,1,0:T(8,128)S(1)}, bf16[1024,4096]{1,0:T(8,128)(2,1)S(1)}) custom-call(s32[1,1]{1,0:T(1,128)S(6)} %copy.9.count, s32[128]{0:T(128)} %bitcast.23, s32[128]{0:T(128)} %bitcast.24, s32[1,128]{1,0:T(1,128)} %bitcast.18, bf16[128,128,128]{2,1,0:T(8,128)(2,1)} %bitcast.21), custom_call_target="tpu_custom_call" | custom-call | tf_op jit(solution)/shard_map/first_products/pallas_call | solution.py:125
  5.6 3.4 %collective-permute-start = (f32[4,136,128]{2,1,0:T(8,128)S(1)}, f32[4,136,128]{2,1,0:T(8,128)S(1)}, u32[]{:S(2)}, u32[]{:S(2)}) collective-permute-start(f32[4,136,128]{2,1,0:T(8,128)S(1)} %get-tuple-element.62), channel_id=1, source_target_pairs={{0,1},{1,0},{2,3},{3,2},{4,5},{5,4},{6,7},{7,6},{8,9},{9,8},{10,11... | collective-permute-start | bytes 835592 | tf_op jit(solution)/shard_map/ppermute | solution.py:314
  9.1 1.2 collective-permute-done.away
  10.5 4.7 %collective-permute-start.2 = (s32[2,72,128]{2,1,0:T(8,128)S(1)}, s32[2,72,128]{2,1,0:T(8,128)S(1)}, u32[]{:S(2)}, u32[]{:S(2)}) collective-permute-start(s32[2,72,128]{2,1,0:T(8,128)S(1)} %get-tuple-element.65), channel_id=1, source_target_pairs={{0,2},{2,4},{4,6},{6,0},{1,7},{3,1},{5,3},{7,5},{8,10},{10,12},{12... | collective-permute-start | bytes 221192 | tf_op jit(solution)/shard_map/ppermute | solution.py:322
  17.3 1.2 collective-permute-start.3
  18.4 3.5 %collective-permute-done.1.far = s32[72,128]{1,0:T(8,128)S(1)} collective-permute-done((s32[72,128]{1,0:T(8,128)S(1)}, s32[72,128]{1,0:T(8,128)S(1)}, u32[]{:S(2)}, u32[]{:S(2)}) %collective-permute-start.1) | collective-permute-done | bytes 36896 | tf_op jit(solution)/shard_map/ppermute | solution.py:319
  22.2 26.4 %all_to_all.35.sources = bf16[32,136,128]{2,1,0:T(8,128)(2,1)S(1)} all-to-all(bf16[32,136,128]{2,1,0:T(8,128)(2,1)S(1)} %broadcast_in_dim.31), channel_id=1, replica_groups=mesh['row_0'=4,'row_1'=2,'row_2'=4,'col_0'=4,'col_1'=2] {'row_0','row_1'..., dimensions={0} | all-to-all | bytes 2228224 | tf_op jit(solution)/shard_map/all_to_all | solution.py:366
  48.5 1.3 away_products.5
  49.9 1.5 collective-permute-start.4
  51.4 1.2 kept_products.5.kept
  54.0 1.8 collective-permute-start.5
  55.8 2.2 collective-permute-done.6.refs_2_
  58.0 1.8 collective-permute-start.7
  59.7 1.9 collective-permute-done.5.refs_1_
  61.9 20.7 %all_to_all.36.sources = bf16[32,136,128]{2,1,0:T(8,128)(2,1)S(1)} all-to-all(bf16[32,136,128]{2,1,0:T(8,128)(2,1)S(1)} %broadcast_in_dim.32), channel_id=1, replica_groups=mesh['row_0'=4,'row_1'=2,'row_2'=4,'col_0'=4,'col_1'=2] {'row_0','row_1'..., dimensions={0} | all-to-all | bytes 2228224 | tf_op jit(solution)/shard_map/all_to_all | solution.py:366
  82.7 1.3 away_products.6
  84.0 2.0 collective-permute-start.8
  86.0 1.2 kept_products.6.kept
  87.5 1.3 collective-permute-start.10
  88.8 3.0 %collective-permute-start.9 = (s32[72,128]{1,0:T(8,128)S(1)}, s32[72,128]{1,0:T(8,128)S(1)}, u32[]{:S(2)}, u32[]{:S(2)}) collective-permute-start(s32[72,128]{1,0:T(8,128)S(1)} %get-tuple-element.79), channel_id=1, source_target_pairs={{0,4},{2,6},{4,0},{6,2},{1,5},{3,7},{5,1},{7,3},{8,12},{10,14},{12... | collective-permute-start | bytes 110600 | tf_op jit(solution)/shard_map/ppermute | solution.py:319
  92.5 1.9 collective-permute-start.11
  95.8 20.1 %all_to_all.37.sources = bf16[32,136,128]{2,1,0:T(8,128)(2,1)S(1)} all-to-all(bf16[32,136,128]{2,1,0:T(8,128)(2,1)S(1)} %broadcast_in_dim.33), channel_id=1, replica_groups=mesh['row_0'=4,'row_1'=2,'row_2'=4,'col_0'=4,'col_1'=2] {'row_0','row_1'..., dimensions={0} | all-to-all | bytes 2228224 | tf_op jit(solution)/shard_map/all_to_all | solution.py:366
  115.9 1.3 away_products.7
  117.2 2.7 %collective-permute-start.12 = (f32[4,136,128]{2,1,0:T(8,128)S(1)}, f32[4,136,128]{2,1,0:T(8,128)S(1)}, u32[]{:S(2)}, u32[]{:S(2)}) collective-permute-start(f32[4,136,128]{2,1,0:T(8,128)S(1)} %get-tuple-element.86), channel_id=1, source_target_pairs={{0,1},{1,0},{2,3},{3,2},{4,5},{5,4},{6,7},{7,6},{8,9},{9,8},{10,11... | collective-permute-start | bytes 835592 | tf_op jit(solution)/shard_map/ppermute | solution.py:314
  119.9 1.2 kept_products.7.kept
  121.4 1.7 collective-permute-start.14
  123.2 3.1 %collective-permute-start.13 = (s32[72,128]{1,0:T(8,128)S(1)}, s32[72,128]{1,0:T(8,128)S(1)}, u32[]{:S(2)}, u32[]{:S(2)}) collective-permute-start(s32[72,128]{1,0:T(8,128)S(1)} %get-tuple-element.88), channel_id=1, source_target_pairs={{0,4},{2,6},{4,0},{6,2},{1,5},{3,7},{5,1},{7,3},{8,12},{10,14},{12... | collective-permute-start | bytes 110600 | tf_op jit(solution)/shard_map/ppermute | solution.py:319
  126.4 1.9 collective-permute-start.15
  128.3 2.8 %collective-permute-done.13.refs_1_ = s32[72,128]{1,0:T(8,128)S(1)} collective-permute-done((s32[72,128]{1,0:T(8,128)S(1)}, s32[72,128]{1,0:T(8,128)S(1)}, u32[]{:S(2)}, u32[]{:S(2)}) %collective-permute-start.13) | collective-permute-done | bytes 36896 | tf_op jit(solution)/shard_map/ppermute | solution.py:319
  131.4 20.8 %all_to_all.38.sources = bf16[32,136,128]{2,1,0:T(8,128)(2,1)S(1)} all-to-all(bf16[32,136,128]{2,1,0:T(8,128)(2,1)S(1)} %broadcast_in_dim.34), channel_id=1, replica_groups=mesh['row_0'=4,'row_1'=2,'row_2'=4,'col_0'=4,'col_1'=2] {'row_0','row_1'..., dimensions={0} | all-to-all | bytes 2228224 | tf_op jit(solution)/shard_map/all_to_all | solution.py:366
  152.2 1.3 away_products.8
  153.5 2.4 %collective-permute-start.16 = (f32[4,136,128]{2,1,0:T(8,128)S(1)}, f32[4,136,128]{2,1,0:T(8,128)S(1)}, u32[]{:S(2)}, u32[]{:S(2)}) collective-permute-start(f32[4,136,128]{2,1,0:T(8,128)S(1)} %get-tuple-element.95), channel_id=1, source_target_pairs={{0,1},{1,0},{2,3},{3,2},{4,5},{5,4},{6,7},{7,6},{8,9},{9,8},{10,11... | collective-permute-start | bytes 835592 | tf_op jit(solution)/shard_map/ppermute | solution.py:314
  155.9 1.2 kept_products.8.kept
  157.4 1.7 collective-permute-start.18
  159.1 1.5 collective-permute-start.17
  160.6 1.8 collective-permute-done.18.refs_2_
  162.4 1.9 collective-permute-start.19
  164.3 1.6 collective-permute-done.17.refs_1_
  166.1 20.9 %all_to_all.39.sources = bf16[32,136,128]{2,1,0:T(8,128)(2,1)S(1)} all-to-all(bf16[32,136,128]{2,1,0:T(8,128)(2,1)S(1)} %broadcast_in_dim.35), channel_id=1, replica_groups=mesh['row_0'=4,'row_1'=2,'row_2'=4,'col_0'=4,'col_1'=2] {'row_0','row_1'..., dimensions={0} | all-to-all | bytes 2228224 | tf_op jit(solution)/shard_map/all_to_all | solution.py:366
  187.0 1.3 away_products.9
  188.4 2.0 collective-permute-start.20
  190.3 1.2 kept_products.9.kept
  191.8 1.5 collective-permute-start.22
  193.3 3.1 %collective-permute-start.21 = (s32[72,128]{1,0:T(8,128)S(1)}, s32[72,128]{1,0:T(8,128)S(1)}, u32[]{:S(2)}, u32[]{:S(2)}) collective-permute-start(s32[72,128]{1,0:T(8,128)S(1)} %get-tuple-element.106), channel_id=1, source_target_pairs={{0,4},{2,6},{4,0},{6,2},{1,5},{3,7},{5,1},{7,3},{8,12},{10,14},{12... | collective-permute-start | bytes 110600 | tf_op jit(solution)/shard_map/ppermute | solution.py:319
  196.8 1.9 collective-permute-start.23
  198.7 1.3 collective-permute-done.21.refs_1_
  200.1 13.7 %all_to_all.40 = f32[16,8,128]{2,1,0:T(8,128)S(1)} all-to-all(f32[16,8,128]{2,1,0:T(8,128)S(1)} %broadcast_in_dim.36), channel_id=1, replica_groups=mesh['row_0'=4,'row_1'=2,'row_2'=4,'col_0'=4,'col_1'=2] {'row_1','col_0'..., dimensions={0} | all-to-all | bytes 131072 | tf_op jit(solution)/shard_map/all_to_all | solution.py:328
  213.9 9.2 %all_to_all.41.squares = f32[16,8,128]{2,1,0:T(8,128)S(1)} all-to-all(f32[16,8,128]{2,1,0:T(8,128)S(1)} %broadcast_in_dim.37), channel_id=1, replica_groups=mesh['row_0'=4,'row_1'=2,'row_2'=4,'col_0'=4,'col_1'=2] {'row_0','row_2'}, dimensions={0} | all-to-all | bytes 131072 | tf_op jit(solution)/shard_map/all_to_all | solution.py:328
  (50 shorter events, 9.1 us)
Async XLA Ops:
  1.3 20.6 %copy-start = (s32[1,128]{1,0:T(1,128)S(1)}, s32[1,128]{1,0:T(1,128)}, u32[]{:S(2)}) copy-start(s32[1,128]{1,0:T(1,128)} %refs_4_.9) | copy-start | bytes 1540
  5.6 4.6 %collective-permute-start = (f32[4,136,128]{2,1,0:T(8,128)S(1)}, f32[4,136,128]{2,1,0:T(8,128)S(1)}, u32[]{:S(2)}, u32[]{:S(2)}) collective-permute-start(f32[4,136,128]{2,1,0:T(8,128)S(1)} %get-tuple-element.62), channel_id=1, source_target_pairs={{0,1},{1,0},{2,3},{3,2},{4,5},{5,4},{6,7},{7,6},{8,9},{9,8},{10,11... | collective-permute-start | bytes 835592 | tf_op jit(solution)/shard_map/ppermute | solution.py:314
  10.5 6.8 %collective-permute-start.2 = (s32[2,72,128]{2,1,0:T(8,128)S(1)}, s32[2,72,128]{2,1,0:T(8,128)S(1)}, u32[]{:S(2)}, u32[]{:S(2)}) collective-permute-start(s32[2,72,128]{2,1,0:T(8,128)S(1)} %get-tuple-element.65), channel_id=1, source_target_pairs={{0,2},{2,4},{4,6},{6,0},{1,7},{3,1},{5,3},{7,5},{8,10},{10,12},{12... | collective-permute-start | bytes 221192 | tf_op jit(solution)/shard_map/ppermute | solution.py:322
  15.2 6.7 %collective-permute-start.1 = (s32[72,128]{1,0:T(8,128)S(1)}, s32[72,128]{1,0:T(8,128)S(1)}, u32[]{:S(2)}, u32[]{:S(2)}) collective-permute-start(s32[72,128]{1,0:T(8,128)S(1)} %get-tuple-element.64), channel_id=1, source_target_pairs={{0,4},{2,6},{4,0},{6,2},{1,5},{3,7},{5,1},{7,3},{8,12},{10,14},{12... | collective-permute-start | bytes 110600 | tf_op jit(solution)/shard_map/ppermute | solution.py:319
  17.3 4.6 %collective-permute-start.3 = (s32[72,128]{1,0:T(8,128)S(1)}, s32[72,128]{1,0:T(8,128)S(1)}, u32[]{:S(2)}, u32[]{:S(2)}) collective-permute-start(s32[72,128]{1,0:T(8,128)S(1)} %slice_bitcast_fusion.5), channel_id=1, source_target_pairs={{0,1},{1,0},{2,3},{3,2},{4,5},{5,4},{6,7},{7,6},{8,9},{9,8},{10,11... | collective-permute-start | bytes 110600 | tf_op jit(solution)/shard_map/ppermute | solution.py:314
  49.9 2.8 %collective-permute-start.4 = (f32[4,136,128]{2,1,0:T(8,128)S(1)}, f32[4,136,128]{2,1,0:T(8,128)S(1)}, u32[]{:S(2)}, u32[]{:S(2)}) collective-permute-start(f32[4,136,128]{2,1,0:T(8,128)S(1)} %get-tuple-element.69), channel_id=1, source_target_pairs={{0,1},{1,0},{2,3},{3,2},{4,5},{5,4},{6,7},{7,6},{8,9},{9,8},{10,11... | collective-permute-start | bytes 835592 | tf_op jit(solution)/shard_map/ppermute | solution.py:314
  51.4 10.3 %copy-start.1 = (s32[128]{0:T(128)S(1)}, s32[128]{0:T(128)}, u32[]{:S(2)}) copy-start(s32[128]{0:T(128)} %param.11) | copy-start | bytes 1540
  52.9 5.1 %collective-permute-start.6 = (s32[2,72,128]{2,1,0:T(8,128)S(1)}, s32[2,72,128]{2,1,0:T(8,128)S(1)}, u32[]{:S(2)}, u32[]{:S(2)}) collective-permute-start(s32[2,72,128]{2,1,0:T(8,128)S(1)} %get-tuple-element.72), channel_id=1, source_target_pairs={{0,2},{2,4},{4,6},{6,0},{1,7},{3,1},{5,3},{7,5},{8,10},{10,12},{12... | collective-permute-start | bytes 221192 | tf_op jit(solution)/shard_map/ppermute | solution.py:322
  54.0 7.7 %collective-permute-start.5 = (s32[72,128]{1,0:T(8,128)S(1)}, s32[72,128]{1,0:T(8,128)S(1)}, u32[]{:S(2)}, u32[]{:S(2)}) collective-permute-start(s32[72,128]{1,0:T(8,128)S(1)} %get-tuple-element.71), channel_id=1, source_target_pairs={{0,4},{2,6},{4,0},{6,2},{1,5},{3,7},{5,1},{7,3},{8,12},{10,14},{12... | collective-permute-start | bytes 110600 | tf_op jit(solution)/shard_map/ppermute | solution.py:319
  58.0 3.7 %collective-permute-start.7 = (s32[72,128]{1,0:T(8,128)S(1)}, s32[72,128]{1,0:T(8,128)S(1)}, u32[]{:S(2)}, u32[]{:S(2)}) collective-permute-start(s32[72,128]{1,0:T(8,128)S(1)} %slice_bitcast_fusion.4), channel_id=1, source_target_pairs={{0,1},{1,0},{2,3},{3,2},{4,5},{5,4},{6,7},{7,6},{8,9},{9,8},{10,11... | collective-permute-start | bytes 110600 | tf_op jit(solution)/shard_map/ppermute | solution.py:314
  84.0 3.3 %collective-permute-start.8 = (f32[4,136,128]{2,1,0:T(8,128)S(1)}, f32[4,136,128]{2,1,0:T(8,128)S(1)}, u32[]{:S(2)}, u32[]{:S(2)}) collective-permute-start(f32[4,136,128]{2,1,0:T(8,128)S(1)} %get-tuple-element.77), channel_id=1, source_target_pairs={{0,1},{1,0},{2,3},{3,2},{4,5},{5,4},{6,7},{7,6},{8,9},{9,8},{10,11... | collective-permute-start | bytes 835592 | tf_op jit(solution)/shard_map/ppermute | solution.py:314
  87.5 5.0 %collective-permute-start.10 = (s32[2,72,128]{2,1,0:T(8,128)S(1)}, s32[2,72,128]{2,1,0:T(8,128)S(1)}, u32[]{:S(2)}, u32[]{:S(2)}) collective-permute-start(s32[2,72,128]{2,1,0:T(8,128)S(1)} %get-tuple-element.80), channel_id=1, source_target_pairs={{0,2},{2,4},{4,6},{6,0},{1,7},{3,1},{5,3},{7,5},{8,10},{10,12},{12... | collective-permute-start | bytes 221192 | tf_op jit(solution)/shard_map/ppermute | solution.py:322
  88.8 6.7 %collective-permute-start.9 = (s32[72,128]{1,0:T(8,128)S(1)}, s32[72,128]{1,0:T(8,128)S(1)}, u32[]{:S(2)}, u32[]{:S(2)}) collective-permute-start(s32[72,128]{1,0:T(8,128)S(1)} %get-tuple-element.79), channel_id=1, source_target_pairs={{0,4},{2,6},{4,0},{6,2},{1,5},{3,7},{5,1},{7,3},{8,12},{10,14},{12... | collective-permute-start | bytes 110600 | tf_op jit(solution)/shard_map/ppermute | solution.py:319
  92.5 3.0 %collective-permute-start.11 = (s32[72,128]{1,0:T(8,128)S(1)}, s32[72,128]{1,0:T(8,128)S(1)}, u32[]{:S(2)}, u32[]{:S(2)}) collective-permute-start(s32[72,128]{1,0:T(8,128)S(1)} %slice_bitcast_fusion.3), channel_id=1, source_target_pairs={{0,1},{1,0},{2,3},{3,2},{4,5},{5,4},{6,7},{7,6},{8,9},{9,8},{10,11... | collective-permute-start | bytes 110600 | tf_op jit(solution)/shard_map/ppermute | solution.py:314
  117.2 4.0 %collective-permute-start.12 = (f32[4,136,128]{2,1,0:T(8,128)S(1)}, f32[4,136,128]{2,1,0:T(8,128)S(1)}, u32[]{:S(2)}, u32[]{:S(2)}) collective-permute-start(f32[4,136,128]{2,1,0:T(8,128)S(1)} %get-tuple-element.86), channel_id=1, source_target_pairs={{0,1},{1,0},{2,3},{3,2},{4,5},{5,4},{6,7},{7,6},{8,9},{9,8},{10,11... | collective-permute-start | bytes 835592 | tf_op jit(solution)/shard_map/ppermute | solution.py:314
  121.4 5.0 %collective-permute-start.14 = (s32[2,72,128]{2,1,0:T(8,128)S(1)}, s32[2,72,128]{2,1,0:T(8,128)S(1)}, u32[]{:S(2)}, u32[]{:S(2)}) collective-permute-start(s32[2,72,128]{2,1,0:T(8,128)S(1)} %get-tuple-element.89), channel_id=1, source_target_pairs={{0,2},{2,4},{4,6},{6,0},{1,7},{3,1},{5,3},{7,5},{8,10},{10,12},{12... | collective-permute-start | bytes 221192 | tf_op jit(solution)/shard_map/ppermute | solution.py:322
  123.2 7.9 %collective-permute-start.13 = (s32[72,128]{1,0:T(8,128)S(1)}, s32[72,128]{1,0:T(8,128)S(1)}, u32[]{:S(2)}, u32[]{:S(2)}) collective-permute-start(s32[72,128]{1,0:T(8,128)S(1)} %get-tuple-element.88), channel_id=1, source_target_pairs={{0,4},{2,6},{4,0},{6,2},{1,5},{3,7},{5,1},{7,3},{8,12},{10,14},{12... | collective-permute-start | bytes 110600 | tf_op jit(solution)/shard_map/ppermute | solution.py:319
  126.4 4.7 %collective-permute-start.15 = (s32[72,128]{1,0:T(8,128)S(1)}, s32[72,128]{1,0:T(8,128)S(1)}, u32[]{:S(2)}, u32[]{:S(2)}) collective-permute-start(s32[72,128]{1,0:T(8,128)S(1)} %slice_bitcast_fusion.2), channel_id=1, source_target_pairs={{0,1},{1,0},{2,3},{3,2},{4,5},{5,4},{6,7},{7,6},{8,9},{9,8},{10,11... | collective-permute-start | bytes 110600 | tf_op jit(solution)/shard_map/ppermute | solution.py:314
  153.5 3.6 %collective-permute-start.16 = (f32[4,136,128]{2,1,0:T(8,128)S(1)}, f32[4,136,128]{2,1,0:T(8,128)S(1)}, u32[]{:S(2)}, u32[]{:S(2)}) collective-permute-start(f32[4,136,128]{2,1,0:T(8,128)S(1)} %get-tuple-element.95), channel_id=1, source_target_pairs={{0,1},{1,0},{2,3},{3,2},{4,5},{5,4},{6,7},{7,6},{8,9},{9,8},{10,11... | collective-permute-start | bytes 835592 | tf_op jit(solution)/shard_map/ppermute | solution.py:314
  157.4 5.0 %collective-permute-start.18 = (s32[2,72,128]{2,1,0:T(8,128)S(1)}, s32[2,72,128]{2,1,0:T(8,128)S(1)}, u32[]{:S(2)}, u32[]{:S(2)}) collective-permute-start(s32[2,72,128]{2,1,0:T(8,128)S(1)} %get-tuple-element.98), channel_id=1, source_target_pairs={{0,2},{2,4},{4,6},{6,0},{1,7},{3,1},{5,3},{7,5},{8,10},{10,12},{12... | collective-permute-start | bytes 221192 | tf_op jit(solution)/shard_map/ppermute | solution.py:322
  159.1 6.8 %collective-permute-start.17 = (s32[72,128]{1,0:T(8,128)S(1)}, s32[72,128]{1,0:T(8,128)S(1)}, u32[]{:S(2)}, u32[]{:S(2)}) collective-permute-start(s32[72,128]{1,0:T(8,128)S(1)} %get-tuple-element.97), channel_id=1, source_target_pairs={{0,4},{2,6},{4,0},{6,2},{1,5},{3,7},{5,1},{7,3},{8,12},{10,14},{12... | collective-permute-start | bytes 110600 | tf_op jit(solution)/shard_map/ppermute | solution.py:319
  162.4 3.5 %collective-permute-start.19 = (s32[72,128]{1,0:T(8,128)S(1)}, s32[72,128]{1,0:T(8,128)S(1)}, u32[]{:S(2)}, u32[]{:S(2)}) collective-permute-start(s32[72,128]{1,0:T(8,128)S(1)} %slice_bitcast_fusion.1), channel_id=1, source_target_pairs={{0,1},{1,0},{2,3},{3,2},{4,5},{5,4},{6,7},{7,6},{8,9},{9,8},{10,11... | collective-permute-start | bytes 110600 | tf_op jit(solution)/shard_map/ppermute | solution.py:314
  188.4 3.2 %collective-permute-start.20 = (f32[4,136,128]{2,1,0:T(8,128)S(1)}, f32[4,136,128]{2,1,0:T(8,128)S(1)}, u32[]{:S(2)}, u32[]{:S(2)}) collective-permute-start(f32[4,136,128]{2,1,0:T(8,128)S(1)} %get-tuple-element.104), channel_id=1, source_target_pairs={{0,1},{1,0},{2,3},{3,2},{4,5},{5,4},{6,7},{7,6},{8,9},{9,8},{10,11... | collective-permute-start | bytes 835592 | tf_op jit(solution)/shard_map/ppermute | solution.py:314
  191.8 5.0 %collective-permute-start.22 = (s32[2,72,128]{2,1,0:T(8,128)S(1)}, s32[2,72,128]{2,1,0:T(8,128)S(1)}, u32[]{:S(2)}, u32[]{:S(2)}) collective-permute-start(s32[2,72,128]{2,1,0:T(8,128)S(1)} %get-tuple-element.107), channel_id=1, source_target_pairs={{0,2},{2,4},{4,6},{6,0},{1,7},{3,1},{5,3},{7,5},{8,10},{10,12},{12... | collective-permute-start | bytes 221192 | tf_op jit(solution)/shard_map/ppermute | solution.py:322
  193.3 6.7 %collective-permute-start.21 = (s32[72,128]{1,0:T(8,128)S(1)}, s32[72,128]{1,0:T(8,128)S(1)}, u32[]{:S(2)}, u32[]{:S(2)}) collective-permute-start(s32[72,128]{1,0:T(8,128)S(1)} %get-tuple-element.106), channel_id=1, source_target_pairs={{0,4},{2,6},{4,0},{6,2},{1,5},{3,7},{5,1},{7,3},{8,12},{10,14},{12... | collective-permute-start | bytes 110600 | tf_op jit(solution)/shard_map/ppermute | solution.py:319
  196.8 3.2 %collective-permute-start.23 = (s32[72,128]{1,0:T(8,128)S(1)}, s32[72,128]{1,0:T(8,128)S(1)}, u32[]{:S(2)}, u32[]{:S(2)}) collective-permute-start(s32[72,128]{1,0:T(8,128)S(1)} %slice_bitcast_fusion), channel_id=1, source_target_pairs={{0,1},{1,0},{2,3},{3,2},{4,5},{5,4},{6,7},{7,6},{8,9},{9,8},{10,11... | collective-permute-start | bytes 110600 | tf_op jit(solution)/shard_map/ppermute | solution.py:314
